TPU v7x, 32 devices: a whole 2x2x4 slice. The times are simulated.
32 devices in a mesh: blk: 8 (over y, x, core), head: 4 (over z).
Axes of the slice: x: 2, y: 2, z: 4, core: 2. Of those that a mesh axis runs over, the one named last changes fastest.
Arguments:
- tokens: bfloat16 [8192, 1024], P(('blk', 'head')), may hold values from -6 to 6
- g_mix: bfloat16 [1024], P(('blk', 'head')), may hold values from 0.5 to 1.5
- w_qkv: bfloat16 [1024, 768], P(('blk', 'head')), may hold values from -0.1875 to 0.1875
- w_mamba_in: bfloat16 [1024, 3352], P(('blk', 'head')), may hold values from -0.1875 to 0.1875
- conv_w: bfloat16 [4, 1792], P(None, ('blk', 'head')), may hold values from -3 to 3
- conv_b: bfloat16 [1792], P(('blk', 'head')), may hold values from -3 to 3
- dt_bias: float32 [24], P('head'), may hold values from -5 to -2
- a_log: float32 [24], P('head'), may hold values from -4.5 to 0.5
- d_skip: float32 [24], P('head'), may hold values from 0.5 to 2
- w_attn_out: bfloat16 [512, 1024], P(('blk', 'head')), may hold values from -1.5 to 1.5
- w_mamba_out: bfloat16 [1536, 1024], P(('blk', 'head')), may hold values from -0.15625 to 0.15625
- g_ffn: bfloat16 [1024], P(('blk', 'head')), may hold values from 0.5 to 1.5
- w_gate: bfloat16 [1024, 2048], P(('blk', 'head')), may hold values from -0.1875 to 0.1875
- w_up: bfloat16 [1024, 2048], P(('blk', 'head')), may hold values from -0.1875 to 0.1875
- w_down: bfloat16 [2048, 1024], P(('blk', 'head')), may hold values from -0.125 to 0.125
- doc_lengths: int32 [4], replicated, may hold values from 1 to 4096, 8192 in all
- cotangent: bfloat16 [8192, 1024], P(('blk', 'head')), may hold values from -6 to 6
Outputs:
- output: bfloat16 [8192, 1024], P(('blk', 'head'))
- grad_tokens: float32 [8192, 1024], P(('blk', 'head'))
- grad_g_mix: float32 [1024], P(('blk', 'head'))
- grad_w_qkv: float32 [1024, 768], P(('blk', 'head'))
- grad_w_mamba_in: float32 [1024, 3352], P(('blk', 'head'))
- grad_conv_w: float32 [4, 1792], P(None, ('blk', 'head'))
- grad_conv_b: float32 [1792], P(('blk', 'head'))
- grad_dt_bias: float32 [24], P('head')
- grad_a_log: float32 [24], P('head')
- grad_d_skip: float32 [24], P('head')
- grad_w_attn_out: float32 [512, 1024], P(('blk', 'head'))
- grad_w_mamba_out: float32 [1536, 1024], P(('blk', 'head'))
- grad_g_ffn: float32 [1024], P(('blk', 'head'))
- grad_w_gate: float32 [1024, 2048], P(('blk', 'head'))
- grad_w_up: float32 [1024, 2048], P(('blk', 'head'))
- grad_w_down: float32 [2048, 1024], P(('blk', 'head'))
Inputs may be any that keep to these rules, and one draw needn't show every extreme that they name: `doc_lengths`: lengths of the 4 documents of the stream in order; they sum to 8192 and the longest is exactly 4096.
All inputs are finite; a program needn't handle non-finite values.
Results may differ from a plain program's by a relative error of at most 0.012.
The roundings to bfloat16 on the way count: a program that leaves them out, or rounds other values in their place, can miss the bound.
Values may be sent and summed in bfloat16 or wider, within the bound.
A program may use at most 256 MiB of HBM per device.

v0:
```python
import jax
import jax.numpy as jnp
from jax import lax
from jax.sharding import PartitionSpec as P

QHEADS = 8
KVHEADS = 2
HDIM = 64
MHEADS = 24
STATE = 128
CONVW = 4
DOCMAX = 4096
SPAN = 256
QBLOCK = 512


EPS = 1e-06
HIGH = lax.Precision.HIGHEST
NEG = -1e30


def from_behind(array, axis, by):
    peers = lax.axis_size(axis)
    pairs = [(i, i + by) for i in range(peers) if 0 <= i + by < peers]
    return lax.ppermute(array, axis, pairs)


def carried_in_2(array, axis, join, neutral):
    place = lax.axis_index(axis)
    gathered = jax.tree.map(
        lambda a, kind: lax.all_gather(a.astype(kind), axis), array, (jnp.bfloat16, jnp.bfloat16)
    )
    state = jax.tree.map(lambda a, e: jnp.zeros_like(a) + jnp.asarray(e, a.dtype), array, neutral)

    def carried_one(step, state):
        return join(
            state,
            jax.tree.map(
                lambda a, own: lax.dynamic_index_in_dim(a, step, 0, False).astype(own.dtype),
                gathered,
                array,
            ),
        )

    return lax.fori_loop(0, place, carried_one, state)


def prefix(array, axis, join, neutral):
    count = lax.axis_size(axis)
    place = lax.axis_index(axis)
    ahead = count - 1 - place
    gathered = jax.tree.map(
        lambda a, kind: lax.all_gather(a.astype(kind), axis),
        array,
        jax.tree.map(lambda a: jnp.bfloat16 if a.dtype == jnp.float32 else a.dtype, array),
    )
    state = jax.tree.map(lambda a, e: jnp.zeros_like(a) + jnp.asarray(e, a.dtype), array, neutral)

    def prefix_one(step, state):
        source = count - 1 - step
        return join(
            state,
            jax.tree.map(
                lambda a, own: lax.dynamic_index_in_dim(a, source, 0, False).astype(own.dtype),
                gathered,
                array,
            ),
        )

    return lax.fori_loop(0, ahead, prefix_one, state)


def dot_low(left_side, right_side):
    return jnp.dot(left_side, right_side, preferred_element_type=jnp.float32)


def dot_left_t(left_side, right_side):
    return lax.dot_general(
        left_side, right_side, (((0,), (0,)), ((), ())), preferred_element_type=jnp.float32
    )


def dot_right_t(left_side, right_side):
    return lax.dot_general(
        left_side, right_side, (((1,), (1,)), ((), ())), preferred_element_type=jnp.float32
    )


def dot_high(left_side, right_side):
    return jnp.dot(left_side, right_side, precision=HIGH, preferred_element_type=jnp.float32)


def rms_gain(values, gain_vec):
    return values * lax.rsqrt(jnp.mean(values * values, axis=-1, keepdims=True) + EPS) * gain_vec


def softplus(values):
    return jnp.log1p(jnp.exp(values))


def doc_ids(positions, starts):
    inside = (starts[None, :] <= positions[:, None]).astype(jnp.int32)
    return jnp.sum(inside, axis=1) - 1


def make_payload(q_part, k_part, v_part, z_part, x_part, bc_part, dt_part, groups):
    row_count = q_part.shape[0]
    key_values = jnp.concatenate(
        [k_part.reshape(row_count, KVHEADS, HDIM), v_part.reshape(row_count, KVHEADS, HDIM)], axis=2
    )
    key_values = jnp.repeat(key_values, groups // KVHEADS, axis=1)
    shared = jnp.broadcast_to(bc_part[:, None, :], (row_count, groups, bc_part.shape[1]))
    return jnp.concatenate(
        [
            q_part.reshape(row_count, groups, -1),
            key_values,
            z_part.reshape(row_count, groups, -1),
            x_part.reshape(row_count, groups, -1),
            shared,
            dt_part.reshape(row_count, groups, -1),
        ],
        axis=2,
    )


def causal_conv(rows_in, row_docs, tap_weights, shifts):
    count_out = rows_in.shape[0] - CONVW + 1
    current = row_docs[CONVW - 1 :]
    summed = shifts[None, :]
    for tap_index in range(CONVW):
        same_doc = (row_docs[tap_index : tap_index + count_out] == current).astype(jnp.float32)[
            :, None
        ]
        summed = (
            summed
            + tap_weights[tap_index][None, :]
            * rows_in[tap_index : tap_index + count_out]
            * same_doc
        )
    return summed


def ssd_span(ssm_state, inputs, decay_rate, skip_gain):
    x_heads, step_size, b_state, c_state, span_docs, doc_prev = inputs
    length = step_size.shape[0]
    positions = jnp.arange(length, dtype=jnp.int32)
    lower_mask = positions[:, None] >= positions[None, :]
    cum_decay = dot_high(lower_mask.astype(jnp.float32), step_size * decay_rate[None, :])
    same_doc = lower_mask & (span_docs[:, None] == span_docs[None, :])
    decay_table = jnp.exp(
        jnp.where(same_doc[:, :, None], cum_decay[:, None, :] - cum_decay[None, :, :], NEG)
    )
    mixing = decay_table * dot_high(c_state, b_state.T)[:, :, None] * step_size[None, :, :]
    output = jnp.einsum("ijh,jhp->ihp", mixing, x_heads, precision=HIGH)
    entry_rate = jnp.exp(cum_decay) * (span_docs == doc_prev).astype(jnp.float32)[:, None]
    output = output + entry_rate[:, :, None] * jnp.einsum(
        "hpn,in->ihp", ssm_state, c_state, precision=HIGH
    )
    output = output + skip_gain[None, :, None] * x_heads
    end_weight = (
        jnp.exp(cum_decay[-1][None, :] - cum_decay)
        * (span_docs == span_docs[-1]).astype(jnp.float32)[:, None]
        * step_size
    )
    keep_rate = jnp.exp(cum_decay[-1]) * (span_docs[-1] == doc_prev).astype(jnp.float32)
    fresh_state = jnp.einsum("jh,jhp,jn->hpn", end_weight, x_heads, b_state, precision=HIGH)
    return (keep_rate[:, None, None] * ssm_state + fresh_state, output, cum_decay)


def chain(earlier, later):
    return (earlier[0] * later[0], later[0][:, None, None] * earlier[1] + later[1])


def masked_scores(q_block, key_part, q_pos, q_doc, key_pos, key_docs, score_scale):
    scores = (
        jnp.einsum("bhd,kd->hbk", q_block, key_part, preferred_element_type=jnp.float32)
        * score_scale
    )
    allowed = (key_docs[None, :] == q_doc[:, None]) & (key_pos[None, :] <= q_pos[:, None])
    return jnp.where(allowed[None], scores, NEG)


def per_device(
    tokens,
    g_mix,
    w_qkv,
    w_mamba_in,
    conv_w,
    conv_b,
    dt_bias,
    a_log,
    d_skip,
    w_attn_out,
    w_mamba_out,
    g_ffn,
    w_gate,
    w_up,
    w_down,
    doc_lengths,
    cotangent,
):
    head_count = lax.axis_size("head")
    head_index = lax.axis_index("head")
    blk_index = lax.axis_index("blk")
    tok_rows = tokens.shape[0]
    group_rows = tok_rows * head_count
    q_heads = QHEADS // head_count
    m_heads = MHEADS // head_count
    q_width = q_heads * HDIM
    m_width = m_heads * HDIM
    q_total = QHEADS * HDIM
    kv_total = KVHEADS * HDIM
    m_total = MHEADS * HDIM
    channels = m_width + 2 * STATE
    rim_rows = CONVW - 1
    cycle_depth = (DOCMAX - 1) // group_rows + 1
    score_scale = HDIM ** (-0.5)
    block_count = group_rows // QBLOCK
    span_count = group_rows // SPAN
    window = QBLOCK + DOCMAX
    window_base = cycle_depth * group_rows - DOCMAX
    gathered = (
        lax.all_gather(g_mix, ("blk", "head"), axis=0, tiled=True),
        lax.all_gather(w_qkv, ("blk", "head"), axis=0, tiled=True),
        lax.all_gather(w_mamba_in, ("blk", "head"), axis=0, tiled=True),
        lax.all_gather(conv_w, ("blk", "head"), axis=1, tiled=True),
        lax.all_gather(conv_b, ("blk", "head"), axis=0, tiled=True),
        lax.all_gather(w_attn_out, ("blk", "head"), axis=0, tiled=True),
        lax.all_gather(w_mamba_out, ("blk", "head"), axis=0, tiled=True),
        lax.all_gather(g_ffn, ("blk", "head"), axis=0, tiled=True),
        lax.all_gather(w_gate, ("blk", "head"), axis=0, tiled=True),
        lax.all_gather(w_up, ("blk", "head"), axis=0, tiled=True),
        lax.all_gather(w_down, ("blk", "head"), axis=0, tiled=True),
    )
    (
        gain_mix,
        whole_qkv,
        whole_min,
        whole_cw,
        whole_cb,
        whole_ao,
        whole_mo,
        gain_ffn,
        whole_gate,
        whole_up,
        whole_down,
    ) = gathered
    tok_float = tokens.astype(jnp.float32)
    normed_in, norm_in_pull = jax.vjp(rms_gain, tok_float, gain_mix.astype(jnp.float32))
    normed = normed_in.astype(jnp.bfloat16)
    proj_qkv = dot_low(normed, whole_qkv)
    proj_mamba = dot_low(normed, whole_min)
    pieces = (
        proj_qkv[:, :q_total],
        proj_qkv[:, q_total : q_total + kv_total],
        proj_qkv[:, q_total + kv_total :],
        proj_mamba[:, :m_total],
        proj_mamba[:, m_total : 2 * m_total],
        proj_mamba[:, 2 * m_total : 2 * m_total + 2 * STATE],
        proj_mamba[:, 2 * m_total + 2 * STATE :],
    )

    def layout(*pieces_in):
        return make_payload(*pieces_in, head_count)

    payload, layout_pull = jax.vjp(layout, *pieces)
    at_heads = lax.all_to_all(
        payload.astype(jnp.bfloat16), "head", split_axis=1, concat_axis=0, tiled=True
    )[:, 0, :]
    starts_at = jnp.cumsum(doc_lengths) - doc_lengths
    first_row = blk_index * group_rows
    row_pos = first_row + jnp.arange(group_rows, dtype=jnp.int32)
    token_docs = doc_ids(row_pos, starts_at)
    ext_docs = doc_ids(
        first_row - rim_rows + jnp.arange(group_rows + rim_rows, dtype=jnp.int32), starts_at
    )
    doc_before = ext_docs[rim_rows - 1]
    queries = at_heads[:, :q_width].reshape(group_rows, q_heads, HDIM)
    key_values = at_heads[:, q_width : q_width + 2 * HDIM]
    z_col = q_width + 2 * HDIM
    gate_z = at_heads[:, z_col : z_col + m_width]
    conv_in = at_heads[:, z_col + m_width : z_col + m_width + channels]
    dt_raw = at_heads[:, z_col + m_width + channels :]
    rim_in = from_behind(conv_in[group_rows - rim_rows :], "blk", 1)
    conv_taps = jnp.concatenate(
        [
            lax.dynamic_slice_in_dim(whole_cw, head_index * m_width, m_width, 1),
            whole_cw[:, m_total:],
        ],
        axis=1,
    ).astype(jnp.float32)
    conv_shift = jnp.concatenate(
        [lax.dynamic_slice_in_dim(whole_cb, head_index * m_width, m_width, 0), whole_cb[m_total:]]
    ).astype(jnp.float32)
    span_prev = jnp.concatenate([doc_before[None], token_docs[:-1]]).reshape(span_count, SPAN)[:, 0]

    def local_mixer(conv_rows, dt_input, tap_weights, shifts, dt_shift, log_rate, skip_gain):
        activated = jax.nn.silu(causal_conv(conv_rows, ext_docs, tap_weights, shifts))
        x_heads = activated[:, :m_width].reshape(group_rows, m_heads, HDIM)
        b_state = activated[:, m_width : m_width + STATE]
        c_state = activated[:, m_width + STATE :]
        step_size = softplus(dt_input + dt_shift[None, :])
        decay_rate = -jnp.exp(log_rate)
        spanned = (
            x_heads.reshape(span_count, SPAN, m_heads, HDIM),
            step_size.reshape(span_count, SPAN, m_heads),
            b_state.reshape(span_count, SPAN, STATE),
            c_state.reshape(span_count, SPAN, STATE),
            token_docs.reshape(span_count, SPAN),
            span_prev,
        )

        def group_step(carried, inputs):
            new_state, output, cum_decay = ssd_span(carried[0], inputs, decay_rate, skip_gain)
            return (
                (new_state, carried[1] + cum_decay[-1]),
                (output, carried[1][None, :] + cum_decay),
            )

        start_state = (
            jnp.zeros((m_heads, HDIM, STATE), jnp.float32),
            jnp.zeros((m_heads,), jnp.float32),
        )
        (local_state, total_decay), (outputs, cum_group) = lax.scan(
            group_step, start_state, spanned
        )
        keep_rate = jnp.exp(total_decay) * (token_docs[-1] == doc_before).astype(jnp.float32)
        return (
            outputs.reshape(group_rows, m_heads, HDIM),
            local_state,
            keep_rate,
            c_state,
            cum_group.reshape(group_rows, m_heads),
        )

    conv_rows = jnp.concatenate([rim_in, conv_in], axis=0).astype(jnp.float32)
    mixer_out, mixer_pull = jax.vjp(
        local_mixer,
        conv_rows,
        dt_raw.astype(jnp.float32),
        conv_taps,
        conv_shift,
        dt_bias,
        a_log,
        d_skip,
    )
    y_local, local_state, keep_rate, c_state, cum_group = mixer_out
    scan_unit = (jnp.ones((m_heads,), jnp.float32), jnp.zeros((m_heads, HDIM, STATE), jnp.float32))
    state_in = carried_in_2((keep_rate, local_state), "blk", chain, scan_unit)[1]
    before_mask = (token_docs == doc_before).astype(jnp.float32)

    def finish(y_part, c_part, cum_part, entry_state, z_part):
        entry_rate = before_mask[:, None] * jnp.exp(cum_part)
        carried_in = jnp.einsum("hpn,tn->thp", entry_state, c_part, precision=HIGH)
        full_y = y_part + entry_rate[:, :, None] * carried_in
        return (full_y * jax.nn.silu(z_part)).reshape(group_rows, m_width)

    mamba_y, finish_pull = jax.vjp(
        finish,
        y_local,
        c_state,
        cum_group,
        state_in,
        gate_z.astype(jnp.float32).reshape(group_rows, m_heads, HDIM),
    )
    cycle_blocks = [key_values]
    moving = key_values
    for cycle_step in range(cycle_depth):
        moving = from_behind(moving, "blk", 1)
        cycle_blocks.append(moving)
    key_all = jnp.concatenate(cycle_blocks[::-1], axis=0)
    key_pos = (
        first_row
        - cycle_depth * group_rows
        + jnp.arange((cycle_depth + 1) * group_rows, dtype=jnp.int32)
    )
    key_docs = doc_ids(key_pos, starts_at)
    key_part = key_all[:, :HDIM]
    value_part = key_all[:, HDIM:]
    q_blocks = queries.reshape(block_count, QBLOCK, q_heads, HDIM)
    pos_blocks = row_pos.reshape(block_count, QBLOCK)
    doc_blocks = token_docs.reshape(block_count, QBLOCK)
    block_ids = jnp.arange(block_count, dtype=jnp.int32)

    def key_window(block_id):
        offset = window_base + block_id * QBLOCK
        return (
            offset,
            lax.dynamic_slice_in_dim(key_part, offset, window, 0),
            lax.dynamic_slice_in_dim(value_part, offset, window, 0),
            lax.dynamic_slice_in_dim(key_pos, offset, window, 0),
            lax.dynamic_slice_in_dim(key_docs, offset, window, 0),
        )

    def attend(inputs):
        q_block, q_pos, q_doc, block_id = inputs
        offset, keys_near, values_near, pos_near, docs_near = key_window(block_id)
        scores = masked_scores(q_block, keys_near, q_pos, q_doc, pos_near, docs_near, score_scale)
        row_top = jnp.max(scores, axis=-1, keepdims=True)
        raised = jnp.exp(scores - row_top)
        row_total = jnp.sum(raised, axis=-1, keepdims=True)
        output = jnp.einsum(
            "hbk,kd->bhd",
            (raised / row_total).astype(jnp.bfloat16),
            values_near,
            preferred_element_type=jnp.float32,
        )
        return (output, (row_top + jnp.log(row_total))[:, :, 0])

    attn_out, log_sums = lax.map(attend, (q_blocks, pos_blocks, doc_blocks, block_ids))
    attn_flat = attn_out.reshape(group_rows, q_width)
    back_heads = jnp.concatenate([attn_flat, mamba_y], axis=1).astype(jnp.bfloat16)[:, None, :]
    at_tokens = lax.all_to_all(back_heads, "head", split_axis=0, concat_axis=1, tiled=True)
    attn_tok = at_tokens[:, :, :q_width].reshape(tok_rows, q_total)
    mamba_tok = at_tokens[:, :, q_width:].reshape(tok_rows, m_total)
    mixed = tok_float + dot_low(attn_tok, whole_ao) + dot_low(mamba_tok, whole_mo)
    normed_ffn, norm_ffn_pull = jax.vjp(rms_gain, mixed, gain_ffn.astype(jnp.float32))
    ffn_in = normed_ffn.astype(jnp.bfloat16)
    gate_act = dot_low(ffn_in, whole_gate)
    up_act = dot_low(ffn_in, whole_up)
    hidden = (jax.nn.silu(gate_act) * up_act).astype(jnp.bfloat16)
    result = (mixed + dot_low(hidden, whole_down)).astype(jnp.bfloat16)
    gathered_again = (
        lax.all_gather(g_mix, ("blk", "head"), axis=0, tiled=True),
        lax.all_gather(w_qkv, ("blk", "head"), axis=0, tiled=True),
        lax.all_gather(w_mamba_in, ("blk", "head"), axis=0, tiled=True),
        lax.all_gather(conv_w, ("blk", "head"), axis=1, tiled=True),
        lax.all_gather(conv_b, ("blk", "head"), axis=0, tiled=True),
        lax.all_gather(w_attn_out, ("blk", "head"), axis=0, tiled=True),
        lax.all_gather(w_mamba_out, ("blk", "head"), axis=0, tiled=True),
        lax.all_gather(g_ffn, ("blk", "head"), axis=0, tiled=True),
        lax.all_gather(w_gate, ("blk", "head"), axis=0, tiled=True),
        lax.all_gather(w_up, ("blk", "head"), axis=0, tiled=True),
        lax.all_gather(w_down, ("blk", "head"), axis=0, tiled=True),
    )
    (
        gain_mix,
        whole_qkv,
        whole_min,
        whole_cw,
        whole_cb,
        whole_ao,
        whole_mo,
        gain_ffn,
        whole_gate,
        whole_up,
        whole_down,
    ) = gathered_again
    d_hidden = dot_right_t(cotangent, whole_down)
    grad_down = dot_left_t(hidden, cotangent)
    gate_sig = jax.nn.sigmoid(gate_act)
    d_gate = (d_hidden * up_act * gate_sig * (1.0 + gate_act * (1.0 - gate_sig))).astype(
        jnp.bfloat16
    )
    d_up = (d_hidden * gate_act * gate_sig).astype(jnp.bfloat16)
    grad_gate = dot_left_t(ffn_in, d_gate)
    grad_up = dot_left_t(ffn_in, d_up)
    d_ffn_in = dot_right_t(d_gate, whole_gate) + dot_right_t(d_up, whole_up)
    d_mixed_norm, grad_gain_ffn = norm_ffn_pull(d_ffn_in)
    d_mixed = cotangent.astype(jnp.float32) + d_mixed_norm
    d_branch = d_mixed.astype(jnp.bfloat16)
    grad_ao = dot_left_t(attn_tok, d_branch)
    grad_mo = dot_left_t(mamba_tok, d_branch)
    d_attn = dot_right_t(d_branch, whole_ao).reshape(tok_rows, head_count, q_width)
    d_mamba = dot_right_t(d_branch, whole_mo).reshape(tok_rows, head_count, m_width)
    d_back = jnp.concatenate([d_attn, d_mamba], axis=2).astype(jnp.bfloat16)
    d_heads = lax.all_to_all(d_back, "head", split_axis=1, concat_axis=0, tiled=True)[:, 0, :]
    d_y_local, d_c_state, d_cum, d_entry, d_gate_z = finish_pull(
        d_heads[:, q_width:].astype(jnp.float32)
    )
    carried_back = prefix((keep_rate, d_entry), "blk", chain, scan_unit)[1]
    d_keep = jnp.sum(carried_back * state_in, axis=(1, 2))
    d_conv_rows, d_dt_raw, d_taps, d_shift, d_dt_bias, d_a_log, d_d_skip = mixer_pull(
        (d_y_local, carried_back, d_keep, d_c_state, d_cum)
    )
    rim_back = from_behind(d_conv_rows[:rim_rows], "blk", -1)
    d_conv_in = d_conv_rows[rim_rows:].at[group_rows - rim_rows :].add(rim_back)
    d_out_blocks = d_heads[:, :q_width].reshape(block_count, QBLOCK, q_heads, HDIM)

    def attend_back(d_keys, inputs):
        q_block, d_block, sums_block, q_pos, q_doc, block_id = inputs
        offset, keys_near, values_near, pos_near, docs_near = key_window(block_id)
        scores = masked_scores(q_block, keys_near, q_pos, q_doc, pos_near, docs_near, score_scale)
        soft_weights = jnp.exp(scores - sums_block[:, :, None])
        d_soft = jnp.einsum("bhd,kd->hbk", d_block, values_near, preferred_element_type=jnp.float32)
        row_dot = jnp.sum(soft_weights * d_soft, axis=-1, keepdims=True)
        d_scores = (soft_weights * (d_soft - row_dot)).astype(jnp.bfloat16)
        d_query = (
            jnp.einsum("hbk,kd->bhd", d_scores, keys_near, preferred_element_type=jnp.float32)
            * score_scale
        )
        d_key = (
            jnp.einsum("hbk,bhd->kd", d_scores, q_block, preferred_element_type=jnp.float32)
            * score_scale
        )
        d_value = jnp.einsum(
            "hbk,bhd->kd",
            soft_weights.astype(jnp.bfloat16),
            d_block,
            preferred_element_type=jnp.float32,
        )
        current = lax.dynamic_slice_in_dim(d_keys, offset, window, 0)
        updated = current + jnp.concatenate([d_key, d_value], axis=1)
        return (lax.dynamic_update_slice_in_dim(d_keys, updated, offset, 0), d_query)

    d_kv_all, d_queries = lax.scan(
        attend_back,
        jnp.zeros(((cycle_depth + 1) * group_rows, 2 * HDIM), jnp.float32),
        (q_blocks, d_out_blocks, log_sums, pos_blocks, doc_blocks, block_ids),
    )
    kv_pieces = d_kv_all.reshape(cycle_depth + 1, group_rows, 2 * HDIM)
    d_kv = kv_pieces[0]
    for cycle_step in range(cycle_depth):
        d_kv = (
            from_behind(d_kv.astype(jnp.bfloat16), "blk", -1).astype(d_kv.dtype)
            + kv_pieces[cycle_step + 1]
        )
    d_payload = jnp.concatenate(
        [
            d_queries.reshape(group_rows, q_width),
            d_kv,
            d_gate_z.reshape(group_rows, m_width),
            d_conv_in,
            d_dt_raw,
        ],
        axis=1,
    ).astype(jnp.bfloat16)[:, None, :]
    d_token_side = lax.all_to_all(d_payload, "head", split_axis=0, concat_axis=1, tiled=True)
    d_pieces = layout_pull(d_token_side.astype(jnp.float32))
    d_pieces = [piece.astype(jnp.bfloat16) for piece in d_pieces]
    d_proj_qkv = jnp.concatenate(d_pieces[:3], axis=1)
    d_proj_mamba = jnp.concatenate(d_pieces[3:], axis=1)
    grad_qkv = dot_left_t(normed, d_proj_qkv)
    grad_min = dot_left_t(normed, d_proj_mamba)
    d_normed = dot_right_t(d_proj_qkv, whole_qkv) + dot_right_t(d_proj_mamba, whole_min)
    d_tok_norm, grad_gain_mix = norm_in_pull(d_normed)
    grad_tokens = d_mixed + d_tok_norm
    grad_cw = jnp.zeros((CONVW, m_total + 2 * STATE), jnp.float32)
    grad_cw = lax.dynamic_update_slice_in_dim(grad_cw, d_taps[:, :m_width], head_index * m_width, 1)
    grad_cw = grad_cw.at[:, m_total:].set(d_taps[:, m_width:])
    grad_cb = lax.dynamic_update_slice_in_dim(
        jnp.zeros((m_total + 2 * STATE,), jnp.float32), d_shift[:m_width], head_index * m_width, 0
    )
    grad_cb = grad_cb.at[m_total:].set(d_shift[m_width:])
    reduced = (
        lax.psum_scatter(grad_gain_mix, ("blk", "head"), scatter_dimension=0, tiled=True),
        lax.psum_scatter(grad_qkv, ("blk", "head"), scatter_dimension=0, tiled=True),
        lax.psum_scatter(grad_min, ("blk", "head"), scatter_dimension=0, tiled=True),
        lax.psum_scatter(grad_cw, ("blk", "head"), scatter_dimension=1, tiled=True),
        lax.psum_scatter(grad_cb, ("blk", "head"), scatter_dimension=0, tiled=True),
        lax.psum_scatter(grad_ao, ("blk", "head"), scatter_dimension=0, tiled=True),
        lax.psum_scatter(grad_mo, ("blk", "head"), scatter_dimension=0, tiled=True),
        lax.psum_scatter(grad_gain_ffn, ("blk", "head"), scatter_dimension=0, tiled=True),
        lax.psum_scatter(grad_gate, ("blk", "head"), scatter_dimension=0, tiled=True),
        lax.psum_scatter(grad_up, ("blk", "head"), scatter_dimension=0, tiled=True),
        lax.psum_scatter(grad_down, ("blk", "head"), scatter_dimension=0, tiled=True),
    )
    head_grads = lax.psum((d_dt_bias, d_a_log, d_d_skip), "blk")
    return (
        result,
        grad_tokens,
        reduced[0],
        reduced[1],
        reduced[2],
        reduced[3],
        reduced[4],
        head_grads[0],
        head_grads[1],
        head_grads[2],
        reduced[5],
        reduced[6],
        reduced[7],
        reduced[8],
        reduced[9],
        reduced[10],
    )


def solution(mesh):
    in_specs = (
        P(("blk", "head"), None),
        P(("blk", "head")),
        P(("blk", "head"), None),
        P(("blk", "head"), None),
        P(None, ("blk", "head")),
        P(("blk", "head")),
        P("head"),
        P("head"),
        P("head"),
        P(("blk", "head"), None),
        P(("blk", "head"), None),
        P(("blk", "head")),
        P(("blk", "head"), None),
        P(("blk", "head"), None),
        P(("blk", "head"), None),
        P(),
        P(("blk", "head"), None),
    )
    out_specs = (
        P(("blk", "head"), None),
        P(("blk", "head"), None),
        P(("blk", "head")),
        P(("blk", "head"), None),
        P(("blk", "head"), None),
        P(None, ("blk", "head")),
        P(("blk", "head")),
        P("head"),
        P("head"),
        P("head"),
        P(("blk", "head"), None),
        P(("blk", "head"), None),
        P(("blk", "head")),
        P(("blk", "head"), None),
        P(("blk", "head"), None),
        P(("blk", "head"), None),
    )
    return jax.shard_map(
        per_device, mesh=mesh, in_specs=in_specs, out_specs=out_specs, check_vma=False
    )
```

profile of v0, /device:TPU:0, one launch (start us, length us, event | category | flops | bytes accessed | tf_op | source)
XLA Modules:
  0.0 2057.1 jit_solution(7691453192860712203)
XLA Ops:
  13.7 42.1 %all-reduce.24 = (bf16[1024]{0:T(1024)(128)(2,1)S(1)}, bf16[1792]{0:T(1024)(128)(2,1)S(1)}, bf16[1024]{0:T(1024)(128)(2,1)}) all-reduce(bf16[1024]{0:T(1024)(128)(2,1)S(1)} %dynamic-update-slice.15, bf16[1792]{0:T(1024)(128)(2,1)S(1)} %dynamic-update-slice.16, ...), channel_id=1, replica_groups=mesh['blk'=8,'head'=4] {'blk','head'}, use_global_device_ids=true, to_apply=%add.14 | all-reduce | flops 3840 | bytes 15360
  57.6 11.0 all-gather.12.cloned.1.call-done
  72.7 69.8 %all-gather.14.cloned.1.call-done = bf16[1024,3352]{1,0:T(8,128)(2,1)} async-done(((bf16[32,3352]{1,0:T(8,128)(2,1)}), bf16[1024,3352]{1,0:T(8,128)(2,1)}) %all-gather.14.cloned.1.call-update) | async-done | bytes 6864912 | tf_op jit(solution)/shard_map/all_gather | solution.py:225
  157.7 129.3 %all-gather.3 = bf16[32,56,4]{1,2,0:T(4,128)(2,1)S(1)} all-gather(bf16[1,56,4]{1,2,0:T(4,128)(2,1)S(1)} %bitcast.848), channel_id=1, replica_groups=mesh['blk'=8,'head'=4] {'blk','head'}, dimensions={0}, use_global_device_ids=true | all-gather | bytes 14784 | tf_op jit(solution)/shard_map/all_gather | solution.py:226
  322.2 120.1 %while.144 = (s32[]{:T(128)}, f32[6,64,128]{2,1,0:T(8,128)S(1)}, f32[6]{0:T(128)S(1)}, f32[4,256,6,64]{1,0,3,2:T(4,128)}, f32[4,256,6]{1,0,2:T(4,128)S(1)}, /*in...) while((s32[]{:T(128)}, f32[6,64,128]{2,1,0:T(8,128)S(1)}, ...), condition=%wide.region_10.11_spmd.clone, body=%wide.region_9.10_spmd.clone.sunk | while | flops 713681920 | bytes 13548272 | solution.py:324
  334.3 9.5 dynamic_update_slice.276
  364.4 9.5 dynamic_update_slice.276
  394.3 9.6 dynamic_update_slice.276
  424.3 9.5 dynamic_update_slice.276
  446.3 12.7 all-reduce.16
  459.1 15.2 all-gather.1
  512.1 38.2 %while.140 = (s32[]{:T(128)}, bf16[2,512,2,64]{1,3,2,0:T(8,128)(2,1)S(1)}, f32[2,2,512]{2,1,0:T(2,128)S(1)}, s32[2]{0:T(128)S(1)}, bf16[5120,64]{0,1:T(8,128)(2,...) while((s32[]{:T(128)}, ...), condition=%wide.region_7.8_spmd, body=%wide.region_4.7_spmd.sunk | while | flops 1271659520 | bytes 67789024 | solution.py:410
  571.2 26.3 %all-to-all-done.1 = bf16[4,2,65536]{2,1,0:T(2,128)(2,1)} async-done(((bf16[4,2,65536]{2,1,0:T(2,128)(2,1)}), bf16[4,2,65536]{2,1,0:T(2,128)(2,1)}, u32[]{:S(2)}, u32[]{:S(2)}) %all-to-all-start.1) | async-done | bytes 1048608 | tf_op jit(solution)/shard_map/all_to_all | solution.py:413
  648.7 26.8 %all-to-all-done.2 = bf16[256,4,512]{2,0,1:T(8,128)(2,1)} async-done(((bf16[256,4,512]{2,0,1:T(8,128)(2,1)}), bf16[256,4,512]{2,0,1:T(8,128)(2,1)}, u32[]{:S(2)}, u32[]{:S(2)}) %all-to-all-start.2) | async-done | bytes 1048608 | tf_op jit(solution)/shard_map/all_to_all | solution.py:467
  692.8 11.4 all-gather.2
  718.3 174.8 %while.145 = (s32[]{:T(128)}, f32[6]{0:T(128)}, f32[6]{0:T(128)}, f32[6,64,128]{2,1,0:T(8,128)S(1)}, f32[6]{0:T(128)S(1)}, /*index=5*/f32[4,256,6,64]{1,0,3,2:T(...) while((s32[]{:T(128)}, f32[6]{0:T(128)}, f32[6]{0:T(128)}, ...), condition=%wide.region_33.34_spmd.clone, body=%wide.region_22.33_spmd.clone.sunk | while | flops 1419470336 | bytes 17075344 | solution.py:324
  725.6 9.5 dynamic_update_slice.283
  768.2 9.5 dynamic_update_slice.283
  812.2 9.5 dynamic_update_slice.283
  856.3 9.5 dynamic_update_slice.283
  906.3 156.3 %while.142 = (s32[]{:T(128)}, f32[5120,128]{1,0:T(8,128)}, bf16[2,512,2,64]{1,3,2,0:T(8,128)(2,1)}, s32[2]{0:T(128)S(1)}, s32[5120]{0:T(1024)S(1)}, /*index=5*/s...) while((s32[]{:T(128)}, f32[5120,128]{1,0:T(8,128)}, ...), condition=%wide.region_17.18_spmd, body=%wide.region_15.17_spmd.sunk | while | flops 3070983168 | bytes 255211392 | solution.py:506
  921.1 16.8 fusion.392
  938.0 19.0 fusion.394
  999.2 16.9 fusion.392
  1016.1 19.0 fusion.394
  1125.2 63.0 %all_to_all.57 = bf16[4,2,164608]{2,1,0:T(2,128)(2,1)S(1)} all-to-all(bf16[4,2,164608]{2,1,0:T(2,128)(2,1)} %reshape.1022), channel_id=1, replica_groups=mesh['blk'=8,'head'=4] {'head'}, dimensions={0} | all-to-all | bytes 5267456 | tf_op jit(solution)/shard_map/all_to_all | solution.py:528
  1250.9 18.1 all-reduce.23
  1285.3 40.0 %all-reduce.22 = (f32[1024]{0:T(1024)S(1)}, f32[4,1792]{1,0:T(4,128)S(1)}, f32[1792]{0:T(1024)S(1)}, f32[1024]{0:T(1024)S(1)}) all-reduce(f32[1024]{0:T(1024)S(1)} %get-tuple-element.2283, f32[4,1792]{1,0:T(4,128)S(1)} %copy-done.71, f32[1792]{0:T(1024)S(1)} %copy-done.99, ...), channel_id=5, replica_groups=mesh['blk'=8,'head'=4] {'blk','head'}, use_global_device_ids=true, to_apply=%region_38.39.clone | all-reduce | flops 11008 | bytes 88064
  1330.5 180.5 %reduce-scatter.19.cloned.1.call-done = f32[32,2048]{1,0:T(8,128)} async-done(((f32[1024,2048]{1,0:T(8,128)}), f32[32,2048]{1,0:T(8,128)}) %reduce-scatter.19.cloned.1.call-update) | async-done | bytes 262160 | tf_op jit(solution)/shard_map/reduce_scatter | solution.py:555
  1511.0 186.2 %reduce-scatter.17.cloned.1.call-done = f32[32,2048]{1,0:T(8,128)} async-done(((f32[1024,2048]{1,0:T(8,128)}), f32[32,2048]{1,0:T(8,128)}) %reduce-scatter.17.cloned.1.call-update) | async-done | bytes 262160 | tf_op jit(solution)/shard_map/reduce_scatter | solution.py:554
  1697.2 186.3 %reduce-scatter.21.cloned.1.call-done = f32[64,1024]{1,0:T(8,128)} async-done(((f32[2048,1024]{1,0:T(8,128)}), f32[64,1024]{1,0:T(8,128)}) %reduce-scatter.21.cloned.1.call-update) | async-done | bytes 262160 | tf_op jit(solution)/shard_map/reduce_scatter | solution.py:556
  1883.5 166.8 %reduce-scatter.11.cloned.1.call-done = f32[32,3352]{1,0:T(8,128)} async-done(((f32[1024,3352]{1,0:T(8,128)}), f32[32,3352]{1,0:T(8,128)}) %reduce-scatter.11.cloned.1.call-update) | async-done | bytes 429072 | tf_op jit(solution)/shard_map/reduce_scatter | solution.py:548
  (947 shorter events, 701.8 us)
Async XLA Ops:
  7.2 61.4 %all-gather.12.cloned.1.call-start = ((), (), s32[]{:S(2)}) async-start(), calls=%async_computation.11 | async-start | bytes 1622016 | tf_op jit(solution)/shard_map/all_gather | solution.py:224
  7.9 134.6 %all-gather.14.cloned.1.call-start = ((), (), s32[]{:S(2)}) async-start(), calls=%async_computation.12 | async-start | bytes 7299072 | tf_op jit(solution)/shard_map/all_gather | solution.py:225
  8.7 592.8 %all-gather.18.cloned.1.call-start = ((), (), s32[]{:S(2)}) async-start(), calls=%async_computation.14 | async-start | bytes 3244032 | tf_op jit(solution)/shard_map/all_gather | solution.py:229
  9.4 596.0 %all-gather.16.cloned.1.call-start = ((), (), s32[]{:S(2)}) async-start(), calls=%async_computation.13 | async-start | bytes 1081344 | tf_op jit(solution)/shard_map/all_gather | solution.py:228
  10.0 597.8 %all-gather.20.cloned.1.call-start = ((), (), s32[]{:S(2)}) async-start(), calls=%async_computation.15 | async-start | bytes 4325376 | tf_op jit(solution)/shard_map/all_gather | solution.py:231
  10.6 602.3 %all-gather.22.cloned.1.call-start = ((), (), s32[]{:S(2)}) async-start(), calls=%async_computation.16 | async-start | bytes 4325376 | tf_op jit(solution)/shard_map/all_gather | solution.py:232
  55.8 86.7 %copy-start.59 = (f32[1024]{0:T(1024)}, f32[1024]{0:T(1024)S(1)}, u32[]{:S(2)}) copy-start(f32[1024]{0:T(1024)S(1)} %convert_element_type.286) | copy-start | bytes 12292
  152.0 138.0 %copy-start.125 = (u32[32]{0:T(128)S(1)}, u32[32]{0:T(128)}, u32[]{:S(2)}) copy-start(u32[32]{0:T(128)} %constant.452) | copy-start | bytes 388
  152.0 139.6 %copy-start.123 = (f32[6]{0:T(128)S(1)}, f32[6]{0:T(128)}, u32[]{:S(2)}) copy-start(f32[6]{0:T(128)} %param.42) | copy-start | bytes 76
  152.0 140.4 %all-to-all-start = ((bf16[256,4,1286]{0,2,1:T(8,128)(2,1)}), bf16[256,4,1286]{0,2,1:T(8,128)(2,1)S(1)}, u32[]{:S(2)}, u32[]{:S(2)}) async-start(bf16[256,4,1286]{0,2,1:T(8,128)(2,1)} %constant_dynamic-update-slice_fusion.4), calls=%async_computation | async-start | bytes 5275648 | tf_op jit(solution)/shard_map/all_to_all | solution.py:267
  155.8 461.9 %all-gather.24.cloned.1.call-start = ((), (), s32[]{:S(2)}) async-start(), calls=%async_computation.17 | async-start | bytes 4325376 | tf_op jit(solution)/shard_map/all_gather | solution.py:233
  300.6 173.6 %collective-permute-start = (bf16[1024,128]{1,0:T(8,128)(2,1)}, bf16[1024,128]{1,0:T(8,128)(2,1)}, u32[]{:S(2)}, u32[]{:S(2)}) collective-permute-start(bf16[1024,128]{1,0:T(8,128)(2,1)} %slice.295), channel_id=1, source_target_pairs={{0,4},{4,8},{8,12},{12,16},{16,20},{20,24},{24,28},{1,5},{5,9},{9,... | collective-permute-start | bytes 786440 | tf_op jit(solution)/shard_map/ppermute | solution.py:25
  302.6 4.0 collective-permute-start.4
  474.3 3.8 collective-permute-start.1
  478.0 7.8 collective-permute-start.2
  485.9 15.1 collective-permute-start.3
  566.9 30.6 %all-to-all-start.1 = ((bf16[4,2,65536]{2,1,0:T(2,128)(2,1)}), bf16[4,2,65536]{2,1,0:T(2,128)(2,1)}, u32[]{:S(2)}, u32[]{:S(2)}) async-start(bf16[4,2,65536]{2,1,0:T(2,128)(2,1)} %reshape.1020), calls=%async_computation.1 | async-start | bytes 2097152 | tf_op jit(solution)/shard_map/all_to_all | solution.py:413
  571.1 759.4 %reduce-scatter.13.cloned.1.call-start = ((), (), s32[]{:S(2)}) async-start(), calls=%async_computation.20 | async-start | bytes 2162688 | tf_op jit(solution)/shard_map/reduce_scatter | solution.py:551
  636.9 38.7 %all-to-all-start.2 = ((bf16[256,4,512]{2,0,1:T(8,128)(2,1)}), bf16[256,4,512]{2,0,1:T(8,128)(2,1)}, u32[]{:S(2)}, u32[]{:S(2)}) async-start(bf16[256,4,512]{2,0,1:T(8,128)(2,1)} %pad_maximum_fusion.2), calls=%async_computation.2 | async-start | bytes 2097152 | tf_op jit(solution)/shard_map/all_to_all | solution.py:467
  641.2 689.3 %reduce-scatter.15.cloned.1.call-start = ((), (), s32[]{:S(2)}) async-start(), calls=%async_computation.21 | async-start | bytes 6488064 | tf_op jit(solution)/shard_map/reduce_scatter | solution.py:552
  648.7 681.9 %reduce-scatter.9.cloned.1.call-start = ((), (), s32[]{:S(2)}) async-start(), calls=%async_computation.18 | async-start | bytes 3244032 | tf_op jit(solution)/shard_map/reduce_scatter | solution.py:547
  906.3 158.7 %copy-start.79 = (f32[1024]{0:T(1024)S(1)}, f32[1024]{0:T(1024)}, u32[]{:S(2)}) copy-start(f32[1024]{0:T(1024)} %copy-done.78) | copy-start | bytes 12292
  906.3 158.7 %copy-start.81 = (f32[1024]{0:T(1024)S(1)}, f32[1024]{0:T(1024)}, u32[]{:S(2)}) copy-start(f32[1024]{0:T(1024)} %copy-done.80) | copy-start | bytes 12292
  1063.7 18.2 collective-permute-start.5
  1080.3 22.5 %collective-permute-start.9 = (f32[3,640]{1,0:T(4,128)S(1)}, f32[3,640]{1,0:T(4,128)S(1)}, u32[]{:S(2)}, u32[]{:S(2)}) collective-permute-start(f32[3,640]{1,0:T(4,128)S(1)} %pad_add_fusion.1), channel_id=1, source_target_pairs={{4,0},{8,4},{12,8},{16,12},{20,16},{24,20},{28,24},{5,1},{9,5},{13... | collective-permute-start | bytes 23048 | tf_op jit(solution)/shard_map/ppermute | solution.py:25
  1082.0 4.8 collective-permute-start.6
  1087.6 9.3 collective-permute-start.7
  1098.6 8.7 collective-permute-start.8
  1216.0 295.0 %reduce-scatter.19.cloned.1.call-start = ((), (), s32[]{:S(2)}) async-start(), calls=%async_computation.23 | async-start | bytes 8650752 | tf_op jit(solution)/shard_map/reduce_scatter | solution.py:555
  1222.1 475.1 %reduce-scatter.17.cloned.1.call-start = ((), (), s32[]{:S(2)}) async-start(), calls=%async_computation.22 | async-start | bytes 8650752 | tf_op jit(solution)/shard_map/reduce_scatter | solution.py:554
  1228.2 655.3 %reduce-scatter.21.cloned.1.call-start = ((), (), s32[]{:S(2)}) async-start(), calls=%async_computation.24 | async-start | bytes 8650752 | tf_op jit(solution)/shard_map/reduce_scatter | solution.py:556
  1234.2 816.1 %reduce-scatter.11.cloned.1.call-start = ((), (), s32[]{:S(2)}) async-start(), calls=%async_computation.19 | async-start | bytes 14598144 | tf_op jit(solution)/shard_map/reduce_scatter | solution.py:548
  (162 other events, 2252.7 us)
Sparse Core Ops, SparseCore 0:
  10.9 57.6 all-gather.11
  71.4 71.0 all-gather.13
  145.4 86.5 all-gather.17
  234.8 53.1 all-gather.15
  290.8 60.6 all-gather.19
  354.3 60.5 all-gather.21
  417.9 63.7 all-gather.23
  632.3 146.4 reduce-scatter.12
  785.0 114.4 reduce-scatter.14
  1216.1 107.2 reduce-scatter.8
  1326.3 184.6 reduce-scatter.18
  1513.7 183.4 reduce-scatter.16
  1700.1 183.4 reduce-scatter.20
  1889.9 160.2 reduce-scatter.10
where the time goes:
time: 2070 us; the launch traced here: 2060 us
  waiting for transfers between devices  862 us (42%)
  blocking collectives  332 us (16%)
  matrix products  299 us (14%)
  local copies, waits for them, and re-layouts  286 us (14%)
  other arithmetic  212 us (10%)
  starting transfers between devices  38.5 us (2%)
    reduce_scatter x1, waiting for transfers between devices, per_device(): lax.psum_scatter(grad_down, ('blk', 'head'), scatter_dimension=0, tiled=T...  186 us
    reduce_scatter x1, waiting for transfers between devices, per_device(): lax.psum_scatter(grad_gate, ('blk', 'head'), scatter_dimension=0, tiled=T...  186 us
    reduce_scatter x1, waiting for transfers between devices, per_device(): lax.psum_scatter(grad_up, ('blk', 'head'), scatter_dimension=0, tiled=True)  180 us
    reduce_scatter x1, waiting for transfers between devices, per_device(): lax.psum_scatter(grad_min, ('blk', 'head'), scatter_dimension=0, tiled=True)  167 us
    all_gather x1, blocking collectives, per_device(): lax.all_gather(conv_w, ('blk', 'head'), axis=1, tiled=True)  129 us
    unnamed x3, blocking collectives  94.8 us
    dynamic_update_slice x48, local copies, waits for them, and re-layouts, local_mixer(): lax.scan(group_step, start_state, spanned)  91.1 us
    all_gather x1, waiting for transfers between devices, per_device(): lax.all_gather(w_mamba_in, ('blk', 'head'), axis=0, tiled=True)  69.8 us
  transfers between devices with their start and end apart: 27, of which 11 were waited for; matrix products, arithmetic and copies ran while one was open for 38% of the time, Pallas kernels for 0%

commit v1 on v0

v1 whole, which is shorter than its diff:
```python
import functools

import jax
import jax.numpy as jnp
from jax import lax
from jax.experimental import pallas as pl
from jax.experimental.pallas import tpu as pltpu
from jax.sharding import Mesh
from jax.sharding import PartitionSpec as P

QHEADS = 8
KVHEADS = 2
HDIM = 64
MHEADS = 24
STATE = 128
CONVW = 4
DOCMAX = 4096
SPAN = 256
TP = 8
RIM = 8

EPS = 1e-06
HIGH = lax.Precision.HIGHEST
NEG = -1e30
BF = jnp.bfloat16
F32 = jnp.float32
ALL = ("grp", "tp", "head")
SEQ = ("grp", "head")

MH = MHEADS // TP
MW = MH * HDIM
CH = 2 * STATE + MW
COL_Q = CH
COL_Z = 512
COL_DT = COL_Z + MW
COL_KV = 768
COLS = 896
SLAB = MW + 8


def dot(a, b):
    return jnp.dot(a, b, preferred_element_type=F32)


def dot_lt(a, b):
    return lax.dot_general(a, b, (((0,), (0,)), ((), ())), preferred_element_type=F32)


def dot_rt(a, b):
    return lax.dot_general(a, b, (((1,), (1,)), ((), ())), preferred_element_type=F32)


def hdot(a, b):
    return jnp.dot(a, b, precision=HIGH, preferred_element_type=F32)


def hdot_lt(a, b):
    return lax.dot_general(
        a, b, (((0,), (0,)), ((), ())), precision=HIGH, preferred_element_type=F32
    )


def hdot_rt(a, b):
    return lax.dot_general(
        a, b, (((1,), (1,)), ((), ())), precision=HIGH, preferred_element_type=F32
    )


def sigmoid(v):
    return 1.0 / (1.0 + jnp.exp(-v))


def iota(shape, axis):
    return lax.broadcasted_iota(jnp.int32, shape, axis)


def heads_wide(cols):
    return jnp.concatenate(
        [jnp.broadcast_to(cols[:, h : h + 1], (cols.shape[0], HDIM)) for h in range(MH)], axis=1
    )


def conv_pre(ext, off, taps, bias):
    total = jnp.broadcast_to(bias, (SPAN, ext.shape[1]))
    for k in range(CONVW):
        back = CONVW - 1 - k
        moved = ext if back == 0 else pltpu.roll(ext, back, 0)
        total = total + jnp.where(off >= back, moved[RIM:] * taps[k : k + 1], 0.0)
    return total


def span_parts(dtr, dtb, alog):
    step = jnp.log1p(jnp.exp(dtr + dtb))
    rate = -jnp.exp(alog)
    tri = (iota((SPAN, SPAN), 0) >= iota((SPAN, SPAN), 1)).astype(F32)
    cum = hdot(tri, step * rate)
    return step, rate, cum


def mixer_local(sc, pay, ds, taps, bias, dtb, alog, dsk, u_out, cum_out, y_out, slab_out):
    i = pl.program_id(0)
    first = sc[0, i]
    ds_last = sc[1, i]
    pos = first + iota((SPAN, 1), 0)
    start = ds[0]
    ext = pay[0, :, :CH].astype(F32)
    c = conv_pre(ext, pos - start, taps[...], bias[...])
    u = c * sigmoid(c)
    u_out[0] = u
    bs, cs, x = u[:, :STATE], u[:, STATE : 2 * STATE], u[:, 2 * STATE :]
    dtr = pay[0, RIM:, COL_Z : COL_Z + 256].astype(F32)[:, MW:]
    dtr = jnp.concatenate([dtr, jnp.zeros((SPAN, 64), F32)], axis=1)
    step, rate, cum = span_parts(dtr, dtb[...], alog[...])
    cum_out[0] = cum
    cum_t = cum.T
    step_t = step.T
    gram = hdot_rt(cs, bs)
    mask = (first + iota((SPAN, SPAN), 1) >= start) & (iota((SPAN, SPAN), 0) >= iota((SPAN, SPAN), 1))
    ys = []
    for h in range(MH):
        decay = jnp.exp(jnp.where(mask, cum[:, h : h + 1] - cum_t[h : h + 1], NEG))
        mixing = decay * gram * step_t[h : h + 1]
        xh = x[:, h * HDIM : (h + 1) * HDIM]
        ys.append(hdot(mixing, xh) + dsk[0:1, h : h + 1] * xh)
    y_out[0] = jnp.concatenate(ys, axis=1)
    last = cum[SPAN - 1 :]
    weight = jnp.where(pos >= ds_last, jnp.exp(last - cum) * step, 0.0)
    fresh = hdot_lt(x * heads_wide(weight), bs)
    keep = jnp.where(ds_last < first, jnp.exp(last), 0.0)
    rows = [jnp.broadcast_to(keep[:, h : h + 1], (1, STATE)) for h in range(MH)]
    rows.append(jnp.zeros((8 - MH, STATE), F32))
    slab_out[0] = jnp.concatenate([fresh] + rows, axis=0).astype(BF)


def place_of(c, n_head):
    return (c // (TP * n_head)) * n_head + c % n_head, (c // n_head) % TP


def keep_wide(slab):
    return jnp.concatenate(
        [
            jnp.broadcast_to(slab[MW + h : MW + h + 1].astype(F32), (HDIM, STATE))
            for h in range(MH)
        ],
        axis=0,
    )


def mixer_finish(n_head, sc, slabs, u, cum, yl, pay, ds, o, branch_out, y_out, state_out, states):
    i = pl.program_id(0)
    mine = sc[3, 0]

    @pl.when(i == 0)
    def _():
        def one(c, state):
            sp, ic = place_of(c, n_head)

            @pl.when(sp == mine)
            def _():
                states[ic] = state

            slab = slabs[sp, ic]
            return keep_wide(slab) * state + slab[:MW].astype(F32)

        total = slabs.shape[0] * TP
        lax.fori_loop(0, total, one, jnp.zeros((MW, STATE), F32))

    first = sc[0, i]
    state = states[i]
    state_out[0] = state
    entry = jnp.where(ds[0] < first, jnp.exp(cum[0]), 0.0)
    carried = hdot_rt(u[0, :, STATE : 2 * STATE], state)
    y = yl[0] + heads_wide(entry) * carried
    y_out[0] = y
    z = pay[0, RIM:, :MW].astype(F32)
    ym = y * (z * sigmoid(z))
    branch_out[0] = jnp.concatenate([o[0][:, :HDIM], ym], axis=1).astype(BF)


def mixer_entry(sc, dh, u, cum, pay, ds, entry_out):
    i = pl.program_id(0)
    first = sc[0, i]
    z = pay[0, RIM:, :MW].astype(F32)
    dym = dh[0].astype(F32)[:, HDIM:]
    entry = jnp.where(ds[0] < first, jnp.exp(cum[0]), 0.0)
    scaled = dym * (z * sigmoid(z)) * heads_wide(entry)
    entry_out[0] = hdot_lt(scaled, u[0, :, STATE : 2 * STATE]).astype(BF)


def mixer_back(
    n_head,
    sc,
    slabs,
    d_entries,
    dh,
    pay,
    ds,
    state,
    y,
    dq,
    dkv,
    taps,
    bias,
    dtb,
    alog,
    dsk,
    dpay_out,
    dtap_out,
    dsmall_out,
    carried,
):
    i = pl.program_id(0)
    mine = sc[3, 0]

    @pl.when(i == 0)
    def _():
        total = slabs.shape[0] * TP

        def one(step, adj):
            sp, ic = place_of(total - 1 - step, n_head)

            @pl.when(sp == mine)
            def _():
                carried[ic] = adj

            return keep_wide(slabs[sp, ic]) * adj + d_entries[sp, ic].astype(F32)

        lax.fori_loop(0, total, one, jnp.zeros((MW, STATE), F32))
        dtap_out[...] = jnp.zeros_like(dtap_out)
        dsmall_out[...] = jnp.zeros_like(dsmall_out)

    first = sc[0, i]
    ds_last = sc[1, i]
    pos = first + iota((SPAN, 1), 0)
    start = ds[0]
    off = pos - start
    ext = pay[0, :, :CH].astype(F32)
    c = conv_pre(ext, off, taps[...], bias[...])
    sig_c = sigmoid(c)
    u = c * sig_c
    bs, cs, x = u[:, :STATE], u[:, STATE : 2 * STATE], u[:, 2 * STATE :]
    zdt = pay[0, RIM:, COL_Z : COL_Z + 256].astype(F32)
    z = zdt[:, :MW]
    dtr = jnp.concatenate([zdt[:, MW:], jnp.zeros((SPAN, 64), F32)], axis=1)
    step, rate, cum = span_parts(dtr, dtb[...], alog[...])
    cum_t = cum.T
    step_t = step.T
    gram = hdot_rt(cs, bs)
    mask = (first + iota((SPAN, SPAN), 1) >= start) & (iota((SPAN, SPAN), 0) >= iota((SPAN, SPAN), 1))

    dym = dh[0].astype(F32)[:, HDIM:]
    sig_z = sigmoid(z)
    dy = dym * (z * sig_z)
    dz = dym * y[0] * (sig_z * (1.0 + z * (1.0 - sig_z)))

    st = state[0]
    adj = carried[i]
    entry = jnp.where(start < first, jnp.exp(cum), 0.0)
    last = cum[SPAN - 1 :]
    fade = jnp.where(pos >= ds_last, jnp.exp(last - cum), 0.0)
    weight = fade * step
    keep = jnp.where(ds_last < first, jnp.exp(last), 0.0)
    lane = iota((1, STATE), 1)

    back_b = hdot_rt(bs, adj)
    carried_y = hdot_rt(cs, st)
    dy_entry = dy * heads_wide(entry)
    x_weight = x * heads_wide(weight)
    d_c = hdot(dy_entry, st)
    d_b = hdot(x_weight, adj)
    d_x = back_b * heads_wide(weight)
    adj_state = adj * st

    d_gram = jnp.zeros((SPAN, SPAN), F32)
    d_cum = jnp.zeros((SPAN, STATE), F32)
    d_step = jnp.zeros((SPAN, STATE), F32)
    d_last = jnp.zeros((1, STATE), F32)
    d_dsk = jnp.zeros((1, STATE), F32)
    rows_step = jnp.zeros((STATE, SPAN), F32)
    dxs = []
    for h in range(MH):
        part = slice(h * HDIM, (h + 1) * HDIM)
        xh, dyh = x[:, part], dy[:, part]
        decay = jnp.exp(jnp.where(mask, cum[:, h : h + 1] - cum_t[h : h + 1], NEG))
        d_mix = hdot_rt(dyh, xh)
        inner = d_mix * decay
        step_row = step_t[h : h + 1]
        d_gram = d_gram + inner * step_row
        inner = inner * gram
        mixing = decay * gram * step_row
        dxs.append(d_x[:, part] + hdot_lt(mixing, dyh) + dsk[0:1, h : h + 1] * dyh)
        row_sum = jnp.sum(inner, axis=0, keepdims=True)
        rows_step = jnp.where(iota((STATE, SPAN), 0) == h, row_sum, rows_step)
        is_h = lane == h
        col = jnp.sum(inner * step_row, axis=1, keepdims=True)
        d_ent = jnp.sum(dyh * carried_y[:, part], axis=1, keepdims=True)
        d_wgt = jnp.sum(back_b[:, part] * xh, axis=1, keepdims=True)
        d_cum = jnp.where(is_h, col + d_ent * entry - d_wgt * weight, d_cum)
        d_step = jnp.where(is_h, d_wgt * fade, d_step)
        d_keep = jnp.sum(adj_state[part], keepdims=True)
        d_last = jnp.where(
            is_h, jnp.sum(d_wgt * weight, axis=0, keepdims=True) + d_keep * keep, d_last
        )
        d_dsk = jnp.where(is_h, jnp.sum(dyh * xh, keepdims=True), d_dsk)
    row_step = rows_step.T
    d_step = d_step + row_step
    d_cum = d_cum - row_step * step
    d_cum = d_cum + jnp.where(iota((SPAN, STATE), 0) == SPAN - 1, d_last, 0.0)
    tri_up = (iota((SPAN, SPAN), 1) >= iota((SPAN, SPAN), 0)).astype(F32)
    d_da = hdot(tri_up, d_cum)
    d_step = d_step + d_da * rate
    d_alog = jnp.sum(d_da * step, axis=0, keepdims=True) * rate
    d_dtr = d_step * sigmoid(dtr + dtb[...])
    d_dtb = jnp.sum(d_dtr, axis=0, keepdims=True)
    d_c = d_c + hdot(d_gram, bs)
    d_b = d_b + hdot_lt(d_gram, cs)
    d_u = jnp.concatenate([d_b, d_c] + dxs, axis=1)
    d_conv = d_u * (sig_c * (1.0 + c * (1.0 - sig_c)))
    d_ext = jnp.zeros((RIM + SPAN, CH), F32)
    tap_rows = []
    for k in range(CONVW):
        back = CONVW - 1 - k
        moved = ext if back == 0 else pltpu.roll(ext, back, 0)
        masked = jnp.where(off >= back, d_conv, 0.0)
        tap_rows.append(jnp.sum(masked * moved[RIM:], axis=0, keepdims=True))
        wide = jnp.concatenate([jnp.zeros((RIM, CH), F32), masked * taps[k : k + 1]], axis=0)
        d_ext = d_ext + (wide if back == 0 else pltpu.roll(wide, RIM + SPAN - back, 0))
    tap_rows.append(jnp.sum(d_conv, axis=0, keepdims=True))
    tap_rows.append(jnp.zeros((3, CH), F32))
    dtap_out[...] += jnp.concatenate(tap_rows, axis=0)
    dsmall_out[...] += jnp.concatenate([d_dtb, d_alog, d_dsk, jnp.zeros((5, STATE), F32)], axis=0)
    own = jnp.concatenate(
        [dq[0][:, HDIM:], dz, d_dtr[:, :64], dkv[0].astype(F32)], axis=1
    )
    right = jnp.concatenate([jnp.zeros((RIM, COLS - CH), F32), own], axis=0)
    dpay_out[0] = jnp.concatenate([d_ext, right], axis=1).astype(BF)


def attend(n_head, sc, pay_q, ds, kv, o_out, lse_out):
    i = pl.program_id(0)
    first = sc[0, i]
    low = sc[2, i]
    base = sc[4, i]
    mine = first // SPAN
    lane = iota((SPAN, 128), 1)
    q = jnp.where(lane >= HDIM, pay_q[0, RIM:] * jnp.asarray(HDIM**-0.5, BF), jnp.asarray(0, BF))
    start = ds[0]
    pos = first + iota((SPAN, 1), 0)

    def one(c, carry):
        top, total, acc = carry
        sp, ic = place_of(c, n_head)
        sp = sp - base
        keys = kv[sp, ic]
        s = dot_rt(q, keys)
        key = c * SPAN + iota((SPAN, SPAN), 1)
        s = jnp.where((key >= start) & (key <= pos), s, NEG)
        new_top = jnp.maximum(top, jnp.max(s, axis=1, keepdims=True))
        fade = jnp.exp(top - new_top)
        p = jnp.exp(s - new_top)
        total = total * fade + jnp.sum(p, axis=1, keepdims=True)
        return new_top, total, acc * fade + dot(p.astype(BF), keys)

    carry = (jnp.full((SPAN, 1), NEG, F32), jnp.zeros((SPAN, 1), F32), jnp.zeros((SPAN, 128), F32))
    carry = one(mine, carry)
    top, total, acc = lax.fori_loop(low, mine, one, carry)
    o_out[0] = acc / total
    lse_out[0] = top + jnp.log(total)


def attend_back(n_head, sc, pay_q, ds, dh, o, lse, kv, dq_out, dkv_out, acc_kv):
    i = pl.program_id(0)

    @pl.when(i == 0)
    def _():
        acc_kv[...] = jnp.zeros_like(acc_kv)

    first = sc[0, i]
    low = sc[2, i]
    base = sc[4, i]
    mine = first // SPAN
    lane = iota((SPAN, 128), 1)
    scale = HDIM**-0.5
    q = jnp.where(lane >= HDIM, pay_q[0, RIM:] * jnp.asarray(scale, BF), jnp.asarray(0, BF))
    do = jnp.where(lane < HDIM, dh[0], jnp.asarray(0, BF))
    delta = jnp.sum(jnp.where(lane < HDIM, o[0] * do.astype(F32), 0.0), axis=1, keepdims=True)
    start = ds[0]
    pos = first + iota((SPAN, 1), 0)
    sums = lse[0]

    def one(c, d_q):
        sp, ic = place_of(c, n_head)
        sp = sp - base
        keys = kv[sp, ic]
        s = dot_rt(q, keys)
        key = c * SPAN + iota((SPAN, SPAN), 1)
        p = jnp.exp(jnp.where((key >= start) & (key <= pos), s - sums, NEG))
        dp = dot_rt(do, keys)
        d_s = (p * (dp - delta)).astype(BF)
        acc_kv[sp, ic] += dot_lt(d_s, q) + dot_lt(p.astype(BF), do)
        return d_q + dot(d_s, keys)

    dq_out[0] = lax.fori_loop(low, mine + 1, one, jnp.zeros((SPAN, 128), F32)) * scale

    @pl.when(i == TP - 1)
    def _():
        dkv_out[...] = acc_kv[...].astype(BF)


def block(shape, *index):
    def where(i, *_):
        return tuple(i if v == "i" else v for v in index)

    return pl.BlockSpec(shape, where)


def whole(shape):
    return pl.BlockSpec(shape, lambda i, *_: (0,) * len(shape), pipeline_mode=pl.Buffered(1))


def call(kernel, sc, ins, specs, outs, out_specs, scratch, name):
    return pl.pallas_call(
        kernel,
        out_shape=[jax.ShapeDtypeStruct(s, d) for s, d in outs],
        grid_spec=pltpu.PrefetchScalarGridSpec(
            num_scalar_prefetch=1,
            grid=(TP,),
            in_specs=specs,
            out_specs=out_specs,
            scratch_shapes=scratch,
        ),
        compiler_params=pltpu.CompilerParams(
            dimension_semantics=("arbitrary",), vmem_limit_bytes=60 * 1024 * 1024
        ),
        name=name,
    )(sc, *ins)


def norm_parts(values, gain):
    inv = lax.rsqrt(jnp.mean(values * values, axis=-1, keepdims=True) + EPS)
    return values * inv * gain, inv


def norm_back(values, inv, gain, grad):
    scaled = grad * gain
    inner = jnp.mean(scaled * values, axis=-1, keepdims=True)
    d_values = inv * scaled - values * (inv * inv * inv) * inner
    return d_values, jnp.sum(grad * values * inv, axis=0)


def per_device(
    n_grp,
    n_head,
    tokens,
    g_mix,
    w_qkv,
    w_mamba_in,
    conv_w,
    conv_b,
    dt_bias,
    a_log,
    d_skip,
    w_attn_out,
    w_mamba_out,
    g_ffn,
    w_gate,
    w_up,
    w_down,
    doc_lengths,
    cotangent,
):
    t = lax.axis_index("tp")
    g = lax.axis_index("grp")
    h = lax.axis_index("head")
    n_seq = n_grp * n_head
    n_dev = n_seq * TP
    rows, width = tokens.shape
    q_total = QHEADS * HDIM
    kv_total = KVHEADS * HDIM
    m_total = MHEADS * HDIM
    r = w_qkv.shape[0]
    ff = w_gate.shape[1]
    ff_part = ff // TP

    def split_ff(w):
        return w.reshape(r, n_grp, TP, ff // (n_grp * TP)).transpose(2, 0, 1, 3).reshape(TP, r, -1)

    def by_tp(w):
        return w.reshape(r, TP, -1).transpose(1, 0, 2)

    def by_kv(w):
        return jnp.repeat(w.reshape(r, KVHEADS, HDIM).transpose(1, 0, 2), TP // KVHEADS, axis=0)

    bc = w_mamba_in[:, 2 * m_total : 2 * m_total + 2 * STATE]
    packed = jnp.concatenate(
        [
            jnp.broadcast_to(bc[None], (TP, r, 2 * STATE)),
            by_tp(w_mamba_in[:, m_total : 2 * m_total]),
            by_tp(w_qkv[:, :q_total]),
            by_tp(w_mamba_in[:, :m_total]),
            by_tp(w_mamba_in[:, 2 * m_total + 2 * STATE :]),
            jnp.zeros((TP, r, 64 - MH), BF),
            by_kv(w_qkv[:, q_total + kv_total :]),
            by_kv(w_qkv[:, q_total : q_total + kv_total]),
            split_ff(w_gate),
            split_ff(w_up),
        ],
        axis=2,
    )

    def gather_cols(piece):
        mine = lax.all_to_all(piece, "tp", 0, 0, tiled=True)
        every = lax.all_gather(mine, SEQ)
        every = every.reshape(n_grp, n_head, TP, r, -1).transpose(0, 2, 1, 3, 4)
        return every.reshape(n_dev * r, -1)

    w_in = gather_cols(packed[:, :, :COLS])
    w_gu = gather_cols(packed[:, :, COLS:])
    if n_grp == 1:
        w_out_attn = lax.all_gather(w_attn_out, SEQ, tiled=True)
        w_out_mamba = lax.all_gather(w_mamba_out, SEQ, tiled=True)
    else:
        w_out_attn = lax.dynamic_slice_in_dim(
            lax.all_gather(w_attn_out, ALL, tiled=True), t * HDIM, HDIM, 0
        )
        w_out_mamba = lax.dynamic_slice_in_dim(
            lax.all_gather(w_mamba_out, ALL, tiled=True), t * MW, MW, 0
        )
    w_out = jnp.concatenate([w_out_attn, w_out_mamba], axis=0)
    w_dn = lax.all_gather(w_down, SEQ, tiled=True)
    gain_mix = lax.all_gather(g_mix, ALL, tiled=True).astype(F32)[None]
    gain_ffn = lax.all_gather(g_ffn, ALL, tiled=True).astype(F32)[None]
    conv_all = lax.all_gather(jnp.concatenate([conv_w, conv_b[None]], axis=0), ALL)
    conv_all = conv_all.transpose(1, 0, 2).reshape(CONVW + 1, -1).astype(F32)
    conv_mine = jnp.concatenate(
        [conv_all[:, m_total:], lax.dynamic_slice_in_dim(conv_all, t * MW, MW, 1)], axis=1
    )
    taps = jnp.concatenate([conv_mine[:CONVW], jnp.zeros((8 - CONVW, CH), F32)], axis=0)
    bias = conv_mine[CONVW:]
    heads3 = lax.all_gather(jnp.stack([dt_bias, a_log, d_skip]), "head", axis=1, tiled=True)
    heads3 = lax.dynamic_slice_in_dim(heads3, t * MH, MH, 1)
    heads3 = jnp.pad(heads3, ((0, 0), (0, STATE - MH)))
    dtb, alog, dsk = heads3[0:1], heads3[1:2], heads3[2:3]

    starts = jnp.cumsum(doc_lengths) - doc_lengths
    chunk = (g * TP + jnp.arange(TP, dtype=jnp.int32)) * n_head + h
    firsts = chunk * SPAN
    pos = firsts[:, None] + jnp.arange(SPAN, dtype=jnp.int32)[None]
    doc_start = jnp.max(jnp.where(starts[None, None] <= pos[:, :, None], starts[None, None], 0), axis=2)
    mine = jnp.full((TP,), g * n_head + h, jnp.int32)
    n_win = n_head if n_grp == 1 else 2 * n_head
    base = jnp.full((TP,), (g + 1) * n_head - n_win, jnp.int32)
    sc = jnp.stack([firsts, doc_start[:, -1], doc_start[:, 0] // SPAN, mine, base]).astype(jnp.int32)
    ds = doc_start[:, :, None].astype(jnp.int32)

    rim = lax.ppermute(tokens[rows - RIM :], ALL, [(f, f + 1) for f in range(n_dev - 1)])
    ext_tokens = lax.all_gather(jnp.concatenate([rim, tokens], axis=0), "tp", tiled=True)
    cot_all = lax.all_gather(cotangent, "tp", tiled=True)

    normed = norm_parts(ext_tokens.astype(F32), gain_mix)[0].astype(BF)
    pay = dot(normed, w_in).astype(BF).reshape(TP, RIM + SPAN, COLS)

    f_u, f_c, f_y, f_ds = (1, SPAN, CH), (1, SPAN, STATE), (1, SPAN, MW), (1, SPAN, 1)
    s_pay = block((1, RIM + SPAN, COLS), "i", 0, 0)
    s_ds = block(f_ds, "i", 0, 0)
    s_z = block((1, RIM + SPAN, 256), "i", 0, 2)
    s_params = [whole((8, CH)), whole((1, CH))] + [whole((1, STATE))] * 3
    params = (taps, bias, dtb, alog, dsk)
    u, cum, y_local, slab = call(
        mixer_local,
        sc,
        (pay, ds) + params,
        [s_pay, s_ds] + s_params,
        [
            ((TP, SPAN, CH), F32),
            ((TP, SPAN, STATE), F32),
            ((TP, SPAN, MW), F32),
            ((TP, SLAB, STATE), BF),
        ],
        [
            block(f_u, "i", 0, 0),
            block(f_c, "i", 0, 0),
            block(f_y, "i", 0, 0),
            block((1, SLAB, STATE), "i", 0, 0),
        ],
        [],
        "mixer_local",
    )
    kv = lax.all_gather(pay[:, RIM:, COL_KV:], "head")
    if n_grp > 1:
        before = lax.ppermute(kv, "grp", [(a, a + 1) for a in range(n_grp - 1)])
        kv = jnp.concatenate([before, kv], axis=0)
    slabs = lax.all_gather(slab, SEQ)

    s_q = block((1, RIM + SPAN, 128), "i", 0, 3)
    s_o = block((1, SPAN, 128), "i", 0, 0)
    s_kv = whole((n_win, TP, SPAN, 128))
    o, lse = call(
        functools.partial(attend, n_head),
        sc,
        (pay, ds, kv),
        [s_q, s_ds, s_kv],
        [((TP, SPAN, 128), F32), ((TP, SPAN, 1), F32)],
        [s_o, s_ds],
        [],
        "attend",
    )
    s_slabs = whole((n_seq, TP, SLAB, STATE))
    s_state = block((1, MW, STATE), "i", 0, 0)
    branch, y_all, state_in = call(
        functools.partial(mixer_finish, n_head),
        sc,
        (slabs, u, cum, y_local, pay, ds, o),
        [s_slabs, block(f_u, "i", 0, 0), block(f_c, "i", 0, 0), block(f_y, "i", 0, 0), s_z, s_ds, s_o],
        [((TP, SPAN, 256), BF), ((TP, SPAN, MW), F32), ((TP, MW, STATE), F32)],
        [block((1, SPAN, 256), "i", 0, 0), block(f_y, "i", 0, 0), s_state],
        [pltpu.VMEM((TP, MW, STATE), F32)],
        "mixer_finish",
    )
    branch = branch.reshape(TP * SPAN, 256)

    def to_tokens(partial):
        return lax.psum_scatter(partial.astype(BF), "tp", tiled=True).astype(F32)

    mixed = tokens.astype(F32) + to_tokens(dot(branch, w_out))
    ffn_local, inv_ffn = norm_parts(mixed, gain_ffn)
    ffn_in = lax.all_gather(ffn_local.astype(BF), "tp", tiled=True)
    gate = dot(ffn_in, w_gu[:, :ff_part])
    up = dot(ffn_in, w_gu[:, ff_part:])
    sig = sigmoid(gate)
    hidden = (gate * sig * up).astype(BF)
    result = (mixed + to_tokens(dot(hidden, w_dn))).astype(BF)

    d_hidden = dot_rt(cot_all, w_dn)
    g_down = dot_lt(hidden, cot_all)
    d_gate = (d_hidden * up * sig * (1.0 + gate * (1.0 - sig))).astype(BF)
    d_up = (d_hidden * gate * sig).astype(BF)
    d_gu = jnp.concatenate([d_gate, d_up], axis=1)
    g_gu = dot_lt(ffn_in, d_gu)
    d_ffn = to_tokens(dot_rt(d_gu, w_gu))
    d_norm, grad_gain_ffn = norm_back(mixed, inv_ffn, gain_ffn, d_ffn)
    d_mixed = cotangent.astype(F32) + d_norm
    d_branch = lax.all_gather(d_mixed.astype(BF), "tp", tiled=True)
    g_out = dot_lt(branch, d_branch)
    dh = dot_rt(d_branch, w_out).astype(BF).reshape(TP, SPAN, 256)
    s_dh = block((1, SPAN, 256), "i", 0, 0)
    (d_entry,) = call(
        mixer_entry,
        sc,
        (dh, u, cum, pay, ds),
        [s_dh, block(f_u, "i", 0, 0), block(f_c, "i", 0, 0), s_z, s_ds],
        [((TP, MW, STATE), BF)],
        [s_state],
        [],
        "mixer_entry",
    )
    d_entries = lax.all_gather(d_entry, SEQ)
    dq, dkv = call(
        functools.partial(attend_back, n_head),
        sc,
        (pay, ds, dh, o, lse, kv),
        [s_q, s_ds, block((1, SPAN, 128), "i", 0, 0), s_o, s_ds, s_kv],
        [((TP, SPAN, 128), F32), ((n_win, TP, SPAN, 128), BF)],
        [s_o, s_kv],
        [pltpu.VMEM((n_win, TP, SPAN, 128), F32)],
        "attend_back",
    )
    if n_grp > 1:
        back = lax.ppermute(dkv[:n_head], "grp", [(a + 1, a) for a in range(n_grp - 1)])
        dkv = dkv[n_head:] + back
    dkv = lax.psum_scatter(dkv, "head", scatter_dimension=0, tiled=True)[0]
    d_pay, d_taps, d_small = call(
        functools.partial(mixer_back, n_head),
        sc,
        (slabs, d_entries, dh, pay, ds, state_in, y_all, dq, dkv) + params,
        [s_slabs, whole((n_seq, TP, MW, STATE)), s_dh, s_pay, s_ds, s_state]
        + [block(f_y, "i", 0, 0), s_o, s_o]
        + s_params,
        [((TP, RIM + SPAN, COLS), BF), ((8, CH), F32), ((8, STATE), F32)],
        [s_pay, whole((8, CH)), whole((8, STATE))],
        [pltpu.VMEM((TP, MW, STATE), F32)],
        "mixer_back",
    )
    d_pay = d_pay.reshape(TP * (RIM + SPAN), COLS)
    g_in = dot_lt(normed, d_pay)
    d_norm_in = to_tokens(dot_rt(d_pay, w_in))
    rim_back = lax.ppermute(d_norm_in[:RIM].astype(BF), ALL, [(f + 1, f) for f in range(n_dev - 1)])
    d_norm_in = d_norm_in[RIM:].at[rows - RIM :].add(rim_back.astype(F32))
    tok = tokens.astype(F32)
    inv_mix = norm_parts(tok, gain_mix)[1]
    d_tok, grad_gain_mix = norm_back(tok, inv_mix, gain_mix, d_norm_in)
    grad_tokens = d_mixed + d_tok

    def scatter_cols(grad):
        ordered = grad.reshape(n_grp, TP, n_head, r, -1).transpose(0, 2, 1, 3, 4)
        ordered = ordered.reshape(n_seq, TP, r, -1).astype(BF)
        mine = lax.psum_scatter(ordered, SEQ, scatter_dimension=0, tiled=True)[0]
        return lax.all_to_all(mine, "tp", 0, 0, tiled=True).astype(F32)

    parts = scatter_cols(g_in)
    parts_gu = scatter_cols(g_gu)

    def join_tp(p):
        return p.transpose(1, 0, 2).reshape(r, -1)

    def join_kv(p):
        return join_tp(jnp.sum(p.reshape(KVHEADS, TP // KVHEADS, r, HDIM), axis=1))

    def join_ff(p):
        return p.reshape(TP, r, n_grp, -1).transpose(1, 2, 0, 3).reshape(r, ff)

    grad_qkv = jnp.concatenate(
        [
            join_tp(parts[:, :, COL_Q : COL_Q + HDIM]),
            join_kv(parts[:, :, COL_KV + HDIM :]),
            join_kv(parts[:, :, COL_KV : COL_KV + HDIM]),
        ],
        axis=1,
    )
    grad_min = jnp.concatenate(
        [
            join_tp(parts[:, :, COL_Z : COL_Z + MW]),
            join_tp(parts[:, :, 2 * STATE : CH]),
            jnp.sum(parts[:, :, : 2 * STATE], axis=0),
            join_tp(parts[:, :, COL_DT : COL_DT + MH]),
        ],
        axis=1,
    )
    grad_gate = join_ff(parts_gu[:, :, :ff_part])
    grad_up = join_ff(parts_gu[:, :, ff_part:])
    grad_down = lax.psum_scatter(g_down.astype(BF), SEQ, tiled=True).astype(F32)
    if n_grp == 1:
        grad_ao = lax.psum_scatter(g_out[:HDIM].astype(BF), SEQ, tiled=True).astype(F32)
        grad_mo = lax.psum_scatter(g_out[HDIM:].astype(BF), SEQ, tiled=True).astype(F32)
    else:
        full = jnp.zeros((q_total, width), F32)
        full = lax.dynamic_update_slice_in_dim(full, g_out[:HDIM], t * HDIM, 0)
        grad_ao = lax.psum_scatter(full, ALL, tiled=True)
        full = jnp.zeros((m_total, width), F32)
        full = lax.dynamic_update_slice_in_dim(full, g_out[HDIM:], t * MW, 0)
        grad_mo = lax.psum_scatter(full, ALL, tiled=True)
    conv_grad = jnp.zeros((CONVW + 1, m_total + 2 * STATE), F32)
    conv_grad = lax.dynamic_update_slice_in_dim(
        conv_grad, d_taps[: CONVW + 1, 2 * STATE :], t * MW, 1
    )
    conv_grad = conv_grad.at[:, m_total:].set(d_taps[: CONVW + 1, : 2 * STATE])
    conv_grad = lax.psum_scatter(conv_grad, ALL, scatter_dimension=1, tiled=True)
    gains = lax.psum_scatter(
        jnp.stack([grad_gain_mix, grad_gain_ffn]), ALL, scatter_dimension=1, tiled=True
    )
    small = jnp.zeros((3, MHEADS), F32)
    small = lax.dynamic_update_slice_in_dim(small, d_small[:3, :MH], t * MH, 1)
    small = lax.psum(small, ALL)
    per_head = MHEADS // n_head
    small = lax.dynamic_slice_in_dim(small, h * per_head, per_head, 1)
    return (
        result,
        grad_tokens,
        gains[0],
        grad_qkv,
        grad_min,
        conv_grad[:CONVW],
        conv_grad[CONVW],
        small[0],
        small[1],
        small[2],
        grad_ao,
        grad_mo,
        gains[1],
        grad_gate,
        grad_up,
        grad_down,
    )


def solution(mesh):
    n_blk, n_head = mesh.devices.shape
    n_grp = n_blk // TP
    fine = Mesh(mesh.devices.reshape(n_grp, TP, n_head), ALL)
    row = P(ALL, None)
    vec = P(ALL)
    col = P(None, ALL)
    head = P("head")
    in_specs = (
        (row, vec, row, row, col, vec, head, head, head, row, row, vec, row, row, row, P(), row)
    )
    out_specs = (
        (row, row, vec, row, row, col, vec, head, head, head, row, row, vec, row, row, row)
    )
    return jax.shard_map(
        functools.partial(per_device, n_grp, n_head),
        mesh=fine,
        in_specs=in_specs,
        out_specs=out_specs,
        check_vma=False,
    )
```

time: 2070 us -> 1130 us (0.55)
  waiting for transfers between devices: 862 us -> 565 us
  local copies, waits for them, and re-layouts: 286 us -> 44.5 us
  matrix products: 299 us -> 65.3 us
  other arithmetic: 212 us -> 26.9 us
  Pallas kernels: 0 us -> 144 us
  blocking collectives: 332 us -> 247 us
  starting transfers between devices: 38.5 us -> 13.3 us
    reduce_scatter x7 -> x8, waiting for transfers between devices: 720 us -> 209 us  [the longest x4 169 us: to_tokens(): return lax.psum_scatter(partial.astype(BF), 'tp', tiled=True).astype(F32)]
    dot_general x94 -> x13, matrix products: 299 us -> 65.3 us  [the longest x4 23.2 us: dot_rt(): lax.dot_general(a, b, (((1,), (1,)), ((), ())), preferred_element_type=F32)]
    unnamed x14 -> x21, waiting for transfers between devices: 4.45 us -> 198 us
    pallas_call x0 -> x6, Pallas kernels: none -> 144 us  [call(): pl.pallas_call(kernel, out_shape=[jax.ShapeDtypeStruct(s, d) for s, d in...]
    dynamic_update_slice x54 -> x2, local copies, waits for them, and re-layouts: 99.3 us -> 0.43 us  [the longest x1 0.28 us: per_device(): lax.dynamic_update_slice_in_dim(conv_grad, d_taps[:CONVW + 1, 2 * STATE:]...]
    all_gather x7 -> x9, waiting for transfers between devices: 80.8 us -> 145 us  [the longest x1 36.7 us: per_device(): d_branch = lax.all_gather(d_mixed.astype(BF), 'tp', tiled=True)]
    unnamed x265 -> x89, local copies, waits for them, and re-layouts: 61.5 us -> 11.4 us
    convert_element_type x31 -> x12, other arithmetic: 57.3 us -> 11.3 us  [the longest x1 2.26 us: per_device(): d_branch = lax.all_gather(d_mixed.astype(BF), 'tp', tiled=True)]
  transfers between devices with their start and end apart: 27 -> 23, of which waited for: 11 -> 16; matrix products, arithmetic and copies ran while one was open for 38% -> 7% of each run, Pallas kernels for 0% -> 11%
where the time goes in v1:
time: 1130 us; the launch traced here: 1120 us
  waiting for transfers between devices  565 us (50%)
  blocking collectives  247 us (22%)
  Pallas kernels  144 us (13%)
  matrix products  65.3 us (6%)
  local copies, waits for them, and re-layouts  44.5 us (4%)
  other arithmetic  26.9 us (2%)
  between operations  15.3 us (1%)
  starting transfers between devices  13.3 us (1%)
    unnamed x21, waiting for transfers between devices  198 us
    reduce_scatter x4, waiting for transfers between devices, to_tokens(): return lax.psum_scatter(partial.astype(BF), 'tp', tiled=True).astype(F32)  169 us
    pallas_call x6, Pallas kernels, call(): pl.pallas_call(kernel, out_shape=[jax.ShapeDtypeStruct(s, d) for s, d in...  144 us
    unnamed x2, blocking collectives  87.1 us
    all_gather x1, blocking collectives, per_device(): lax.all_gather(jnp.concatenate([conv_w, conv_b[None]], axis=0), ALL)  70.3 us
    reduce_scatter x1, waiting for transfers between devices, per_device(): dkv = lax.psum_scatter(dkv, 'head', scatter_dimension=0, tiled=True)[0]  39.3 us
    all_gather x1, waiting for transfers between devices, per_device(): d_branch = lax.all_gather(d_mixed.astype(BF), 'tp', tiled=True)  36.7 us
    all_gather x1, waiting for transfers between devices, per_device(): cot_all = lax.all_gather(cotangent, 'tp', tiled=True)  36.6 us
  transfers between devices with their start and end apart: 23, of which 16 were waited for; matrix products, arithmetic and copies ran while one was open for 7% of the time, Pallas kernels for 11%

profile of v1, /device:TPU:0, one launch (start us, length us, event | category | flops | bytes accessed | tf_op | source)
XLA Modules:
  0.0 1121.9 jit_solution(15771104461772931599)
XLA Ops:
  12.5 14.1 %all_to_all.20 = bf16[8,32,896]{2,1,0:T(8,128)(2,1)} all-to-all(bf16[8,32,896]{2,1,0:T(8,128)(2,1)S(1)} %concatenate.36), channel_id=1, replica_groups=mesh['blk'=8,'head'=4] {'blk'}, dimensions={0} | all-to-all | bytes 917504 | tf_op jit(solution)/shard_map/all_to_all | solution.py:512
  33.1 43.1 %all-reduce.8 = (bf16[1024]{0:T(1024)(128)(2,1)S(1)}, bf16[1024]{0:T(1024)(128)(2,1)S(1)}) all-reduce(bf16[1024]{0:T(1024)(128)(2,1)S(1)} %dynamic-update-slice.6, bf16[1024]{0:T(1024)(128)(2,1)S(1)} %dynamic-update-slice.7), channel_id=1, replica_groups=mesh['blk'=8,'head'=4] {'blk','head'}, use_global_device_ids=true, to_apply=%add.2 | all-reduce | flops 2048 | bytes 8192
  78.1 28.9 %all-gather.18.cloned.1.call-done = bf16[2112,1024]{1,0:T(8,128)(2,1)} async-done(((bf16[264,1024]{1,0:T(8,128)(2,1)}), bf16[2112,1024]{1,0:T(8,128)(2,1)}) %all-gather.18.cloned.1.call-update) | async-done | bytes 4325392 | tf_op jit(solution)/shard_map/all_gather | solution.py:557
  107.0 6.4 copy.198
  126.4 70.3 %all-gather.6 = bf16[32,5,56]{2,1,0:T(8,128)(2,1)S(1)} all-gather(bf16[1,5,56]{2,1,0:T(8,128)(2,1)S(1)} %maximum_bitcast_fusion), channel_id=3, replica_groups=mesh['blk'=8,'head'=4] {'blk','head'}, dimensions={0}, use_global_device_ids=true | all-gather | bytes 18480 | tf_op jit(solution)/shard_map/all_gather | solution.py:533
  196.9 11.9 %all-gather.7 = f32[4,6,3]{1,2,0:T(4,128)S(1)} all-gather(f32[1,6,3]{1,2,0:T(4,128)S(1)} %maximum_bitcast_fusion.1), channel_id=1, replica_groups=mesh['blk'=8,'head'=4] {'head'}, dimensions={0}, use_global_device_ids=true | all-gather | bytes 360 | tf_op jit(solution)/shard_map/all_gather | solution.py:540
  213.1 20.4 %mixer_local.1 = (f32[8,256,448]{2,1,0:T(8,128)}, f32[8,256,128]{2,1,0:T(8,128)}, f32[8,256,192]{2,1,0:T(8,128)}, bf16[8,200,128]{2,1,0:T(8,128)(2,1)}) custom-call(s32[5,8]{1,0:T(8,128)} %stack.26.sc, bf16[8,264,896]{2,1,0:T(8,128)(2,1)} %bitcast.179, s32[8,256,1]{2,1,0:T(8,128)} %copy.209.ds, f32[8,448]{1,0:T(8,128)} %concatenate.39.taps, ...), custom_call_target="tpu_custom_call" | custom-call | tf_op jit(solution)/shard_map/mixer_local/pallas_call | solution.py:422
  233.6 14.4 %all_gather.77 = bf16[64,1024]{1,0:T(8,128)(2,1)S(1)} all-gather(bf16[16,1024]{1,0:T(8,128)(2,1)S(1)} %copy-done.15), channel_id=1, replica_groups=mesh['blk'=8,'head'=4] {'head'}, dimensions={0}, use_global_device_ids=true | all-gather | bytes 163840 | tf_op jit(solution)/shard_map/all_gather | solution.py:520
  248.0 17.7 %all_gather.78 = bf16[192,1024]{1,0:T(8,128)(2,1)S(1)} all-gather(bf16[48,1024]{1,0:T(8,128)(2,1)S(1)} %copy-done.14), channel_id=1, replica_groups=mesh['blk'=8,'head'=4] {'head'}, dimensions={0}, use_global_device_ids=true | all-gather | bytes 491520 | tf_op jit(solution)/shard_map/all_gather | solution.py:521
  265.8 25.9 %attend.1 = (f32[8,256,128]{2,1,0:T(8,128)}, f32[8,256,1]{2,1,0:T(8,128)}) custom-call(s32[5,8]{1,0:T(8,128)} %stack.26.sc, bf16[8,264,896]{2,1,0:T(8,128)(2,1)} %bitcast.180, s32[8,256,1]{2,1,0:T(8,128)} %copy.209.ds, bf16[4,8,256,128]{3,2,1,0:T(8,128)(2,1)} %bitcast.188), custom_call_target="tpu_custom_call" | custom-call | tf_op jit(solution)/shard_map/attend/pallas_call | solution.py:422
  291.7 11.8 %mixer_finish.1 = (bf16[8,256,256]{2,1,0:T(8,128)(2,1)}, f32[8,256,192]{2,1,0:T(8,128)}, f32[8,192,128]{2,1,0:T(8,128)}) custom-call(s32[5,8]{1,0:T(8,128)} %stack.26.sc, bf16[4,8,200,128]{3,2,1,0:T(8,128)(2,1)} %bitcast.190, f32[8,256,448]{2,1,0:T(8,128)} %get-tuple-element.55.u, f32[8,256,128]{2,1,0:T(8,128)} %get-tuple-element.56.cum, ...), custom_call_target="tpu_custom_call" | custom-call | tf_op jit(solution)/shard_map/mixer_finish/pallas_call | solution.py:422
  309.2 10.0 all_to_all.21
  320.0 47.6 %reduce-scatter.19.cloned.1.call-done = bf16[256,1024]{1,0:T(8,128)(2,1)} async-done(((bf16[2048,1024]{1,0:T(8,128)(2,1)}), bf16[256,1024]{1,0:T(8,128)(2,1)}) %reduce-scatter.19.cloned.1.call-update) | async-done | bytes 524304 | tf_op jit(solution)/shard_map/reduce_scatter | solution.py:623
  371.1 21.8 %all_gather.83 = bf16[256,1024]{1,0:T(8,128)(2,1)S(1)} all-gather(bf16[64,1024]{1,0:T(8,128)(2,1)S(1)} %copy-done.11), channel_id=1, replica_groups=mesh['blk'=8,'head'=4] {'head'}, dimensions={0}, use_global_device_ids=true | all-gather | bytes 655360 | tf_op jit(solution)/shard_map/all_gather | solution.py:530
  392.9 8.8 all-gather.32.cloned.1.call-done
  403.0 36.6 %all-gather.22.cloned.1.call-done = bf16[2048,1024]{1,0:T(8,128)(2,1)} async-done(((bf16[256,1024]{1,0:T(8,128)(2,1)}), bf16[2048,1024]{1,0:T(8,128)(2,1)}) %all-gather.22.cloned.1.call-update) | async-done | bytes 4194320 | tf_op jit(solution)/shard_map/all_gather | solution.py:558
  444.4 34.3 %all-gather.20.cloned.1.call-done = bf16[2048,1024]{1,0:T(8,128)(2,1)} async-done(((bf16[256,1024]{1,0:T(8,128)(2,1)}), bf16[2048,1024]{1,0:T(8,128)(2,1)}) %all-gather.20.cloned.1.call-update) | async-done | bytes 4194320 | tf_op jit(solution)/shard_map/all_gather | solution.py:627
  491.1 51.1 %reduce-scatter.23.cloned.1.call-done = bf16[256,1024]{1,0:T(8,128)(2,1)} async-done(((bf16[2048,1024]{1,0:T(8,128)(2,1)}), bf16[256,1024]{1,0:T(8,128)(2,1)}) %reduce-scatter.23.cloned.1.call-update) | async-done | bytes 524304 | tf_op jit(solution)/shard_map/reduce_scatter | solution.py:623
  546.1 36.7 %all-gather.24.cloned.1.call-done = bf16[2048,1024]{1,0:T(8,128)(2,1)} async-done(((bf16[256,1024]{1,0:T(8,128)(2,1)}), bf16[2048,1024]{1,0:T(8,128)(2,1)}) %all-gather.24.cloned.1.call-update) | async-done | bytes 4194320 | tf_op jit(solution)/shard_map/all_gather | solution.py:643
  587.4 10.4 mixer_entry.1
  597.8 31.9 %attend_back.1 = (f32[8,256,128]{2,1,0:T(8,128)}, bf16[4,8,256,128]{3,2,1,0:T(8,128)(2,1)}) custom-call(s32[5,8]{1,0:T(8,128)} %stack.26.sc, bf16[8,264,896]{2,1,0:T(8,128)(2,1)} %bitcast.183, s32[8,256,1]{2,1,0:T(8,128)} %copy.209.ds, bf16[8,256,256]{2,1,0:T(8,128)(2,1)} %bitcast.186, f32[8,256,128]{2,1,0:T(8,128)} %get-tuple-element.58.o, ...), custom_call_target="tpu_custom_call" | custom-call | tf_op jit(solution)/shard_map/attend_back/pallas_call | solution.py:422
  639.5 6.2 convolution_convert_fusion.6
  646.8 39.3 %reduce-scatter.25.cloned.1.call-done = bf16[1,8,256,128]{3,2,1,0:T(8,128)(2,1)} async-done(((bf16[4,8,256,128]{3,2,1,0:T(8,128)(2,1)}), bf16[1,8,256,128]{3,2,1,0:T(8,128)(2,1)}) %reduce-scatter.25.cloned.1.call-update) | async-done | bytes 524304 | tf_op jit(solution)/shard_map/reduce_scatter | solution.py:671
  686.1 44.0 %mixer_back.1 = (bf16[8,264,896]{2,1,0:T(8,128)(2,1)}, f32[8,448]{1,0:T(8,128)}, f32[8,128]{1,0:T(8,128)}) custom-call(s32[5,8]{1,0:T(8,128)} %stack.26.sc, bf16[4,8,200,128]{3,2,1,0:T(8,128)(2,1)} %bitcast.191, bf16[4,8,192,128]{3,2,1,0:T(8,128)(2,1)} %bitcast.199, bf16[8,256,256]{2,1,0:T(8,128)(2,1)} %bitcast.187, bf16[8,264,896]{2,1,0:T(8,128)(2,1)} %bitcast.184, ...), custom_call_target="tpu_custom_call" | custom-call | tf_op jit(solution)/shard_map/mixer_back/pallas_call | solution.py:422
  730.0 8.9 convert_bitcast_fusion
  739.0 9.4 convolution_convert_fusion
  759.1 43.9 %all-reduce.7 = (f32[5,1792]{1,0:T(8,128)S(1)}, f32[3,24]{1,0:T(4,128)S(1)}) all-reduce(f32[5,1792]{1,0:T(8,128)S(1)} %slice_dynamic-update-slice_fusion, f32[3,24]{1,0:T(4,128)S(1)} %dynamic_update_slice.7), channel_id=15, replica_groups=mesh['blk'=8,'head'=4] {'blk','head'}, use_global_device_ids=true, to_apply=%region_19.20.clone | all-reduce | flops 9032 | bytes 72256
  804.2 61.6 %all-reduce.12.cloned.1.call-done = (bf16[4,8,32,896]{3,2,0,1:T(8,128)(2,1)}, bf16[4,8,32,512]{3,2,0,1:T(8,128)(2,1)}) async-done(((bf16[4,8,32,896]{3,2,0,1:T(8,128)(2,1)}, bf16[4,8,32,512]{3,2,0,1:T(8,128)(2,1)}), (bf16[4,8,32,896]{3,2,0,1:T(8,128)(2,1)}, bf16[4,8,32,512]{3,2,0,1:T(8,128)(2,1)})) %all-reduce.12.cloned.1.call-update) | async-done | bytes 2883600
  884.2 6.8 all-to-all-done.2
  895.5 24.5 %reduce-scatter.27.cloned.1.call-done = bf16[264,1024]{1,0:T(8,128)(2,1)} async-done(((bf16[2112,1024]{1,0:T(8,128)(2,1)}), bf16[264,1024]{1,0:T(8,128)(2,1)}) %reduce-scatter.27.cloned.1.call-update) | async-done | bytes 540688 | tf_op jit(solution)/shard_map/reduce_scatter | solution.py:623
  928.4 46.0 %reduce-scatter.21.cloned.1.call-done = bf16[256,1024]{1,0:T(8,128)(2,1)} async-done(((bf16[2048,1024]{1,0:T(8,128)(2,1)}), bf16[256,1024]{1,0:T(8,128)(2,1)}) %reduce-scatter.21.cloned.1.call-update) | async-done | bytes 524304 | tf_op jit(solution)/shard_map/reduce_scatter | solution.py:623
  977.3 135.6 %reduce-scatter.35.cloned.1.call-done = f32[32,2]{1,0:T(8,128)} async-done(((f32[1024,2]{1,0:T(8,128)}), f32[32,2]{1,0:T(8,128)}) %reduce-scatter.35.cloned.1.call-update) | async-done | bytes 272
  (268 shorter events, 126.3 us)
Async XLA Ops:
  7.2 69.0 %all-gather.26.cloned.1.call-start = ((), (), s32[]{:S(2)}) async-start(), calls=%async_computation.25 | async-start | bytes 2293760 | tf_op jit(solution)/shard_map/all_gather | solution.py:513
  26.7 80.3 %all-gather.18.cloned.1.call-start = ((), (), s32[]{:S(2)}) async-start(), calls=%async_computation.13 | async-start | bytes 4866048 | tf_op jit(solution)/shard_map/all_gather | solution.py:557
  26.8 4.9 collective-permute-start
  32.5 233.3 %all-gather.30.cloned.1.call-start = ((), (), s32[]{:S(2)}) async-start(), calls=%async_computation.27 | async-start | bytes 2621440 | tf_op jit(solution)/shard_map/all_gather | solution.py:589
  118.2 78.7 %copy-start.26 = (f32[6]{0:T(128)S(1)}, f32[6]{0:T(128)}, u32[]{:S(2)}) copy-start(f32[6]{0:T(128)} %param.29) | copy-start | bytes 76
  126.1 107.5 %copy-start.15 = (bf16[16,1024]{1,0:T(8,128)(2,1)S(1)}, bf16[16,1024]{1,0:T(8,128)(2,1)}, u32[]{:S(2)}) copy-start(bf16[16,1024]{1,0:T(8,128)(2,1)} %param.30) | copy-start | bytes 98308
  126.1 165.6 %all-gather.28.cloned.1.call-start = ((), (), s32[]{:S(2)}) async-start(), calls=%async_computation.26 | async-start | bytes 2048000 | tf_op jit(solution)/shard_map/all_gather | solution.py:593
  126.4 121.6 %copy-start.14 = (bf16[48,1024]{1,0:T(8,128)(2,1)S(1)}, bf16[48,1024]{1,0:T(8,128)(2,1)}, u32[]{:S(2)}) copy-start(bf16[48,1024]{1,0:T(8,128)(2,1)} %param.31) | copy-start | bytes 294916
  233.6 134.1 %reduce-scatter.19.cloned.1.call-start = ((), (), s32[]{:S(2)}) async-start(), calls=%async_computation.14 | async-start | bytes 4718592 | tf_op jit(solution)/shard_map/reduce_scatter | solution.py:623
  308.1 93.5 %all-gather.32.cloned.1.call-start = ((), (), s32[]{:S(2)}) async-start(), calls=%async_computation.28 | async-start | bytes 1310720 | tf_op jit(solution)/shard_map/all_gather | solution.py:513
  319.2 120.4 %all-gather.22.cloned.1.call-start = ((), (), s32[]{:S(2)}) async-start(), calls=%async_computation.17 | async-start | bytes 4718592 | tf_op jit(solution)/shard_map/all_gather | solution.py:558
  320.0 158.7 %all-gather.20.cloned.1.call-start = ((), (), s32[]{:S(2)}) async-start(), calls=%async_computation.15 | async-start | bytes 4718592 | tf_op jit(solution)/shard_map/all_gather | solution.py:627
  369.0 174.7 %copy-start.17 = (f32[256]{0:T(256)}, f32[256]{0:T(256)S(1)}, u32[]{:S(2)}) copy-start(f32[256]{0:T(256)S(1)} %get-tuple-element.106) | copy-start | bytes 3076
  371.0 171.1 %reduce-scatter.23.cloned.1.call-start = ((), (), s32[]{:S(2)}) async-start(), calls=%async_computation.18 | async-start | bytes 4718592 | tf_op jit(solution)/shard_map/reduce_scatter | solution.py:623
  490.8 91.9 %all-gather.24.cloned.1.call-start = ((), (), s32[]{:S(2)}) async-start(), calls=%async_computation.19 | async-start | bytes 4718592 | tf_op jit(solution)/shard_map/all_gather | solution.py:643
  546.0 100.8 %all-gather.34.cloned.1.call-start = ((), (), s32[]{:S(2)}) async-start(), calls=%async_computation.29 | async-start | bytes 1966080 | tf_op jit(solution)/shard_map/all_gather | solution.py:657
  597.8 88.3 %reduce-scatter.25.cloned.1.call-start = ((), (), s32[]{:S(2)}) async-start(), calls=%async_computation.20 | async-start | bytes 2621440 | tf_op jit(solution)/shard_map/reduce_scatter | solution.py:671
  629.7 123.6 %reduce-scatter.33.cloned.1.call-start = ((), (), s32[]{:S(2)}) async-start(), calls=%async_computation.24 | async-start | bytes 655360 | tf_op jit(solution)/shard_map/reduce_scatter | solution.py:731
  634.1 121.5 %reduce-scatter.29.cloned.1.call-start = ((), (), s32[]{:S(2)}) async-start(), calls=%async_computation.22 | async-start | bytes 163840 | tf_op jit(solution)/shard_map/reduce_scatter | solution.py:733
  639.4 117.5 %reduce-scatter.31.cloned.1.call-start = ((), (), s32[]{:S(2)}) async-start(), calls=%async_computation.23 | async-start | bytes 491520 | tf_op jit(solution)/shard_map/reduce_scatter | solution.py:734
  646.5 219.2 %all-reduce.12.cloned.1.call-start = ((), (), s32[]{:S(2)}) async-start(), calls=%async_computation.31 | async-start | bytes 5767168
  739.0 181.1 %reduce-scatter.27.cloned.1.call-start = ((), (), s32[]{:S(2)}) async-start(), calls=%async_computation.21 | async-start | bytes 4866048 | tf_op jit(solution)/shard_map/reduce_scatter | solution.py:623
  748.5 226.0 %reduce-scatter.21.cloned.1.call-start = ((), (), s32[]{:S(2)}) async-start(), calls=%async_computation.16 | async-start | bytes 4718592 | tf_op jit(solution)/shard_map/reduce_scatter | solution.py:623
  868.1 10.6 all-to-all-start.3
  878.6 12.4 %all-to-all-start.2 = ((bf16[8,32,896]{2,1,0:T(8,128)(2,1)}), bf16[8,32,896]{2,1,0:T(8,128)(2,1)S(1)}, u32[]{:S(2)}, u32[]{:S(2)}) async-start(bf16[8,32,896]{2,1,0:T(8,128)(2,1)} %dynamic-slice_bitcast_fusion), calls=%async_computation.7 | async-start | bytes 917504 | tf_op jit(solution)/shard_map/all_to_all | solution.py:698
  882.1 230.8 %reduce-scatter.35.cloned.1.call-start = ((), (), s32[]{:S(2)}) async-start(), calls=%async_computation.30 | async-start | bytes 540672
  893.9 80.5 %copy-start.5 = (bf16[256,1024]{1,0:T(8,128)(2,1)S(1)}, bf16[256,1024]{1,0:T(8,128)(2,1)}, u32[]{:S(2)}) copy-start(bf16[256,1024]{1,0:T(8,128)(2,1)} %reduce-scatter.23.cloned.1.call-done) | copy-start | bytes 1572868
  895.5 79.0 %copy-start.18 = (f32[256]{0:T(256)S(1)}, f32[256]{0:T(256)}, u32[]{:S(2)}) copy-start(f32[256]{0:T(256)} %copy-done.17) | copy-start | bytes 3076
  895.5 79.0 %copy-start.19 = (f32[256]{0:T(256)S(1)}, f32[256]{0:T(256)}, u32[]{:S(2)}) copy-start(f32[256]{0:T(256)} %get-tuple-element.105) | copy-start | bytes 3076
  895.5 79.0 %copy-start.21 = (f32[256]{0:T(256)S(1)}, f32[256]{0:T(256)}, u32[]{:S(2)}) copy-start(f32[256]{0:T(256)} %copy-done.20) | copy-start | bytes 3076
  895.5 79.0 %copy-start.22 = (f32[256]{0:T(256)S(1)}, f32[256]{0:T(256)}, u32[]{:S(2)}) copy-start(f32[256]{0:T(256)} %get-tuple-element.104) | copy-start | bytes 3076
  920.8 5.6 collective-permute-start.1
  (28 other events, 584.3 us)
Sparse Core Ops, SparseCore 0:
  26.8 41.6 all-gather.25
  71.0 35.9 all-gather.17
  126.3 46.4 all-gather.29
  233.7 41.6 all-gather.27
  308.3 59.3 reduce-scatter.18
  369.1 32.5 all-gather.31
  403.6 35.9 all-gather.21
  442.0 36.5 all-gather.19
  491.0 51.1 reduce-scatter.22
  546.1 36.5 all-gather.23
  597.9 36.9 all-gather.33
  637.0 49.0 reduce-scatter.24
  688.4 21.0 reduce-scatter.32
  712.1 17.6 reduce-scatter.28
  732.5 18.9 reduce-scatter.30
  753.8 111.8 all-reduce.11
  869.0 50.9 reduce-scatter.26
  923.3 51.1 reduce-scatter.20
  976.7 136.1 reduce-scatter.34

commit v2 on v1

--- a/solution.py
+++ b/solution.py
@@ -159,10 +159,10 @@
             def _():
                 states[ic] = state
 
-            slab = slabs[sp, ic]
+            slab = slabs[c]
             return keep_wide(slab) * state + slab[:MW].astype(F32)
 
-        total = slabs.shape[0] * TP
+        total = slabs.shape[0]
         lax.fori_loop(0, total, one, jnp.zeros((MW, STATE), F32))
 
     first = sc[0, i]
@@ -214,16 +214,17 @@
 
     @pl.when(i == 0)
     def _():
-        total = slabs.shape[0] * TP
+        total = slabs.shape[0]
 
         def one(step, adj):
-            sp, ic = place_of(total - 1 - step, n_head)
+            c = total - 1 - step
+            sp, ic = place_of(c, n_head)
 
             @pl.when(sp == mine)
             def _():
                 carried[ic] = adj
 
-            return keep_wide(slabs[sp, ic]) * adj + d_entries[sp, ic].astype(F32)
+            return keep_wide(slabs[c]) * adj + d_entries[c].astype(F32)
 
         lax.fori_loop(0, total, one, jnp.zeros((MW, STATE), F32))
         dtap_out[...] = jnp.zeros_like(dtap_out)
@@ -349,9 +350,8 @@
 
     def one(c, carry):
         top, total, acc = carry
-        sp, ic = place_of(c, n_head)
-        sp = sp - base
-        keys = kv[sp, ic]
+        slot = c - base
+        keys = kv[slot]
         s = dot_rt(q, keys)
         key = c * SPAN + iota((SPAN, SPAN), 1)
         s = jnp.where((key >= start) & (key <= pos), s, NEG)
@@ -389,15 +389,14 @@
     sums = lse[0]
 
     def one(c, d_q):
-        sp, ic = place_of(c, n_head)
-        sp = sp - base
-        keys = kv[sp, ic]
+        slot = c - base
+        keys = kv[slot]
         s = dot_rt(q, keys)
         key = c * SPAN + iota((SPAN, SPAN), 1)
         p = jnp.exp(jnp.where((key >= start) & (key <= pos), s - sums, NEG))
         dp = dot_rt(do, keys)
         d_s = (p * (dp - delta)).astype(BF)
-        acc_kv[sp, ic] += dot_lt(d_s, q) + dot_lt(p.astype(BF), do)
+        acc_kv[slot] += dot_lt(d_s, q) + dot_lt(p.astype(BF), do)
         return d_q + dot(d_s, keys)
 
     dq_out[0] = lax.fori_loop(low, mine + 1, one, jnp.zeros((SPAN, 128), F32)) * scale
@@ -434,6 +433,388 @@
         ),
         name=name,
     )(sc, *ins)
+
+
+class Job:
+    def __init__(self, x, out, scratch, sems, peers, steps, plain):
+        self.x, self.out, self.scratch, self.sems = x, out, scratch, sems
+        self.peers, self.steps, self.plain = peers, steps, plain
+
+
+class Spot:
+    def __init__(self, n_head):
+        self.n_head = n_head
+        self.g = lax.axis_index("grp")
+        self.t = lax.axis_index("tp")
+        self.h = lax.axis_index("head")
+
+    def plane(self, k):
+        return (self.g, self.t ^ k, self.h)
+
+    def line(self, k):
+        return (self.g, self.t, lax.rem(self.h + k + self.n_head, self.n_head))
+
+    def chunk(self, k):
+        count = TP * self.n_head
+        f = lax.rem(self.t * self.n_head + self.h + k + count, count)
+        return (self.g, f // self.n_head, lax.rem(f, self.n_head))
+
+
+def communicate(name, cid, n_grp, n_head, jobs):
+    if n_grp > 1 or n_head != 4:
+        return [job.plain(n_grp, n_head) for job in jobs]
+
+    def kernel(*refs):
+        spot = Spot(n_head)
+        n = len(jobs)
+        ins, outs, rest = refs[:n], refs[n : 2 * n], list(refs[2 * n :])
+        barrier = pltpu.get_barrier_semaphore()
+        total = 0
+        for job in jobs:
+            for peer in job.peers(spot):
+                pl.semaphore_signal(
+                    barrier, inc=1, device_id=peer, device_id_type=pl.DeviceIdType.MESH
+                )
+                total += 1
+        pl.semaphore_wait(barrier, total)
+        running = []
+        for job, x, out in zip(jobs, ins, outs):
+            scratch = [rest.pop(0) for _ in job.scratch]
+            send_sem, recv_sem, own_sem = rest.pop(0), rest.pop(0), rest.pop(0)
+
+            def send(src, dst, k, peer, send_sem=send_sem, recv_sem=recv_sem):
+                copy = pltpu.make_async_remote_copy(
+                    src_ref=src,
+                    dst_ref=dst,
+                    send_sem=send_sem.at[k],
+                    recv_sem=recv_sem.at[k],
+                    device_id=peer,
+                    device_id_type=pl.DeviceIdType.MESH,
+                )
+                copy.start()
+                return copy
+
+            def keep(src, dst, own_sem=own_sem):
+                copy = pltpu.make_async_copy(src, dst, own_sem)
+                copy.start()
+                return copy
+
+            running.append(job.steps(spot, send, keep, x, out, *scratch))
+        while running:
+            for steps in list(running):
+                if next(steps, "end") == "end":
+                    running.remove(steps)
+
+    scratch = []
+    for job in jobs:
+        scratch += list(job.scratch)
+        scratch += [
+            pltpu.SemaphoreType.DMA((job.sems,)),
+            pltpu.SemaphoreType.DMA((job.sems,)),
+            pltpu.SemaphoreType.DMA,
+        ]
+    return pl.pallas_call(
+        kernel,
+        out_shape=[job.out for job in jobs],
+        in_specs=[pl.BlockSpec(memory_space=pltpu.VMEM)] * len(jobs),
+        out_specs=[pl.BlockSpec(memory_space=pltpu.VMEM)] * len(jobs),
+        scratch_shapes=scratch,
+        compiler_params=pltpu.CompilerParams(
+            collective_id=cid, has_side_effects=True, vmem_limit_bytes=60 * 1024 * 1024
+        ),
+        name=name,
+    )(*[job.x for job in jobs])
+
+
+def plane_peers(spot):
+    return [spot.plane(1), spot.plane(2), spot.plane(4)]
+
+
+def line_peers(spot):
+    return [spot.line(1), spot.line(-1)]
+
+
+def plane_gather(x):
+    half = x.shape[1] // 2
+    low, high = slice(0, half), slice(half, 2 * half)
+
+    def steps(spot, send, keep, x, out):
+        t = spot.t
+        mate, across, along = spot.plane(1), spot.plane(2), spot.plane(4)
+        own = keep(x, out.at[t])
+        c0 = send(x.at[:, low], out.at[t, :, low], 0, across)
+        c1 = send(x.at[:, high], out.at[t, :, high], 1, along)
+        c2 = send(x.at[:, high], out.at[t, :, high], 2, across)
+        c3 = send(x.at[:, low], out.at[t, :, low], 3, along)
+        c6 = send(x, out.at[t], 6, mate)
+        yield
+        c0.wait_recv()
+        view = out.at[t ^ 2, :, low]
+        c4 = send(view, view, 4, along)
+        passed = [send(view, view, 7, mate)]
+        yield
+        c1.wait_recv()
+        view = out.at[t ^ 4, :, high]
+        c5 = send(view, view, 5, across)
+        passed.append(send(view, view, 8, mate))
+        yield
+        late = [(c2, 2, high), (c3, 4, low), (c4, 6, low), (c5, 6, high)]
+        for k, (copy, who, part) in enumerate(late):
+            copy.wait_recv()
+            view = out.at[t ^ who, :, part]
+            passed.append(send(view, view, 9 + k, mate))
+            yield
+        for copy in [c6] + passed:
+            copy.wait_recv()
+        for copy in [c0, c1, c2, c3, c4, c5, c6] + passed:
+            copy.wait_send()
+        own.wait()
+
+    out = jax.ShapeDtypeStruct((TP,) + x.shape, x.dtype)
+    return Job(x, out, [], 13, plane_peers, steps, lambda *_: lax.all_gather(x, "tp"))
+
+
+def plane_scatter(x):
+    _, rows, width = x.shape
+    half = width // 2
+    low, high = slice(0, half), slice(half, width)
+
+    def steps(spot, send, keep, x, out, mates, sums, near, far):
+        t = spot.t
+        mate, across, along = spot.plane(1), spot.plane(2), spot.plane(4)
+        copies = [send(x.at[t ^ 1 ^ (2 * e)], mates.at[e], e, mate) for e in (3, 1, 2, 0)]
+        c3, c1, c2, c0 = copies
+
+        def both(e, part):
+            return x[t ^ (2 * e), :, part].astype(F32) + mates[e, :, part].astype(F32)
+
+        def ship(k, value, dst, peer):
+            sums[k] = value.astype(BF)
+            copy = send(sums.at[k], dst, 4 + k, peer)
+            copies.append(copy)
+            return copy
+
+        yield
+        c3.wait_recv()
+        q0 = ship(0, both(3, low), near.at[0], across)
+        q1 = ship(1, both(3, high), near.at[1], along)
+        yield
+        c1.wait_recv()
+        p0 = ship(2, both(1, low), near.at[2], across)
+        c2.wait_recv()
+        p1 = ship(3, both(2, high), near.at[3], along)
+        yield
+        q0.wait_recv()
+        r0 = ship(4, both(2, low) + near[0].astype(F32), far.at[0], along)
+        q1.wait_recv()
+        r1 = ship(5, both(1, high) + near[1].astype(F32), far.at[1], across)
+        yield
+        c0.wait_recv()
+        p0.wait_recv()
+        r0.wait_recv()
+        out[:, low] = both(0, low) + near[2].astype(F32) + far[0].astype(F32)
+        p1.wait_recv()
+        r1.wait_recv()
+        out[:, high] = both(0, high) + near[3].astype(F32) + far[1].astype(F32)
+        for copy in copies:
+            copy.wait_send()
+
+    scratch = [
+        pltpu.VMEM((4, rows, width), BF),
+        pltpu.VMEM((6, rows, half), BF),
+        pltpu.VMEM((4, rows, half), BF),
+        pltpu.VMEM((2, rows, half), BF),
+    ]
+    out = jax.ShapeDtypeStruct((rows, width), F32)
+
+    def plain(*_):
+        return lax.psum_scatter(x, "tp", scatter_dimension=0).astype(F32)
+
+    return Job(x, out, scratch, 10, plane_peers, steps, plain)
+
+
+def plane_swap(x):
+    def steps(spot, send, keep, x, out):
+        t = spot.t
+        own = keep(x.at[t], out.at[t])
+        copies = [send(x.at[t ^ k], out.at[t], k, spot.plane(k)) for k in (6, 7, 2, 4, 3, 5, 1)]
+        yield
+        yield
+        yield
+        for copy in copies:
+            copy.wait()
+        own.wait()
+
+    out = jax.ShapeDtypeStruct(x.shape, x.dtype)
+
+    def plain(*_):
+        return lax.all_to_all(x, "tp", 0, 0, tiled=True)
+
+    return Job(
+        x, out, [], TP, lambda spot: [spot.plane(k) for k in range(1, TP)], steps, plain
+    )
+
+
+def halves(shape):
+    if shape[0] > 1:
+        cut = shape[0] // 2
+        return [(slice(0, cut), slice(None)), (slice(cut, 2 * cut), slice(None))]
+    cut = shape[2] // 2
+    return [(slice(None), slice(0, cut)), (slice(None), slice(cut, 2 * cut))]
+
+
+def line_gather(x, axes=SEQ):
+    first, second = halves(x.shape)
+
+    def steps(spot, send, keep, x, out):
+        n = spot.n_head
+        own = keep(x, out.at[:, spot.h])
+        copies = []
+        for s in range(n - 1):
+            pair = []
+            for k, ((lead, cols), way) in enumerate(((first, 1), (second, -1))):
+                slot = lax.rem(spot.h - way * s + n, n)
+                dst = out.at[lead, slot, :, cols]
+                src = x.at[lead, :, cols] if s == 0 else dst
+                pair.append(send(src, dst, 2 * s + k, spot.line(way)))
+            copies += pair
+            yield
+            for copy in pair:
+                copy.wait_recv()
+        for copy in copies:
+            copy.wait_send()
+        own.wait()
+
+    t, r, w = x.shape
+
+    def plain(n_grp, n_head):
+        every = lax.all_gather(x, axes).reshape(-1, n_head, t, r, w)
+        return every.transpose(0, 2, 1, 3, 4).reshape(-1, n_head, r, w)
+
+    out = jax.ShapeDtypeStruct((t, 4, r, w), x.dtype)
+    return Job(x, out, [], 6, line_peers, steps, plain)
+
+
+def line_scatter(x, kind, axes=SEQ):
+    t, n, r, w = x.shape
+    first, second = halves((t, r, w))
+    part = (t // 2, r, w) if t > 1 else (t, r, w // 2)
+
+    def steps(spot, send, keep, x, out, sums, got):
+        h = spot.h
+        right, left, far = (lax.rem(h + k, 4) for k in (1, 3, 2))
+
+        def at(slot, piece):
+            return x.at[piece[0], slot, :, piece[1]]
+
+        def value(slot, piece):
+            return x[piece[0], slot, :, piece[1]].astype(F32)
+
+        c0 = send(at(far, first), got.at[0], 0, spot.line(1))
+        c1 = send(at(far, second), got.at[1], 1, spot.line(-1))
+        c2 = send(at(right, second), got.at[2], 2, spot.line(1))
+        c3 = send(at(left, first), got.at[3], 3, spot.line(-1))
+        yield
+        c0.wait_recv()
+        sums[0] = (value(right, first) + got[0].astype(F32)).astype(BF)
+        c4 = send(sums.at[0], got.at[4], 4, spot.line(1))
+        c1.wait_recv()
+        sums[1] = (value(left, second) + got[1].astype(F32)).astype(BF)
+        c5 = send(sums.at[1], got.at[5], 5, spot.line(-1))
+        yield
+        yield
+        c3.wait_recv()
+        c4.wait_recv()
+        total = value(h, first) + got[3].astype(F32) + got[4].astype(F32)
+        out[first[0], :, first[1]] = total.astype(kind)
+        c2.wait_recv()
+        c5.wait_recv()
+        total = value(h, second) + got[2].astype(F32) + got[5].astype(F32)
+        out[second[0], :, second[1]] = total.astype(kind)
+        for copy in (c0, c1, c2, c3, c4, c5):
+            copy.wait_send()
+
+    def plain(n_grp, n_head):
+        ordered = x.reshape(-1, t if axes == "head" else t // n_grp, n_head, r, w)
+        ordered = ordered.transpose(0, 2, 1, 3, 4).reshape((-1,) + (ordered.shape[1], r, w))
+        return lax.psum_scatter(ordered, axes, scatter_dimension=0, tiled=True)[0].astype(kind)
+
+    out = jax.ShapeDtypeStruct((t, r, w), kind)
+    scratch = [pltpu.VMEM((2,) + part, BF), pltpu.VMEM((6,) + part, BF)]
+    return Job(x, out, scratch, 6, line_peers, steps, plain)
+
+
+def small_peers(spot):
+    return [spot.plane(k) for k in range(1, TP)] + [spot.line(k) for k in range(1, spot.n_head)]
+
+
+def small_gather(x):
+    def steps(spot, send, keep, x, out):
+        out[spot.t, spot.h] = x[...]
+        mine = out.at[spot.t, spot.h]
+        copies = [send(x, mine, k - 1, spot.plane(k)) for k in range(1, TP)]
+        for copy in copies:
+            copy.wait_recv()
+        block = out.at[:, spot.h]
+        later = [send(block, block, 6 + k, spot.line(k)) for k in range(1, spot.n_head)]
+        yield
+        for copy in later:
+            copy.wait_recv()
+        for copy in copies + later:
+            copy.wait_send()
+
+    def plain(*_):
+        return lax.all_gather(x, ALL)
+
+    out = jax.ShapeDtypeStruct((TP, 4) + x.shape, x.dtype)
+    return Job(x, out, [], TP + 2, small_peers, steps, plain)
+
+
+def small_scatter(x):
+    def steps(spot, send, keep, x, out, got, sums, last):
+        t, h = spot.t, spot.h
+        copies = [send(x.at[t ^ k], got.at[k], k - 1, spot.plane(k)) for k in range(1, TP)]
+        for copy in copies:
+            copy.wait_recv()
+        total = x[t]
+        for k in range(1, TP):
+            total = total + got[k]
+        sums[...] = total
+        later = [
+            send(sums.at[lax.rem(h + k, 4)], last.at[k], 6 + k, spot.line(k)) for k in range(1, 4)
+        ]
+        yield
+        for copy in later:
+            copy.wait_recv()
+        out[...] = sums[h] + last[1] + last[2] + last[3]
+        for copy in copies + later:
+            copy.wait_send()
+
+    def plain(*_):
+        return lax.psum_scatter(x.reshape((-1,) + x.shape[2:]), ALL, scatter_dimension=0)
+
+    out = jax.ShapeDtypeStruct(x.shape[2:], x.dtype)
+    scratch = [
+        pltpu.VMEM(x.shape, F32),
+        pltpu.VMEM(x.shape[1:], F32),
+        pltpu.VMEM(x.shape[1:], F32),
+    ]
+    return Job(x, out, scratch, TP + 2, small_peers, steps, plain)
+
+
+def chunk_shift(x, way):
+    def steps(spot, send, keep, x, out):
+        copy = send(x, out, 0, spot.chunk(way))
+        yield
+        yield
+        copy.wait()
+
+    def plain(n_grp, n_head):
+        count = n_grp * TP * n_head
+        return lax.ppermute(x, ALL, [(f, (f + way) % count) for f in range(count)])
+
+    out = jax.ShapeDtypeStruct(x.shape, x.dtype)
+    return Job(x, out, [], 1, lambda spot: [spot.chunk(1), spot.chunk(-1)], steps, plain)
 
 
 def norm_parts(values, gain):
@@ -508,36 +889,43 @@
         axis=2,
     )
 
-    def gather_cols(piece):
-        mine = lax.all_to_all(piece, "tp", 0, 0, tiled=True)
-        every = lax.all_gather(mine, SEQ)
-        every = every.reshape(n_grp, n_head, TP, r, -1).transpose(0, 2, 1, 3, 4)
-        return every.reshape(n_dev * r, -1)
-
-    w_in = gather_cols(packed[:, :, :COLS])
-    w_gu = gather_cols(packed[:, :, COLS:])
-    if n_grp == 1:
-        w_out_attn = lax.all_gather(w_attn_out, SEQ, tiled=True)
-        w_out_mamba = lax.all_gather(w_mamba_out, SEQ, tiled=True)
-    else:
-        w_out_attn = lax.dynamic_slice_in_dim(
-            lax.all_gather(w_attn_out, ALL, tiled=True), t * HDIM, HDIM, 0
-        )
-        w_out_mamba = lax.dynamic_slice_in_dim(
-            lax.all_gather(w_mamba_out, ALL, tiled=True), t * MW, MW, 0
-        )
-    w_out = jnp.concatenate([w_out_attn, w_out_mamba], axis=0)
-    w_dn = lax.all_gather(w_down, SEQ, tiled=True)
-    gain_mix = lax.all_gather(g_mix, ALL, tiled=True).astype(F32)[None]
-    gain_ffn = lax.all_gather(g_ffn, ALL, tiled=True).astype(F32)[None]
-    conv_all = lax.all_gather(jnp.concatenate([conv_w, conv_b[None]], axis=0), ALL)
-    conv_all = conv_all.transpose(1, 0, 2).reshape(CONVW + 1, -1).astype(F32)
+    run = functools.partial(communicate, n_grp=n_grp, n_head=n_head)
+    lanes = 128
+    per_head = MHEADS // n_head
+
+    def in_lanes(v):
+        return jnp.pad(v, ((0, 0),) * (v.ndim - 1) + ((0, lanes - v.shape[-1]),))
+
+    heads = jnp.stack([dt_bias, a_log, d_skip]).reshape(1, -1)
+    packet = jnp.concatenate(
+        [
+            in_lanes(jnp.stack([g_mix, g_ffn]).astype(F32)),
+            in_lanes(jnp.concatenate([conv_w, conv_b[None]], axis=0).astype(F32)),
+            in_lanes(heads),
+        ],
+        axis=0,
+    )
+    smalls, rim, w_in_mine = run(
+        "open",
+        1,
+        jobs=[
+            small_gather(packet),
+            chunk_shift(tokens[rows - RIM :], 1),
+            plane_swap(packed[:, :, :COLS]),
+        ],
+    )
+    smalls = smalls.reshape(n_dev, 8, lanes)
+    gain_mix = smalls[:, 0, : width // n_dev].reshape(1, width)
+    gain_ffn = smalls[:, 1, : width // n_dev].reshape(1, width)
+    conv_cols = conv_w.shape[1]
+    conv_all = smalls[:, 2 : 3 + CONVW, :conv_cols].transpose(1, 0, 2).reshape(CONVW + 1, -1)
     conv_mine = jnp.concatenate(
         [conv_all[:, m_total:], lax.dynamic_slice_in_dim(conv_all, t * MW, MW, 1)], axis=1
     )
     taps = jnp.concatenate([conv_mine[:CONVW], jnp.zeros((8 - CONVW, CH), F32)], axis=0)
     bias = conv_mine[CONVW:]
-    heads3 = lax.all_gather(jnp.stack([dt_bias, a_log, d_skip]), "head", axis=1, tiled=True)
+    heads3 = smalls[:n_head, 7, : 3 * per_head].reshape(n_head, 3, per_head)
+    heads3 = heads3.transpose(1, 0, 2).reshape(3, MHEADS)
     heads3 = lax.dynamic_slice_in_dim(heads3, t * MH, MH, 1)
     heads3 = jnp.pad(heads3, ((0, 0), (0, STATE - MH)))
     dtb, alog, dsk = heads3[0:1], heads3[1:2], heads3[2:3]
@@ -549,15 +937,23 @@
     doc_start = jnp.max(jnp.where(starts[None, None] <= pos[:, :, None], starts[None, None], 0), axis=2)
     mine = jnp.full((TP,), g * n_head + h, jnp.int32)
     n_win = n_head if n_grp == 1 else 2 * n_head
-    base = jnp.full((TP,), (g + 1) * n_head - n_win, jnp.int32)
+    base = jnp.full((TP,), ((g + 1) * n_head - n_win) * TP, jnp.int32)
     sc = jnp.stack([firsts, doc_start[:, -1], doc_start[:, 0] // SPAN, mine, base]).astype(jnp.int32)
     ds = doc_start[:, :, None].astype(jnp.int32)
 
-    rim = lax.ppermute(tokens[rows - RIM :], ALL, [(f, f + 1) for f in range(n_dev - 1)])
-    ext_tokens = lax.all_gather(jnp.concatenate([rim, tokens], axis=0), "tp", tiled=True)
-    cot_all = lax.all_gather(cotangent, "tp", tiled=True)
-
-    normed = norm_parts(ext_tokens.astype(F32), gain_mix)[0].astype(BF)
+    ext = jnp.concatenate([rim, tokens], axis=0).astype(F32)
+    normed_mine, inv_ext = norm_parts(ext, gain_mix)
+    normed, w_in, w_gu_mine = run(
+        "inputs",
+        2,
+        jobs=[
+            plane_gather(normed_mine.astype(BF)),
+            line_gather(w_in_mine),
+            plane_swap(packed[:, :, COLS:]),
+        ],
+    )
+    normed = normed.reshape(TP * (RIM + SPAN), width)
+    w_in = w_in.reshape(width, COLS)
     pay = dot(normed, w_in).astype(BF).reshape(TP, RIM + SPAN, COLS)
 
     f_u, f_c, f_y, f_ds = (1, SPAN, CH), (1, SPAN, STATE), (1, SPAN, MW), (1, SPAN, 1)
@@ -586,15 +982,29 @@
         [],
         "mixer_local",
     )
-    kv = lax.all_gather(pay[:, RIM:, COL_KV:], "head")
+    moves = [
+        line_gather(pay[:, RIM:, COL_KV:], "head"),
+        line_gather(slab),
+        plane_gather(cotangent),
+    ]
+    if n_grp == 1:
+        moves += [line_gather(w_attn_out[None]), line_gather(w_mamba_out[None])]
+    kv, slabs, cot_all, *w_outs = run("states", 3, jobs=moves)
+    kv = kv.reshape(TP * n_head, SPAN, 128)
     if n_grp > 1:
         before = lax.ppermute(kv, "grp", [(a, a + 1) for a in range(n_grp - 1)])
         kv = jnp.concatenate([before, kv], axis=0)
-    slabs = lax.all_gather(slab, SEQ)
+        w_outs = [
+            lax.dynamic_slice_in_dim(lax.all_gather(w, ALL, tiled=True), t * size, size, 0)
+            for w, size in ((w_attn_out, HDIM), (w_mamba_out, MW))
+        ]
+    w_out = jnp.concatenate([w.reshape(-1, width) for w in w_outs], axis=0)
+    slabs = slabs.reshape(n_seq * TP, SLAB, STATE)
+    cot_all = cot_all.reshape(TP * SPAN, width)
 
     s_q = block((1, RIM + SPAN, 128), "i", 0, 3)
     s_o = block((1, SPAN, 128), "i", 0, 0)
-    s_kv = whole((n_win, TP, SPAN, 128))
+    s_kv = whole((n_win * TP, SPAN, 128))
     o, lse = call(
         functools.partial(attend, n_head),
         sc,
@@ -605,7 +1015,7 @@
         [],
         "attend",
     )
-    s_slabs = whole((n_seq, TP, SLAB, STATE))
+    s_slabs = whole((n_seq * TP, SLAB, STATE))
     s_state = block((1, MW, STATE), "i", 0, 0)
     branch, y_all, state_in = call(
         functools.partial(mixer_finish, n_head),
@@ -619,17 +1029,29 @@
     )
     branch = branch.reshape(TP * SPAN, 256)
 
-    def to_tokens(partial):
-        return lax.psum_scatter(partial.astype(BF), "tp", tiled=True).astype(F32)
-
-    mixed = tokens.astype(F32) + to_tokens(dot(branch, w_out))
+    def by_token(partial):
+        return plane_scatter(partial.astype(BF).reshape(TP, -1, width))
+
+    mixed, w_gu, w_dn = run(
+        "middle",
+        4,
+        jobs=[
+            by_token(dot(branch, w_out)),
+            line_gather(w_gu_mine),
+            line_gather(w_down[None]),
+        ],
+    )
+    w_gu = w_gu.reshape(width, 2 * ff_part)
+    w_dn = w_dn.reshape(ff_part, width)
+    mixed = tokens.astype(F32) + mixed
     ffn_local, inv_ffn = norm_parts(mixed, gain_ffn)
-    ffn_in = lax.all_gather(ffn_local.astype(BF), "tp", tiled=True)
+    (ffn_in,) = run("ffn", 5, jobs=[plane_gather(ffn_local.astype(BF))])
+    ffn_in = ffn_in.reshape(TP * SPAN, width)
     gate = dot(ffn_in, w_gu[:, :ff_part])
     up = dot(ffn_in, w_gu[:, ff_part:])
     sig = sigmoid(gate)
     hidden = (gate * sig * up).astype(BF)
-    result = (mixed + to_tokens(dot(hidden, w_dn))).astype(BF)
+    ffn_out = by_token(dot(hidden, w_dn))
 
     d_hidden = dot_rt(cot_all, w_dn)
     g_down = dot_lt(hidden, cot_all)
@@ -637,10 +1059,26 @@
     d_up = (d_hidden * gate * sig).astype(BF)
     d_gu = jnp.concatenate([d_gate, d_up], axis=1)
     g_gu = dot_lt(ffn_in, d_gu)
-    d_ffn = to_tokens(dot_rt(d_gu, w_gu))
+    d_ffn, grad_down = run(
+        "ffn_back",
+        6,
+        jobs=[
+            by_token(dot_rt(d_gu, w_gu)),
+            line_scatter(g_down.astype(BF).reshape(n_grp, n_head, -1, width), F32),
+        ],
+    )
+    grad_down = grad_down.reshape(-1, width)
     d_norm, grad_gain_ffn = norm_back(mixed, inv_ffn, gain_ffn, d_ffn)
     d_mixed = cotangent.astype(F32) + d_norm
-    d_branch = lax.all_gather(d_mixed.astype(BF), "tp", tiled=True)
+    d_branch, g_gu = run(
+        "branch_back",
+        7,
+        jobs=[
+            plane_gather(d_mixed.astype(BF)),
+            line_scatter(g_gu.astype(BF).reshape(n_grp * TP, n_head, r, -1), BF),
+        ],
+    )
+    d_branch = d_branch.reshape(TP * SPAN, width)
     g_out = dot_lt(branch, d_branch)
     dh = dot_rt(d_branch, w_out).astype(BF).reshape(TP, SPAN, 256)
     s_dh = block((1, SPAN, 256), "i", 0, 0)
@@ -654,26 +1092,38 @@
         [],
         "mixer_entry",
     )
-    d_entries = lax.all_gather(d_entry, SEQ)
     dq, dkv = call(
         functools.partial(attend_back, n_head),
         sc,
         (pay, ds, dh, o, lse, kv),
         [s_q, s_ds, block((1, SPAN, 128), "i", 0, 0), s_o, s_ds, s_kv],
-        [((TP, SPAN, 128), F32), ((n_win, TP, SPAN, 128), BF)],
+        [((TP, SPAN, 128), F32), ((n_win * TP, SPAN, 128), BF)],
         [s_o, s_kv],
-        [pltpu.VMEM((n_win, TP, SPAN, 128), F32)],
+        [pltpu.VMEM((n_win * TP, SPAN, 128), F32)],
         "attend_back",
     )
     if n_grp > 1:
-        back = lax.ppermute(dkv[:n_head], "grp", [(a + 1, a) for a in range(n_grp - 1)])
-        dkv = dkv[n_head:] + back
-    dkv = lax.psum_scatter(dkv, "head", scatter_dimension=0, tiled=True)[0]
+        back = lax.ppermute(dkv[: TP * n_head], "grp", [(a + 1, a) for a in range(n_grp - 1)])
+        dkv = dkv[TP * n_head :] + back
+    moves = [
+        line_scatter(dkv.reshape(TP, n_head, SPAN, 128), BF, "head"),
+        line_gather(d_entry),
+        ffn_out,
+        plane_swap(g_gu),
+    ]
+    if n_grp == 1:
+        moves += [
+            line_scatter(g_out[:HDIM].astype(BF).reshape(1, n_head, -1, width), F32),
+            line_scatter(g_out[HDIM:].astype(BF).reshape(1, n_head, -1, width), F32),
+        ]
+    dkv, d_entries, ffn_out, parts_gu, *g_outs = run("states_back", 8, jobs=moves)
+    d_entries = d_entries.reshape(n_seq * TP, MW, STATE)
+    result = (mixed + ffn_out).astype(BF)
     d_pay, d_taps, d_small = call(
         functools.partial(mixer_back, n_head),
         sc,
         (slabs, d_entries, dh, pay, ds, state_in, y_all, dq, dkv) + params,
-        [s_slabs, whole((n_seq, TP, MW, STATE)), s_dh, s_pay, s_ds, s_state]
+        [s_slabs, whole((n_seq * TP, MW, STATE)), s_dh, s_pay, s_ds, s_state]
         + [block(f_y, "i", 0, 0), s_o, s_o]
         + s_params,
         [((TP, RIM + SPAN, COLS), BF), ((8, CH), F32), ((8, STATE), F32)],
@@ -683,22 +1133,45 @@
     )
     d_pay = d_pay.reshape(TP * (RIM + SPAN), COLS)
     g_in = dot_lt(normed, d_pay)
-    d_norm_in = to_tokens(dot_rt(d_pay, w_in))
-    rim_back = lax.ppermute(d_norm_in[:RIM].astype(BF), ALL, [(f + 1, f) for f in range(n_dev - 1)])
+    d_norm_in, g_in = run(
+        "inputs_back",
+        9,
+        jobs=[
+            by_token(dot_rt(d_pay, w_in)),
+            line_scatter(g_in.astype(BF).reshape(n_grp * TP, n_head, r, COLS), BF),
+        ],
+    )
+    grad_gain_mix = jnp.sum(d_norm_in * ext * inv_ext, axis=0)
+
+    conv_grad = jnp.zeros((CONVW + 1, m_total + 2 * STATE), F32)
+    conv_grad = lax.dynamic_update_slice_in_dim(
+        conv_grad, d_taps[: CONVW + 1, 2 * STATE :], t * MW, 1
+    )
+    conv_grad = conv_grad.at[:, m_total:].set(d_taps[: CONVW + 1, : 2 * STATE])
+    small = jnp.zeros((3, MHEADS), F32)
+    small = lax.dynamic_update_slice_in_dim(small, d_small[:3, :MH], t * MH, 1)
+    small = small.reshape(3, n_head, per_head).transpose(1, 0, 2).reshape(1, n_head, 1, -1)
+    packets = jnp.concatenate(
+        [
+            in_lanes(jnp.stack([grad_gain_mix, grad_gain_ffn]).reshape(2, n_dev, -1).transpose(1, 0, 2)),
+            in_lanes(conv_grad.reshape(CONVW + 1, n_dev, -1).transpose(1, 0, 2)),
+            in_lanes(jnp.broadcast_to(small, (n_grp * TP, n_head, 1, 3 * per_head)).reshape(n_dev, 1, -1)),
+        ],
+        axis=1,
+    )
+    smalls, parts, rim_back = run(
+        "close",
+        10,
+        jobs=[
+            small_scatter(packets.reshape(n_grp * TP, n_head, 8, lanes)),
+            plane_swap(g_in),
+            chunk_shift(d_norm_in[:RIM].astype(BF), -1),
+        ],
+    )
     d_norm_in = d_norm_in[RIM:].at[rows - RIM :].add(rim_back.astype(F32))
-    tok = tokens.astype(F32)
-    inv_mix = norm_parts(tok, gain_mix)[1]
-    d_tok, grad_gain_mix = norm_back(tok, inv_mix, gain_mix, d_norm_in)
+    d_tok, _ = norm_back(ext[RIM:], inv_ext[RIM:], gain_mix, d_norm_in)
     grad_tokens = d_mixed + d_tok
-
-    def scatter_cols(grad):
-        ordered = grad.reshape(n_grp, TP, n_head, r, -1).transpose(0, 2, 1, 3, 4)
-        ordered = ordered.reshape(n_seq, TP, r, -1).astype(BF)
-        mine = lax.psum_scatter(ordered, SEQ, scatter_dimension=0, tiled=True)[0]
-        return lax.all_to_all(mine, "tp", 0, 0, tiled=True).astype(F32)
-
-    parts = scatter_cols(g_in)
-    parts_gu = scatter_cols(g_gu)
+    parts, parts_gu = parts.astype(F32), parts_gu.astype(F32)
 
     def join_tp(p):
         return p.transpose(1, 0, 2).reshape(r, -1)
@@ -728,10 +1201,8 @@
     )
     grad_gate = join_ff(parts_gu[:, :, :ff_part])
     grad_up = join_ff(parts_gu[:, :, ff_part:])
-    grad_down = lax.psum_scatter(g_down.astype(BF), SEQ, tiled=True).astype(F32)
     if n_grp == 1:
-        grad_ao = lax.psum_scatter(g_out[:HDIM].astype(BF), SEQ, tiled=True).astype(F32)
-        grad_mo = lax.psum_scatter(g_out[HDIM:].astype(BF), SEQ, tiled=True).astype(F32)
+        grad_ao, grad_mo = (v.reshape(-1, width) for v in g_outs)
     else:
         full = jnp.zeros((q_total, width), F32)
         full = lax.dynamic_update_slice_in_dim(full, g_out[:HDIM], t * HDIM, 0)
@@ -739,20 +1210,9 @@
         full = jnp.zeros((m_total, width), F32)
         full = lax.dynamic_update_slice_in_dim(full, g_out[HDIM:], t * MW, 0)
         grad_mo = lax.psum_scatter(full, ALL, tiled=True)
-    conv_grad = jnp.zeros((CONVW + 1, m_total + 2 * STATE), F32)
-    conv_grad = lax.dynamic_update_slice_in_dim(
-        conv_grad, d_taps[: CONVW + 1, 2 * STATE :], t * MW, 1
-    )
-    conv_grad = conv_grad.at[:, m_total:].set(d_taps[: CONVW + 1, : 2 * STATE])
-    conv_grad = lax.psum_scatter(conv_grad, ALL, scatter_dimension=1, tiled=True)
-    gains = lax.psum_scatter(
-        jnp.stack([grad_gain_mix, grad_gain_ffn]), ALL, scatter_dimension=1, tiled=True
-    )
-    small = jnp.zeros((3, MHEADS), F32)
-    small = lax.dynamic_update_slice_in_dim(small, d_small[:3, :MH], t * MH, 1)
-    small = lax.psum(small, ALL)
-    per_head = MHEADS // n_head
-    small = lax.dynamic_slice_in_dim(small, h * per_head, per_head, 1)
+    gains = smalls[:2, : width // n_dev]
+    conv_grad = smalls[2 : 3 + CONVW, :conv_cols]
+    small = smalls[7, : 3 * per_head].reshape(3, per_head)
     return (
         result,
         grad_tokens,

time: 1130 us -> 682 us (0.60)
  waiting for transfers between devices: 565 us -> 0 us
  Pallas kernels: 144 us -> 552 us
  blocking collectives: 247 us -> 0 us
  between operations: 15.3 us -> 1.69 us
  starting transfers between devices: 13.3 us -> 0 us
    pallas_call x0 -> x10, Pallas kernels: none -> 410 us  [communicate(): pl.pallas_call(kernel, out_shape=[job.out for job in jobs], in_specs=[pl....]
    reduce_scatter x8 -> x0, waiting for transfers between devices: 209 us -> none  [the longest x4 169 us: to_tokens(): return lax.psum_scatter(partial.astype(BF), 'tp', tiled=True).astype(F32)]
    unnamed x21 -> x0, waiting for transfers between devices: 198 us -> none
    all_gather x9 -> x0, waiting for transfers between devices: 145 us -> none  [the longest x1 36.7 us: per_device(): d_branch = lax.all_gather(d_mixed.astype(BF), 'tp', tiled=True)]
    all_gather x5 -> x0, blocking collectives: 136 us -> none  [the longest x1 70.3 us: per_device(): lax.all_gather(jnp.concatenate([conv_w, conv_b[None]], axis=0), ALL)]
    unnamed x2 -> x0, blocking collectives: 87.1 us -> none
    all_to_all x2 -> x0, blocking collectives: 24.1 us -> none  [gather_cols(): mine = lax.all_to_all(piece, 'tp', 0, 0, tiled=True)]
  transfers between devices with their start and end apart: 23 -> 0, of which waited for: 16 -> 0; matrix products, arithmetic and copies ran while one was open for 7% -> 0% of each run, Pallas kernels for 11% -> 0%
where the time goes in v2:
time: 682 us; the launch traced here: 673 us
  Pallas kernels  552 us (81%)
  matrix products  59.4 us (9%)
  local copies, waits for them, and re-layouts  40.4 us (6%)
  other arithmetic  18.7 us (3%)
    pallas_call x10, Pallas kernels, communicate(): pl.pallas_call(kernel, out_shape=[job.out for job in jobs], in_specs=[pl....  410 us
    pallas_call x6, Pallas kernels, call(): pl.pallas_call(kernel, out_shape=[jax.ShapeDtypeStruct(s, d) for s, d in...  142 us
    dot_general x5, matrix products, dot(): return jnp.dot(a, b, preferred_element_type=F32)  22.9 us
    dot_general x4, matrix products, dot_lt(): lax.dot_general(a, b, (((0,), (0,)), ((), ())), preferred_element_type=F32)  18.3 us
    dot_general x4, matrix products, dot_rt(): lax.dot_general(a, b, (((1,), (1,)), ((), ())), preferred_element_type=F32)  18.3 us

profile of v2, /device:TPU:0, one launch (start us, length us, event | category | flops | bytes accessed | tf_op | source)
XLA Modules:
  0.0 672.6 jit_solution(5422814225416565863)
XLA Ops:
  7.5 18.0 %open.1 = (f32[8,4,8,128]{3,2,1,0:T(8,128)}, bf16[8,1024]{1,0:T(8,128)(2,1)}, bf16[8,32,896]{2,1,0:T(8,128)(2,1)}) custom-call(f32[8,128]{1,0:T(8,128)} %select_maximum_fusion.2.refs_0_, bf16[8,1024]{1,0:T(8,128)(2,1)} %slice.206.refs_1_, bf16[8,32,896]{2,1,0:T(8,128)(2,1)} %concatenate.44.refs_2_), custom_call_target="tpu_custom_call" | custom-call | tf_op jit(solution)/shard_map/open/pallas_call | solution.py:516
  30.1 42.2 %inputs.1 = (bf16[8,264,1024]{2,1,0:T(8,128)(2,1)}, bf16[8,4,32,896]{3,2,1,0:T(8,128)(2,1)}, bf16[8,32,512]{2,1,0:T(8,128)(2,1)}) custom-call(bf16[264,1024]{1,0:T(8,128)(2,1)} %multiply_convert_fusion.3.refs_0_, bf16[8,32,896]{2,1,0:T(8,128)(2,1)} %get-tuple-element.85.refs_1_, bf16[8,32,512]{2,1,0:T(8,128)(2,1)} %pad_maximum_fusion.8.refs_2_), custom_call_target="tpu_custom_call" | custom-call | tf_op jit(solution)/shard_map/inputs/pallas_call | solution.py:516
  72.3 9.3 %convolution_convert_fusion.1 = bf16[2112,896]{1,0:T(8,128)(2,1)} fusion(bf16[2112,1024]{1,0:T(8,128)(2,1)} %bitcast.246, bf16[1024,896]{1,0:T(8,128)(2,1)} %bitcast.251), kind=kOutput, calls=%fused_computation.1 | convolution fusion | flops 3877429248 | bytes 9945088 | tf_op jit(solution)/shard_map/dot_general | solution.py:42
  86.4 20.4 %mixer_local.1 = (f32[8,256,448]{2,1,0:T(8,128)}, f32[8,256,128]{2,1,0:T(8,128)}, f32[8,256,192]{2,1,0:T(8,128)}, bf16[8,200,128]{2,1,0:T(8,128)(2,1)}) custom-call(s32[5,8]{1,0:T(8,128)} %stack.35.sc, bf16[8,264,896]{2,1,0:T(8,128)(2,1)} %bitcast.169, s32[8,256,1]{2,1,0:T(8,128)} %copy.138.ds, f32[8,448]{1,0:T(8,128)} %concatenate.48.taps, ...), custom_call_target="tpu_custom_call" | custom-call | tf_op jit(solution)/shard_map/mixer_local/pallas_call | solution.py:421
  106.7 1.9 slice.257.refs_0_
  108.6 80.5 %states.1 = (bf16[8,4,256,128]{3,2,1,0:T(8,128)(2,1)}, bf16[8,4,200,128]{3,2,1,0:T(8,128)(2,1)}, bf16[8,256,1024]{2,1,0:T(8,128)(2,1)}, bf16[1,4,16,1024]{3,2,1,0:T(8,128)(2,1)}, bf16[1,4,48,1024]{3,2,1,0:T(8,128)(2,1)}) custom-call(bf16[8,256,128]{2,1,0:T(8,128)(2,1)} %slice.257.refs_0_, bf16[8,200,128]{2,1,0:T(8,128)(2,1)} %get-tuple-element.88.refs_1_, ...), custom_call_target="tpu_custom_call" | custom-call | tf_op jit(solution)/shard_map/states/pallas_call | solution.py:516
  189.1 24.7 %attend.1 = (f32[8,256,128]{2,1,0:T(8,128)}, f32[8,256,1]{2,1,0:T(8,128)}) custom-call(s32[5,8]{1,0:T(8,128)} %stack.35.sc, bf16[8,264,896]{2,1,0:T(8,128)(2,1)} %bitcast.171, s32[8,256,1]{2,1,0:T(8,128)} %copy.138.ds, bf16[32,256,128]{2,1,0:T(8,128)(2,1)} %bitcast.181), custom_call_target="tpu_custom_call" | custom-call | tf_op jit(solution)/shard_map/attend/pallas_call | solution.py:421
  213.9 11.9 %mixer_finish.1 = (bf16[8,256,256]{2,1,0:T(8,128)(2,1)}, f32[8,256,192]{2,1,0:T(8,128)}, f32[8,192,128]{2,1,0:T(8,128)}) custom-call(s32[5,8]{1,0:T(8,128)} %stack.35.sc, bf16[32,200,128]{2,1,0:T(8,128)(2,1)} %bitcast.183, f32[8,256,448]{2,1,0:T(8,128)} %get-tuple-element.90.u, f32[8,256,128]{2,1,0:T(8,128)} %get-tuple-element.91.cum, ...), custom_call_target="tpu_custom_call" | custom-call | tf_op jit(solution)/shard_map/mixer_finish/pallas_call | solution.py:421
  225.7 4.4 convolution_convert_fusion.4
  230.1 43.2 %middle.1 = (f32[256,1024]{1,0:T(8,128)}, bf16[8,4,32,512]{3,2,1,0:T(8,128)(2,1)}, bf16[1,4,64,1024]{3,2,1,0:T(8,128)(2,1)}) custom-call(bf16[8,256,1024]{2,1,0:T(8,128)(2,1)} %bitcast.177, bf16[8,32,512]{2,1,0:T(8,128)(2,1)} %get-tuple-element.98.refs_1_, bf16[1,64,1024]{2,1,0:T(8,128)(2,1)} %bitcast.222), custom_call_target="tpu_custom_call" | custom-call | tf_op jit(solution)/shard_map/middle/pallas_call | solution.py:516
  273.4 5.0 fusion.23
  279.7 24.5 %ffn.1 = bf16[8,256,1024]{2,1,0:T(8,128)(2,1)} custom-call(bf16[256,1024]{1,0:T(8,128)(2,1)} %multiply_convert_fusion.4.refs_0_), custom_call_target="tpu_custom_call" | custom-call | tf_op jit(solution)/shard_map/ffn/pallas_call | solution.py:516
  304.2 3.6 fusion.1
  308.3 2.2 multiply_convert_fusion
  310.6 3.3 convolution_convert_fusion.6
  313.9 2.1 convolution_convert_fusion.7
  316.0 4.4 convolution_convert_fusion.3
  320.4 27.6 %ffn_back.1 = (f32[256,1024]{1,0:T(8,128)}, f32[1,64,1024]{2,1,0:T(8,128)}) custom-call(bf16[8,256,1024]{2,1,0:T(8,128)(2,1)} %bitcast.189, bf16[1,4,64,1024]{3,2,1,0:T(8,128)(2,1)} %bitcast.201), custom_call_target="tpu_custom_call" | custom-call | tf_op jit(solution)/shard_map/ffn_back/pallas_call | solution.py:516
  350.8 25.7 %branch_back.1 = (bf16[8,256,1024]{2,1,0:T(8,128)(2,1)}, bf16[8,32,512]{2,1,0:T(8,128)(2,1)}) custom-call(bf16[256,1024]{1,0:T(8,128)(2,1)} %get-tuple-element.134.refs_0_, bf16[8,4,32,512]{3,2,1,0:T(8,128)(2,1)} %bitcast.195), custom_call_target="tpu_custom_call" | custom-call | tf_op jit(solution)/shard_map/branch_back/pallas_call | solution.py:516
  376.5 3.8 fusion
  381.8 3.3 convolution_convert_fusion.2
  385.1 2.3 convolution_convert_fusion.5
  387.4 10.4 %mixer_entry.1.refs_1_ = bf16[8,192,128]{2,1,0:T(8,128)(2,1)} custom-call(s32[5,8]{1,0:T(8,128)} %stack.35.sc, bf16[8,256,256]{2,1,0:T(8,128)(2,1)} %bitcast.178, f32[8,256,448]{2,1,0:T(8,128)} %get-tuple-element.90.u, f32[8,256,128]{2,1,0:T(8,128)} %get-tuple-element.91.cum, bf16[8,264,896]{2,1,0:T(8,128)(2,1)} %bitcast.173, s32[8,256,1]{2,1,0:T(8,128)} %copy.138.ds), custom_call_target="tpu_custom_call" | custom-call | tf_op jit(solution)/shard_map/mixer_entry/pallas_call | solution.py:421
  397.9 30.6 %attend_back.1 = (f32[8,256,128]{2,1,0:T(8,128)}, bf16[32,256,128]{2,1,0:T(8,128)(2,1)}) custom-call(s32[5,8]{1,0:T(8,128)} %stack.35.sc, bf16[8,264,896]{2,1,0:T(8,128)(2,1)} %bitcast.174, s32[8,256,1]{2,1,0:T(8,128)} %copy.138.ds, bf16[8,256,256]{2,1,0:T(8,128)(2,1)} %bitcast.179, f32[8,256,128]{2,1,0:T(8,128)} %get-tuple-element.94.o, ...), custom_call_target="tpu_custom_call" | custom-call | tf_op jit(solution)/shard_map/attend_back/pallas_call | solution.py:421
  428.4 94.1 %states_back.1 = (bf16[8,256,128]{2,1,0:T(8,128)(2,1)}, bf16[8,4,192,128]{3,2,1,0:T(8,128)(2,1)}, f32[256,1024]{1,0:T(8,128)}, bf16[8,32,512]{2,1,0:T(8,128)(2,1...) custom-call(bf16[8,4,256,128]{3,2,1,0:T(8,128)(2,1)} %bitcast.191, bf16[8,192,128]{2,1,0:T(8,128)(2,1)} %mixer_entry.1.refs_1_, ...), custom_call_target="tpu_custom_call" | custom-call | tf_op jit(solution)/shard_map/states_back/pallas_call | solution.py:516
  522.5 44.1 %mixer_back.1 = (bf16[8,264,896]{2,1,0:T(8,128)(2,1)}, f32[8,448]{1,0:T(8,128)}, f32[8,128]{1,0:T(8,128)}) custom-call(s32[5,8]{1,0:T(8,128)} %stack.35.sc, bf16[32,200,128]{2,1,0:T(8,128)(2,1)} %bitcast.184, bf16[32,192,128]{2,1,0:T(8,128)(2,1)} %bitcast.194, bf16[8,256,256]{2,1,0:T(8,128)(2,1)} %bitcast.180, bf16[8,264,896]{2,1,0:T(8,128)(2,1)} %bitcast.175, ...), custom_call_target="tpu_custom_call" | custom-call | tf_op jit(solution)/shard_map/mixer_back/pallas_call | solution.py:421
  566.6 9.0 %bitcast_convert_fusion = bf16[1024,896]{1,0:T(8,128)(2,1)} fusion(bf16[8,264,1024]{2,1,0:T(8,128)(2,1)} %get-tuple-element.86, bf16[8,264,896]{2,1,0:T(8,128)(2,1)} %get-tuple-element.114), kind=kOutput, calls=%fused_computation.5 | convolution fusion | flops 3876454400 | bytes 9945088 | tf_op jit(solution)/shard_map/dot_general | solution.py:46
  575.6 6.5 convolution_convert_fusion
  582.1 37.4 %inputs_back.1 = (f32[264,1024]{1,0:T(8,128)}, bf16[8,32,896]{2,1,0:T(8,128)(2,1)}) custom-call(bf16[8,264,1024]{2,1,0:T(8,128)(2,1)} %bitcast.185, bf16[8,4,32,896]{3,2,1,0:T(8,128)(2,1)} %bitcast.192), custom_call_target="tpu_custom_call" | custom-call | tf_op jit(solution)/shard_map/inputs_back/pallas_call | solution.py:516
  624.1 17.2 %close.1 = (f32[8,128]{1,0:T(8,128)}, bf16[8,32,896]{2,1,0:T(8,128)(2,1)}, bf16[8,1024]{1,0:T(8,128)(2,1)}) custom-call(f32[8,4,8,128]{3,2,1,0:T(8,128)} %bitcast.202, bf16[8,32,896]{2,1,0:T(8,128)(2,1)} %get-tuple-element.118.refs_1_, bf16[8,1024]{1,0:T(8,128)(2,1)} %slice.316.refs_2_), custom_call_target="tpu_custom_call" | custom-call | tf_op jit(solution)/shard_map/close/pallas_call | solution.py:516
  645.7 1.8 copy.151
  654.4 1.8 pad_maximum_fusion.5
  (212 shorter events, 53.6 us)
Async XLA Ops:
  0.6 4.1 slice-start
  0.7 5.4 copy-start
  0.7 6.0 copy-start.33
  0.7 6.0 copy-start.27
  0.7 6.0 copy-start.30
  0.7 6.0 copy-start.29
  0.7 6.0 copy-start.28
  0.7 6.1 copy-start.32
  0.7 6.1 copy-start.31
  3.1 26.2 %copy-start.16 = (bf16[32,2048]{1,0:T(8,128)(2,1)S(1)}, bf16[32,2048]{1,0:T(8,128)(2,1)}, u32[]{:S(2)}) copy-start(bf16[32,2048]{1,0:T(8,128)(2,1)} %param.33) | copy-start | bytes 393220
  4.0 25.3 %copy-start.17 = (bf16[32,2048]{1,0:T(8,128)(2,1)S(1)}, bf16[32,2048]{1,0:T(8,128)(2,1)}, u32[]{:S(2)}) copy-start(bf16[32,2048]{1,0:T(8,128)(2,1)} %param.34) | copy-start | bytes 393220
  26.6 45.7 %copy-start.18 = (f32[1024]{0:T(1024)}, f32[1024]{0:T(1024)S(1)}, u32[]{:S(2)}) copy-start(f32[1024]{0:T(1024)S(1)} %mul.225) | copy-start | bytes 12292
  27.5 592.1 %copy-start.21 = (f32[264]{0:T(512)}, f32[264]{0:T(512)S(1)}, u32[]{:S(2)}) copy-start(f32[264]{0:T(512)S(1)} %add_rsqrt_fusion) | copy-start | bytes 3172
  72.3 9.3 %copy-start.13 = (f32[8,4,8,128]{3,2,1,0:T(8,128)S(1)}, f32[8,4,8,128]{3,2,1,0:T(8,128)}, u32[]{:S(2)}) copy-start(f32[8,4,8,128]{3,2,1,0:T(8,128)} %get-tuple-element.84) | copy-start | bytes 393220
  72.3 10.9 %copy-start.39 = (s32[4]{0:T(128)S(1)}, s32[4]{0:T(128)}, u32[]{:S(2)}) copy-start(s32[4]{0:T(128)} %param.36) | copy-start | bytes 52
  213.9 11.9 %copy-start.9 = (bf16[1,4,48,1024]{3,2,1,0:T(8,128)(2,1)S(1)}, bf16[1,4,48,1024]{3,2,1,0:T(8,128)(2,1)}, u32[]{:S(2)}) copy-start(bf16[1,4,48,1024]{3,2,1,0:T(8,128)(2,1)} %get-tuple-element.97) | copy-start | bytes 1179652
  213.9 11.9 %copy-start.15 = (bf16[1,4,16,1024]{3,2,1,0:T(8,128)(2,1)S(1)}, bf16[1,4,16,1024]{3,2,1,0:T(8,128)(2,1)}, u32[]{:S(2)}) copy-start(bf16[1,4,16,1024]{3,2,1,0:T(8,128)(2,1)} %get-tuple-element.96) | copy-start | bytes 393220
  273.4 5.1 copy-start.6
  279.7 24.5 %copy-start.38 = (bf16[8,4,32,512]{3,2,1,0:T(8,128)(2,1)S(1)}, bf16[8,4,32,512]{3,2,1,0:T(8,128)(2,1)}, u32[]{:S(2)}) copy-start(bf16[8,4,32,512]{3,2,1,0:T(8,128)(2,1)} %get-tuple-element.102) | copy-start | bytes 3145732
  304.2 3.7 copy-start.2
  304.2 4.1 copy-start.40
  376.5 5.3 copy-start.8
  566.6 9.0 %copy-start.36 = (bf16[8,264,896]{2,1,0:T(8,128)(2,1)S(1)}, bf16[8,264,896]{2,1,0:T(8,128)(2,1)}, u32[]{:S(2)}) copy-start(bf16[8,264,896]{2,1,0:T(8,128)(2,1)} %get-tuple-element.114) | copy-start | bytes 11354116
  566.6 9.0 %copy-start.37 = (bf16[8,4,32,896]{3,2,1,0:T(8,128)(2,1)S(1)}, bf16[8,4,32,896]{3,2,1,0:T(8,128)(2,1)}, u32[]{:S(2)}) copy-start(bf16[8,4,32,896]{3,2,1,0:T(8,128)(2,1)} %get-tuple-element.87) | copy-start | bytes 5505028
  582.1 37.4 %copy-start.10 = (bf16[8,1024]{1,0:T(8,128)(2,1)S(1)}, bf16[8,1024]{1,0:T(8,128)(2,1)}, u32[]{:S(2)}) copy-start(bf16[8,1024]{1,0:T(8,128)(2,1)} %get-tuple-element.83) | copy-start | bytes 49156
  582.1 39.0 %copy-start.24 = (f32[8,448]{1,0:T(8,128)S(1)}, f32[8,448]{1,0:T(8,128)}, u32[]{:S(2)}) copy-start(f32[8,448]{1,0:T(8,128)} %get-tuple-element.116) | copy-start | bytes 43012
  582.1 39.5 %copy-start.26 = (f32[8,128]{1,0:T(8,128)S(1)}, f32[8,128]{1,0:T(8,128)}, u32[]{:S(2)}) copy-start(f32[8,128]{1,0:T(8,128)} %get-tuple-element.117) | copy-start | bytes 12292
  659.3 3.8 copy-start.23
  659.3 4.7 copy-start.19
  664.3 3.5 copy-start.11
  665.6 3.8 copy-start.7
  667.9 3.7 copy-start.12
  (10 other events, 22.6 us)

commit v3 on v2

--- a/solution.py
+++ b/solution.py
@@ -159,10 +159,10 @@
             def _():
                 states[ic] = state
 
-            slab = slabs[c]
+            slab = slabs[sp, ic]
             return keep_wide(slab) * state + slab[:MW].astype(F32)
 
-        total = slabs.shape[0]
+        total = slabs.shape[0] * TP
         lax.fori_loop(0, total, one, jnp.zeros((MW, STATE), F32))
 
     first = sc[0, i]
@@ -214,17 +214,16 @@
 
     @pl.when(i == 0)
     def _():
-        total = slabs.shape[0]
+        total = slabs.shape[0] * TP
 
         def one(step, adj):
-            c = total - 1 - step
-            sp, ic = place_of(c, n_head)
+            sp, ic = place_of(total - 1 - step, n_head)
 
             @pl.when(sp == mine)
             def _():
                 carried[ic] = adj
 
-            return keep_wide(slabs[c]) * adj + d_entries[c].astype(F32)
+            return keep_wide(slabs[sp, ic]) * adj + d_entries[sp, ic].astype(F32)
 
         lax.fori_loop(0, total, one, jnp.zeros((MW, STATE), F32))
         dtap_out[...] = jnp.zeros_like(dtap_out)
@@ -330,9 +329,11 @@
     tap_rows.append(jnp.zeros((3, CH), F32))
     dtap_out[...] += jnp.concatenate(tap_rows, axis=0)
     dsmall_out[...] += jnp.concatenate([d_dtb, d_alog, d_dsk, jnp.zeros((5, STATE), F32)], axis=0)
-    own = jnp.concatenate(
-        [dq[0][:, HDIM:], dz, d_dtr[:, :64], dkv[0].astype(F32)], axis=1
-    )
+    d_keys = dkv[0].astype(F32)
+    if d_keys.shape[0] < SPAN:
+        d_keys = jnp.concatenate([d_keys] * QUAD, axis=0)
+        d_keys = jnp.where(iota((SPAN, 1), 0) // PART == sc[5, 0], d_keys, 0.0)
+    own = jnp.concatenate([dq[0][:, HDIM:], dz, d_dtr[:, :64], d_keys], axis=1)
     right = jnp.concatenate([jnp.zeros((RIM, COLS - CH), F32), own], axis=0)
     dpay_out[0] = jnp.concatenate([d_ext, right], axis=1).astype(BF)
 
@@ -404,6 +405,47 @@
     @pl.when(i == TP - 1)
     def _():
         dkv_out[...] = acc_kv[...].astype(BF)
+
+
+def assemble(n_grp, parts, parts_gu, qkv_out, in_out, gate_out, up_out):
+    every = [parts[k].astype(F32) for k in range(TP)]
+    per_kv = TP // KVHEADS
+
+    def columns(low, high):
+        return [p[:, low:high] for p in every]
+
+    def per_head(pieces):
+        return [
+            functools.reduce(lambda a, b: a + b, pieces[g * per_kv : (g + 1) * per_kv])
+            for g in range(KVHEADS)
+        ]
+
+    qkv_out[...] = jnp.concatenate(
+        columns(COL_Q, COL_Q + HDIM)
+        + per_head(columns(COL_KV + HDIM, COLS))
+        + per_head(columns(COL_KV, COL_KV + HDIM)),
+        axis=1,
+    )
+    shared = functools.reduce(lambda a, b: a + b, columns(0, 2 * STATE))
+    in_out[...] = jnp.concatenate(
+        columns(COL_Z, COL_Z + MW)
+        + columns(2 * STATE, CH)
+        + [shared]
+        + columns(COL_DT, COL_DT + MH),
+        axis=1,
+    )
+    every = [parts_gu[k].astype(F32) for k in range(TP)]
+    part = parts_gu.shape[2] // 2
+    step = part // n_grp
+    for base, out in ((0, gate_out), (part, up_out)):
+        out[...] = jnp.concatenate(
+            [
+                every[k][:, base + g * step : base + (g + 1) * step]
+                for g in range(n_grp)
+                for k in range(TP)
+            ],
+            axis=1,
+        )
 
 
 def block(shape, *index):
@@ -742,6 +784,147 @@
     out = jax.ShapeDtypeStruct((t, r, w), kind)
     scratch = [pltpu.VMEM((2,) + part, BF), pltpu.VMEM((6,) + part, BF)]
     return Job(x, out, scratch, 6, line_peers, steps, plain)
+
+
+def quad_peers(spot):
+    return line_peers(spot) + [spot.plane(1), spot.plane(2)]
+
+
+QUAD = 4
+PART = SPAN // QUAD
+
+
+def part_rows(r):
+    return pl.ds(pl.multiple_of(r * PART, PART), PART)
+
+
+def quad_gather(x):
+    first, second = halves(x.shape)
+
+    def steps(spot, send, keep, x, out):
+        n = spot.n_head
+        r = spot.t % QUAD
+        mine, other = part_rows(r), part_rows(r ^ 2)
+        own = keep(x, out.at[:, spot.h])
+        copies, crossed = [], []
+        index = 2 * (n - 1)
+        for s in range(n - 1):
+            pair = []
+            for k, ((lead, _), way) in enumerate(((first, 1), (second, -1))):
+                slot = lax.rem(spot.h - way * s + n, n)
+                dst = out.at[lead, slot, mine]
+                src = x.at[lead, mine] if s == 0 else dst
+                pair.append(send(src, dst, 2 * s + k, spot.line(way)))
+            copies += pair
+            yield
+            for k, ((lead, _), way) in enumerate(((first, 1), (second, -1))):
+                pair[k].wait_recv()
+                slot = lax.rem(spot.h - way * (s + 1) + n, n)
+                view = out.at[lead, slot, mine]
+                over = send(view, view, index, spot.plane(2))
+                near = send(view, view, index + 1, spot.plane(1))
+                crossed.append((over, near, lead, slot, index + 2))
+                copies += [over, near]
+                index += 3
+        yield
+        late = []
+        for over, near, lead, slot, k in crossed:
+            over.wait_recv()
+            view = out.at[lead, slot, other]
+            late.append(send(view, view, k, spot.plane(1)))
+        yield
+        for over, near, *_ in crossed:
+            near.wait_recv()
+        for copy in late:
+            copy.wait_recv()
+        for copy in copies + late:
+            copy.wait_send()
+        own.wait()
+
+    t, r, w = x.shape
+
+    def plain(n_grp, n_head):
+        return lax.all_gather(x, "head", axis=1)
+
+    out = jax.ShapeDtypeStruct((t, 4, r, w), x.dtype)
+    return Job(x, out, [], 24, quad_peers, steps, plain)
+
+
+def quad_scatter(x):
+    t, n, r, w = x.shape
+    half = t // 2
+    first, second = slice(0, half), slice(half, t)
+
+    def steps(spot, send, keep, x, out, mates, cross, gets, sums, got, turned):
+        h = spot.h
+        r = spot.t % QUAD
+        slots = [lax.rem(h + k, 4) for k in (2, 1, 3, 0)]
+        to_mate = []
+        for k, slot in enumerate(slots):
+            to_mate.append(
+                (
+                    send(x.at[:, slot, part_rows(r ^ 3)], mates.at[0, k], k, spot.plane(1)),
+                    send(x.at[:, slot, part_rows(r ^ 1)], mates.at[1, k], 4 + k, spot.plane(1)),
+                )
+            )
+        copies = [copy for pair in to_mate for copy in pair]
+        to_far = []
+        for k, slot in enumerate(slots):
+            yield
+            to_mate[k][0].wait_recv()
+            cross[k] = (
+                x[:, slot, part_rows(r ^ 2)].astype(F32) + mates[0, k].astype(F32)
+            ).astype(BF)
+            to_far.append(send(cross.at[k], gets.at[k], 8 + k, spot.plane(2)))
+        copies += to_far
+
+        def total(k):
+            to_mate[k][1].wait_recv()
+            to_far[k].wait_recv()
+            own = x[:, slots[k], part_rows(r)].astype(F32)
+            return own + mates[1, k].astype(F32) + gets[k].astype(F32)
+
+        yield
+        sums[0] = total(0).astype(BF)
+        c0 = send(sums.at[0, first], got.at[0], 12, spot.line(1))
+        c1 = send(sums.at[0, second], got.at[1], 13, spot.line(-1))
+        yield
+        sums[1] = total(1).astype(BF)
+        c2 = send(sums.at[1, second], got.at[2], 14, spot.line(1))
+        sums[2] = total(2).astype(BF)
+        c3 = send(sums.at[2, first], got.at[3], 15, spot.line(-1))
+        yield
+        c0.wait_recv()
+        turned[0] = (sums[1, first].astype(F32) + got[0].astype(F32)).astype(BF)
+        c4 = send(turned.at[0], got.at[4], 16, spot.line(1))
+        c1.wait_recv()
+        turned[1] = (sums[2, second].astype(F32) + got[1].astype(F32)).astype(BF)
+        c5 = send(turned.at[1], got.at[5], 17, spot.line(-1))
+        yield
+        mine = total(3)
+        c3.wait_recv()
+        c4.wait_recv()
+        out[first] = (mine[first] + got[3].astype(F32) + got[4].astype(F32)).astype(BF)
+        c2.wait_recv()
+        c5.wait_recv()
+        out[second] = (mine[second] + got[2].astype(F32) + got[5].astype(F32)).astype(BF)
+        for copy in copies + [c0, c1, c2, c3, c4, c5]:
+            copy.wait_send()
+
+    def plain(n_grp, n_head):
+        return lax.psum_scatter(x, "head", scatter_dimension=1)
+
+    out = jax.ShapeDtypeStruct((t, PART, w), BF)
+    block = (t, PART, w)
+    scratch = [
+        pltpu.VMEM((2, 4) + block, BF),
+        pltpu.VMEM((4,) + block, BF),
+        pltpu.VMEM((4,) + block, BF),
+        pltpu.VMEM((3,) + block, BF),
+        pltpu.VMEM((6, half, PART, w), BF),
+        pltpu.VMEM((2, half, PART, w), BF),
+    ]
+    return Job(x, out, scratch, 18, quad_peers, steps, plain)
 
 
 def small_peers(spot):
@@ -938,18 +1121,20 @@
     mine = jnp.full((TP,), g * n_head + h, jnp.int32)
     n_win = n_head if n_grp == 1 else 2 * n_head
     base = jnp.full((TP,), ((g + 1) * n_head - n_win) * TP, jnp.int32)
-    sc = jnp.stack([firsts, doc_start[:, -1], doc_start[:, 0] // SPAN, mine, base]).astype(jnp.int32)
+    part = jnp.full((TP,), t % QUAD, jnp.int32)
+    sc = jnp.stack([firsts, doc_start[:, -1], doc_start[:, 0] // SPAN, mine, base, part]).astype(jnp.int32)
     ds = doc_start[:, :, None].astype(jnp.int32)
 
     ext = jnp.concatenate([rim, tokens], axis=0).astype(F32)
     normed_mine, inv_ext = norm_parts(ext, gain_mix)
-    normed, w_in, w_gu_mine = run(
+    normed, w_in, w_gu_mine, cot_all = run(
         "inputs",
         2,
         jobs=[
             plane_gather(normed_mine.astype(BF)),
             line_gather(w_in_mine),
             plane_swap(packed[:, :, COLS:]),
+            plane_gather(cotangent),
         ],
     )
     normed = normed.reshape(TP * (RIM + SPAN), width)
@@ -982,14 +1167,12 @@
         [],
         "mixer_local",
     )
-    moves = [
-        line_gather(pay[:, RIM:, COL_KV:], "head"),
-        line_gather(slab),
-        plane_gather(cotangent),
-    ]
+    kv, slab = lax.optimization_barrier((pay[:, RIM:, COL_KV:], slab))
+    slabs = lax.all_gather(slab, SEQ)
+    moves = [quad_gather(kv)]
     if n_grp == 1:
         moves += [line_gather(w_attn_out[None]), line_gather(w_mamba_out[None])]
-    kv, slabs, cot_all, *w_outs = run("states", 3, jobs=moves)
+    kv, *w_outs = run("states", 3, jobs=moves)
     kv = kv.reshape(TP * n_head, SPAN, 128)
     if n_grp > 1:
         before = lax.ppermute(kv, "grp", [(a, a + 1) for a in range(n_grp - 1)])
@@ -999,7 +1182,6 @@
             for w, size in ((w_attn_out, HDIM), (w_mamba_out, MW))
         ]
     w_out = jnp.concatenate([w.reshape(-1, width) for w in w_outs], axis=0)
-    slabs = slabs.reshape(n_seq * TP, SLAB, STATE)
     cot_all = cot_all.reshape(TP * SPAN, width)
 
     s_q = block((1, RIM + SPAN, 128), "i", 0, 3)
@@ -1015,7 +1197,7 @@
         [],
         "attend",
     )
-    s_slabs = whole((n_seq * TP, SLAB, STATE))
+    s_slabs = whole((n_seq, TP, SLAB, STATE))
     s_state = block((1, MW, STATE), "i", 0, 0)
     branch, y_all, state_in = call(
         functools.partial(mixer_finish, n_head),
@@ -1032,26 +1214,24 @@
     def by_token(partial):
         return plane_scatter(partial.astype(BF).reshape(TP, -1, width))
 
-    mixed, w_gu, w_dn = run(
+    mixed, w_dn = run(
         "middle",
         4,
-        jobs=[
-            by_token(dot(branch, w_out)),
-            line_gather(w_gu_mine),
-            line_gather(w_down[None]),
-        ],
-    )
-    w_gu = w_gu.reshape(width, 2 * ff_part)
+        jobs=[by_token(dot(branch, w_out)), line_gather(w_down[None])],
+    )
     w_dn = w_dn.reshape(ff_part, width)
     mixed = tokens.astype(F32) + mixed
     ffn_local, inv_ffn = norm_parts(mixed, gain_ffn)
-    (ffn_in,) = run("ffn", 5, jobs=[plane_gather(ffn_local.astype(BF))])
+    ffn_in, w_gu = run(
+        "ffn", 5, jobs=[plane_gather(ffn_local.astype(BF)), line_gather(w_gu_mine)]
+    )
+    w_gu = w_gu.reshape(width, 2 * ff_part)
     ffn_in = ffn_in.reshape(TP * SPAN, width)
     gate = dot(ffn_in, w_gu[:, :ff_part])
     up = dot(ffn_in, w_gu[:, ff_part:])
     sig = sigmoid(gate)
     hidden = (gate * sig * up).astype(BF)
-    ffn_out = by_token(dot(hidden, w_dn))
+    ffn_out = dot(hidden, w_dn).astype(BF)
 
     d_hidden = dot_rt(cot_all, w_dn)
     g_down = dot_lt(hidden, cot_all)
@@ -1092,6 +1272,8 @@
         [],
         "mixer_entry",
     )
+    dh, d_entry = lax.optimization_barrier((dh, d_entry))
+    d_entries = lax.all_gather(d_entry, SEQ)
     dq, dkv = call(
         functools.partial(attend_back, n_head),
         sc,
@@ -1105,26 +1287,22 @@
     if n_grp > 1:
         back = lax.ppermute(dkv[: TP * n_head], "grp", [(a + 1, a) for a in range(n_grp - 1)])
         dkv = dkv[TP * n_head :] + back
-    moves = [
-        line_scatter(dkv.reshape(TP, n_head, SPAN, 128), BF, "head"),
-        line_gather(d_entry),
-        ffn_out,
-        plane_swap(g_gu),
-    ]
+    moves = [quad_scatter(dkv.reshape(TP, n_head, SPAN, 128)), plane_swap(g_gu)]
     if n_grp == 1:
         moves += [
             line_scatter(g_out[:HDIM].astype(BF).reshape(1, n_head, -1, width), F32),
             line_scatter(g_out[HDIM:].astype(BF).reshape(1, n_head, -1, width), F32),
         ]
-    dkv, d_entries, ffn_out, parts_gu, *g_outs = run("states_back", 8, jobs=moves)
-    d_entries = d_entries.reshape(n_seq * TP, MW, STATE)
+    dkv, parts_gu, *g_outs = run("states_back", 8, jobs=moves)
+    ffn_out, dkv = lax.optimization_barrier((ffn_out, dkv))
+    ffn_out = lax.psum_scatter(ffn_out, "tp", tiled=True).astype(F32)
     result = (mixed + ffn_out).astype(BF)
     d_pay, d_taps, d_small = call(
         functools.partial(mixer_back, n_head),
         sc,
         (slabs, d_entries, dh, pay, ds, state_in, y_all, dq, dkv) + params,
-        [s_slabs, whole((n_seq * TP, MW, STATE)), s_dh, s_pay, s_ds, s_state]
-        + [block(f_y, "i", 0, 0), s_o, s_o]
+        [s_slabs, whole((n_seq, TP, MW, STATE)), s_dh, s_pay, s_ds, s_state]
+        + [block(f_y, "i", 0, 0), s_o, block((1,) + dkv.shape[1:], "i", 0, 0)]
         + s_params,
         [((TP, RIM + SPAN, COLS), BF), ((8, CH), F32), ((8, STATE), F32)],
         [s_pay, whole((8, CH)), whole((8, STATE))],
@@ -1171,36 +1349,13 @@
     d_norm_in = d_norm_in[RIM:].at[rows - RIM :].add(rim_back.astype(F32))
     d_tok, _ = norm_back(ext[RIM:], inv_ext[RIM:], gain_mix, d_norm_in)
     grad_tokens = d_mixed + d_tok
-    parts, parts_gu = parts.astype(F32), parts_gu.astype(F32)
-
-    def join_tp(p):
-        return p.transpose(1, 0, 2).reshape(r, -1)
-
-    def join_kv(p):
-        return join_tp(jnp.sum(p.reshape(KVHEADS, TP // KVHEADS, r, HDIM), axis=1))
-
-    def join_ff(p):
-        return p.reshape(TP, r, n_grp, -1).transpose(1, 2, 0, 3).reshape(r, ff)
-
-    grad_qkv = jnp.concatenate(
-        [
-            join_tp(parts[:, :, COL_Q : COL_Q + HDIM]),
-            join_kv(parts[:, :, COL_KV + HDIM :]),
-            join_kv(parts[:, :, COL_KV : COL_KV + HDIM]),
+    grad_qkv, grad_min, grad_gate, grad_up = pl.pallas_call(
+        functools.partial(assemble, n_grp),
+        out_shape=[
+            jax.ShapeDtypeStruct(w.shape, F32) for w in (w_qkv, w_mamba_in, w_gate, w_up)
         ],
-        axis=1,
-    )
-    grad_min = jnp.concatenate(
-        [
-            join_tp(parts[:, :, COL_Z : COL_Z + MW]),
-            join_tp(parts[:, :, 2 * STATE : CH]),
-            jnp.sum(parts[:, :, : 2 * STATE], axis=0),
-            join_tp(parts[:, :, COL_DT : COL_DT + MH]),
-        ],
-        axis=1,
-    )
-    grad_gate = join_ff(parts_gu[:, :, :ff_part])
-    grad_up = join_ff(parts_gu[:, :, ff_part:])
+        name="assemble",
+    )(parts, parts_gu)
     if n_grp == 1:
         grad_ao, grad_mo = (v.reshape(-1, width) for v in g_outs)
     else:

time: 682 us -> 595 us (0.87); the launches traced: 673 us -> 599 us
  Pallas kernels: 552 us -> 467 us
  between operations: 1.69 us -> 14.6 us
  local copies, waits for them, and re-layouts: 40.4 us -> 28 us
  starting transfers between devices: 0 us -> 11.8 us
    pallas_call x10, Pallas kernels: 410 us -> 319 us  [communicate(): pl.pallas_call(kernel, out_shape=[job.out for job in jobs], in_specs=[pl....]
    all_gather x0 -> x2, starting transfers between devices: none -> 11.8 us  [the longest x1 11.8 us: per_device(): d_entries = lax.all_gather(d_entry, SEQ)]
    reshape x7 -> x0, local copies, waits for them, and re-layouts: 7.99 us -> none  [join_tp(): return p.transpose(1, 0, 2).reshape(r, -1)]
    transpose x10 -> x0, local copies, waits for them, and re-layouts: 7.47 us -> none  [the longest x9 7.43 us: join_tp(): return p.transpose(1, 0, 2).reshape(r, -1)]
  transfers between devices with their start and end apart: 0 -> 3, of which waited for: 0 -> 0; matrix products, arithmetic and copies ran while one was open for 0% -> 6% of each run, Pallas kernels for 0% -> 40%
where the time goes in v3:
time: 595 us; the launch traced here: 599 us
  Pallas kernels  467 us (78%)
  matrix products  56.2 us (9%)
  local copies, waits for them, and re-layouts  28 us (5%)
  other arithmetic  20.6 us (3%)
  between operations  14.6 us (2%)
  starting transfers between devices  11.8 us (2%)
    pallas_call x10, Pallas kernels, communicate(): pl.pallas_call(kernel, out_shape=[job.out for job in jobs], in_specs=[pl....  319 us
    pallas_call x6, Pallas kernels, call(): pl.pallas_call(kernel, out_shape=[jax.ShapeDtypeStruct(s, d) for s, d in...  146 us
    dot_general x5, matrix products, dot(): return jnp.dot(a, b, preferred_element_type=F32)  21.2 us
    dot_general x4, matrix products, dot_rt(): lax.dot_general(a, b, (((1,), (1,)), ((), ())), preferred_element_type=F32)  19.8 us
    dot_general x4, matrix products, dot_lt(): lax.dot_general(a, b, (((0,), (0,)), ((), ())), preferred_element_type=F32)  15.2 us
  transfers between devices with their start and end apart: 3, of which 0 were waited for; matrix products, arithmetic and copies ran while one was open for 6% of the time, Pallas kernels for 40%

profile of v3, /device:TPU:0, one launch (start us, length us, event | category | flops | bytes accessed | tf_op | source)
XLA Modules:
  0.0 598.6 jit_solution(13664612575855865831)
XLA Ops:
  16.6 17.9 %open.1 = (f32[8,4,8,128]{3,2,1,0:T(8,128)}, bf16[8,1024]{1,0:T(8,128)(2,1)}, bf16[8,32,896]{2,1,0:T(8,128)(2,1)}) custom-call(f32[8,128]{1,0:T(8,128)} %select_maximum_fusion.2.refs_0_, bf16[8,1024]{1,0:T(8,128)(2,1)} %slice.179.refs_1_, bf16[8,32,896]{2,1,0:T(8,128)(2,1)} %concatenate.38.refs_2_), custom_call_target="tpu_custom_call" | custom-call | tf_op jit(solution)/shard_map/open/pallas_call | solution.py:558
  43.6 49.3 %inputs.1 = (bf16[8,264,1024]{2,1,0:T(8,128)(2,1)}, bf16[8,4,32,896]{3,2,1,0:T(8,128)(2,1)}, bf16[8,32,512]{2,1,0:T(8,128)(2,1)}, bf16[8,256,1024]{2,1,0:T(8,128)(2,1)}) custom-call(bf16[264,1024]{1,0:T(8,128)(2,1)} %multiply_convert_fusion.3.refs_0_, bf16[8,32,896]{2,1,0:T(8,128)(2,1)} %get-tuple-element.93.refs_1_, ...), custom_call_target="tpu_custom_call" | custom-call | tf_op jit(solution)/shard_map/inputs/pallas_call | solution.py:558
  92.9 7.5 %convolution_convert_fusion.1 = bf16[2112,896]{1,0:T(8,128)(2,1)S(1)} fusion(bf16[2112,1024]{1,0:T(8,128)(2,1)} %bitcast.201, bf16[1024,896]{1,0:T(8,128)(2,1)} %bitcast.211), kind=kOutput, calls=%fused_computation.1 | convolution fusion | flops 3877429248 | bytes 9945088 | tf_op jit(solution)/shard_map/dot_general | solution.py:42
  104.3 20.4 %mixer_local.1 = (f32[8,256,448]{2,1,0:T(8,128)}, f32[8,256,128]{2,1,0:T(8,128)}, f32[8,256,192]{2,1,0:T(8,128)}, bf16[8,200,128]{2,1,0:T(8,128)(2,1)}) custom-call(s32[6,8]{1,0:T(8,128)} %stack.35.sc, bf16[8,264,896]{2,1,0:T(8,128)(2,1)} %bitcast.135, s32[8,256,1]{2,1,0:T(8,128)} %copy.94.ds, f32[8,448]{1,0:T(8,128)} %concatenate.42.taps, ...), custom_call_target="tpu_custom_call" | custom-call | tf_op jit(solution)/shard_map/mixer_local/pallas_call | solution.py:463
  124.7 11.8 %all-gather.7.cloned.1.call-start = ((), (), s32[]{:S(2)}) async-start(), calls=%async_computation.3 | async-start | bytes 1966080 | tf_op jit(solution)/shard_map/all_gather | solution.py:1276
  136.5 41.8 %states.1 = (bf16[8,4,256,128]{3,2,1,0:T(8,128)(2,1)}, bf16[1,4,16,1024]{3,2,1,0:T(8,128)(2,1)}, bf16[1,4,48,1024]{3,2,1,0:T(8,128)(2,1)}) custom-call(bf16[8,256,128]{2,1,0:T(8,128)(2,1)} %slice.221.refs_0_, bf16[1,16,1024]{2,1,0:T(8,128)(2,1)} %bitcast.188, bf16[1,48,1024]{2,1,0:T(8,128)(2,1)} %bitcast.182), custom_call_target="tpu_custom_call" | custom-call | tf_op jit(solution)/shard_map/states/pallas_call | solution.py:558
  178.3 26.0 %attend.1 = (f32[8,256,128]{2,1,0:T(8,128)}, f32[8,256,1]{2,1,0:T(8,128)}) custom-call(s32[6,8]{1,0:T(8,128)} %stack.35.sc, bf16[8,264,896]{2,1,0:T(8,128)(2,1)} %bitcast.136, s32[8,256,1]{2,1,0:T(8,128)} %copy.94.ds, bf16[32,256,128]{2,1,0:T(8,128)(2,1)} %bitcast.145), custom_call_target="tpu_custom_call" | custom-call | tf_op jit(solution)/shard_map/attend/pallas_call | solution.py:463
  204.4 11.9 %mixer_finish.1 = (bf16[8,256,256]{2,1,0:T(8,128)(2,1)}, f32[8,256,192]{2,1,0:T(8,128)}, f32[8,192,128]{2,1,0:T(8,128)}) custom-call(s32[6,8]{1,0:T(8,128)} %stack.35.sc, bf16[4,8,200,128]{3,2,1,0:T(8,128)(2,1)} %bitcast.147, f32[8,256,448]{2,1,0:T(8,128)} %get-tuple-element.98.u, f32[8,256,128]{2,1,0:T(8,128)} %get-tuple-element.99.cum, ...), custom_call_target="tpu_custom_call" | custom-call | tf_op jit(solution)/shard_map/mixer_finish/pallas_call | solution.py:463
  216.3 4.4 convolution_convert_fusion.4
  220.7 38.4 %middle.1 = (f32[256,1024]{1,0:T(8,128)}, bf16[1,4,64,1024]{3,2,1,0:T(8,128)(2,1)}) custom-call(bf16[8,256,1024]{2,1,0:T(8,128)(2,1)} %bitcast.141, bf16[1,64,1024]{2,1,0:T(8,128)(2,1)} %bitcast.179), custom_call_target="tpu_custom_call" | custom-call | tf_op jit(solution)/shard_map/middle/pallas_call | solution.py:558
  261.6 27.7 %ffn.1 = (bf16[8,256,1024]{2,1,0:T(8,128)(2,1)}, bf16[8,4,32,512]{3,2,1,0:T(8,128)(2,1)}) custom-call(bf16[256,1024]{1,0:T(8,128)(2,1)} %multiply_convert_fusion.4.refs_0_, bf16[8,32,512]{2,1,0:T(8,128)(2,1)} %get-tuple-element.108.refs_1_), custom_call_target="tpu_custom_call" | custom-call | tf_op jit(solution)/shard_map/ffn/pallas_call | solution.py:558
  289.3 3.7 fusion.1
  295.5 2.2 multiply_convert_fusion.1
  297.8 3.4 convolution_convert_fusion.6
  301.2 4.4 convolution_convert_fusion.2
  305.6 2.1 convolution_convert_fusion.7
  307.7 27.5 %ffn_back.1 = (f32[256,1024]{1,0:T(8,128)}, f32[1,64,1024]{2,1,0:T(8,128)}) custom-call(bf16[8,256,1024]{2,1,0:T(8,128)(2,1)} %bitcast.150, bf16[1,4,64,1024]{3,2,1,0:T(8,128)(2,1)} %bitcast.159), custom_call_target="tpu_custom_call" | custom-call | tf_op jit(solution)/shard_map/ffn_back/pallas_call | solution.py:558
  338.8 25.3 %branch_back.1 = (bf16[8,256,1024]{2,1,0:T(8,128)(2,1)}, bf16[8,32,512]{2,1,0:T(8,128)(2,1)}) custom-call(bf16[256,1024]{1,0:T(8,128)(2,1)} %get-tuple-element.148.refs_0_, bf16[8,4,32,512]{3,2,1,0:T(8,128)(2,1)} %bitcast.156), custom_call_target="tpu_custom_call" | custom-call | tf_op jit(solution)/shard_map/branch_back/pallas_call | solution.py:558
  364.2 4.5 convolution_convert_fusion.5
  368.6 10.5 %mixer_entry.1 = bf16[8,192,128]{2,1,0:T(8,128)(2,1)} custom-call(s32[6,8]{1,0:T(8,128)} %stack.35.sc, bf16[8,256,256]{2,1,0:T(8,128)(2,1)} %bitcast.142, f32[8,256,448]{2,1,0:T(8,128)} %get-tuple-element.98.u, f32[8,256,128]{2,1,0:T(8,128)} %get-tuple-element.99.cum, bf16[8,264,896]{2,1,0:T(8,128)(2,1)} %bitcast.138, s32[8,256,1]{2,1,0:T(8,128)} %copy.94.ds), custom_call_target="tpu_custom_call" | custom-call | tf_op jit(solution)/shard_map/mixer_entry/pallas_call | solution.py:463
  379.3 3.5 fusion
  384.2 32.3 %attend_back.1 = (f32[8,256,128]{2,1,0:T(8,128)}, bf16[32,256,128]{2,1,0:T(8,128)(2,1)}) custom-call(s32[6,8]{1,0:T(8,128)} %stack.35.sc, bf16[8,264,896]{2,1,0:T(8,128)(2,1)} %bitcast.139, s32[8,256,1]{2,1,0:T(8,128)} %copy.94.ds, bf16[8,256,256]{2,1,0:T(8,128)(2,1)} %bitcast.143, f32[8,256,128]{2,1,0:T(8,128)} %get-tuple-element.103.o, ...), custom_call_target="tpu_custom_call" | custom-call | tf_op jit(solution)/shard_map/attend_back/pallas_call | solution.py:463
  416.5 39.7 %states_back.1 = (bf16[8,64,128]{2,1,0:T(8,128)(2,1)}, bf16[8,32,512]{2,1,0:T(8,128)(2,1)}, f32[1,16,1024]{2,1,0:T(8,128)}, f32[1,48,1024]{2,1,0:T(8,128)}) custom-call(bf16[8,4,256,128]{3,2,1,0:T(8,128)(2,1)} %bitcast.152, bf16[8,32,512]{2,1,0:T(8,128)(2,1)} %get-tuple-element.118.refs_1_, bf16[1,4,16,1024]{3,2,1,0:T(8,128)(2,1)} %bitcast.160, ...), custom_call_target="tpu_custom_call" | custom-call | tf_op jit(solution)/shard_map/states_back/pallas_call | solution.py:558
  456.2 3.3 convolution_convert_fusion.3
  460.8 44.5 %mixer_back.1 = (bf16[8,264,896]{2,1,0:T(8,128)(2,1)}, f32[8,448]{1,0:T(8,128)}, f32[8,128]{1,0:T(8,128)}) custom-call(s32[6,8]{1,0:T(8,128)} %stack.35.sc, bf16[4,8,200,128]{3,2,1,0:T(8,128)(2,1)} %bitcast.148, bf16[4,8,192,128]{3,2,1,0:T(8,128)(2,1)} %bitcast.155, bf16[8,256,256]{2,1,0:T(8,128)(2,1)} %bitcast.144, bf16[8,264,896]{2,1,0:T(8,128)(2,1)} %bitcast.140, ...), custom_call_target="tpu_custom_call" | custom-call | tf_op jit(solution)/shard_map/mixer_back/pallas_call | solution.py:463
  505.4 9.6 %convolution_convert_fusion = bf16[2112,1024]{1,0:T(8,128)(2,1)} fusion(bf16[2112,896]{1,0:T(8,128)(2,1)} %bitcast.210, bf16[1024,896]{1,0:T(8,128)(2,1)} %bitcast.212), kind=kOutput, calls=%fused_computation | convolution fusion | flops 3877699584 | bytes 9945088 | tf_op jit(solution)/shard_map/dot_general | solution.py:50
  515.0 6.2 %bitcast_convert_fusion = bf16[1024,896]{1,0:T(8,128)(2,1)} fusion(bf16[8,264,1024]{2,1,0:T(8,128)(2,1)S(1)} %bitcast.203, bf16[8,264,896]{2,1,0:T(8,128)(2,1)S(1)} %copy-done.22), kind=kOutput, calls=%fused_computation.5 | convolution fusion | flops 3876454400 | bytes 9945088 | tf_op jit(solution)/shard_map/dot_general | solution.py:46
  521.2 35.0 %inputs_back.1 = (f32[264,1024]{1,0:T(8,128)}, bf16[8,32,896]{2,1,0:T(8,128)(2,1)}) custom-call(bf16[8,264,1024]{2,1,0:T(8,128)(2,1)} %bitcast.149, bf16[8,4,32,896]{3,2,1,0:T(8,128)(2,1)} %bitcast.153), custom_call_target="tpu_custom_call" | custom-call | tf_op jit(solution)/shard_map/inputs_back/pallas_call | solution.py:558
  560.9 16.8 %close.1 = (f32[8,128]{1,0:T(8,128)}, bf16[8,32,896]{2,1,0:T(8,128)(2,1)}, bf16[8,1024]{1,0:T(8,128)(2,1)}) custom-call(f32[8,4,8,128]{3,2,1,0:T(8,128)} %bitcast.161, bf16[8,32,896]{2,1,0:T(8,128)(2,1)} %get-tuple-element.130.refs_1_, bf16[8,1024]{1,0:T(8,128)(2,1)} %slice.262.refs_2_), custom_call_target="tpu_custom_call" | custom-call | tf_op jit(solution)/shard_map/close/pallas_call | solution.py:558
  579.0 2.2 assemble.1
  585.0 2.8 subtract_add_fusion
  587.9 2.0 add_convert_fusion
  (171 shorter events, 45.2 us)
Async XLA Ops:
  7.2 8.3 %slice-start = ((bf16[32,3352]{1,0:T(8,128)(2,1)}), bf16[32,256]{1,0:T(8,128)(2,1)S(1)}, s32[]{:S(2)}) async-start(bf16[32,3352]{1,0:T(8,128)(2,1)} %param.24), calls=%async_computation.4 | async-start | bytes 32768 | tf_op jit(solution)/shard_map/slice | solution.py:1058
  7.2 197.2 %all-gather.5.cloned.1.call-start = ((), (), s32[]{:S(2)}) async-start(), calls=%async_computation.2 | async-start | bytes 2048000 | tf_op jit(solution)/shard_map/all_gather | solution.py:1171
  10.6 27.6 %copy-start.24 = (s32[4]{0:T(128)S(1)}, s32[4]{0:T(128)}, u32[]{:S(2)}) copy-start(s32[4]{0:T(128)} %param.36) | copy-start | bytes 52
  10.6 28.1 %copy-start.1 = (bf16[256,1024]{1,0:T(8,128)(2,1)S(1)}, bf16[256,1024]{1,0:T(8,128)(2,1)}, u32[]{:S(2)}) copy-start(bf16[256,1024]{1,0:T(8,128)(2,1)} %param.21) | copy-start | bytes 1572868
  11.0 28.6 %copy-start.14 = (bf16[32,2048]{1,0:T(8,128)(2,1)S(1)}, bf16[32,2048]{1,0:T(8,128)(2,1)}, u32[]{:S(2)}) copy-start(bf16[32,2048]{1,0:T(8,128)(2,1)} %param.33) | copy-start | bytes 393220
  13.4 26.2 %copy-start.15 = (bf16[32,2048]{1,0:T(8,128)(2,1)S(1)}, bf16[32,2048]{1,0:T(8,128)(2,1)}, u32[]{:S(2)}) copy-start(bf16[32,2048]{1,0:T(8,128)(2,1)} %param.34) | copy-start | bytes 393220
  34.5 7.3 %copy-start.10 = (bf16[8,1024]{1,0:T(8,128)(2,1)S(1)}, bf16[8,1024]{1,0:T(8,128)(2,1)}, u32[]{:S(2)}) copy-start(bf16[8,1024]{1,0:T(8,128)(2,1)} %get-tuple-element.91) | copy-start | bytes 49156
  100.4 1.8 copy-start
  124.7 336.1 %all-gather.7.cloned.1.call-start = ((), (), s32[]{:S(2)}) async-start(), calls=%async_computation.3 | async-start | bytes 1966080 | tf_op jit(solution)/shard_map/all_gather | solution.py:1276
  204.4 11.9 %copy-start.9 = (bf16[1,4,48,1024]{3,2,1,0:T(8,128)(2,1)S(1)}, bf16[1,4,48,1024]{3,2,1,0:T(8,128)(2,1)}, u32[]{:S(2)}) copy-start(bf16[1,4,48,1024]{3,2,1,0:T(8,128)(2,1)} %get-tuple-element.106) | copy-start | bytes 1179652
  204.4 11.9 %copy-start.13 = (bf16[1,4,16,1024]{3,2,1,0:T(8,128)(2,1)S(1)}, bf16[1,4,16,1024]{3,2,1,0:T(8,128)(2,1)}, u32[]{:S(2)}) copy-start(bf16[1,4,16,1024]{3,2,1,0:T(8,128)(2,1)} %get-tuple-element.105) | copy-start | bytes 393220
  289.3 3.8 copy-start.8
  289.3 3.8 copy-start.20
  293.1 2.2 copy-start.21
  293.1 2.5 copy-start.23
  297.8 7.9 %copy-start.5 = (bf16[2048,256]{0,1:T(8,128)(2,1)}, bf16[2048,256]{0,1:T(8,128)(2,1)S(1)}, u32[]{:S(2)}) copy-start(bf16[2048,256]{0,1:T(8,128)(2,1)S(1)} %get-tuple-element.153) | copy-start | bytes 3145732
  335.3 1.7 copy-start.3
  335.3 1.7 copy-start.7
  368.6 10.6 %copy-start.4 = (bf16[8,256,256]{2,1,0:T(8,128)(2,1)S(1)}, bf16[8,256,256]{2,1,0:T(8,128)(2,1)}, u32[]{:S(2)}) copy-start(bf16[8,256,256]{2,1,0:T(8,128)(2,1)} %get-tuple-element.104) | copy-start | bytes 3145732
  379.2 208.6 %reduce-scatter.2.cloned.1.call-start = ((), (), s32[]{:S(2)}) async-start(), calls=%async_computation.1 | async-start | bytes 4718592 | tf_op jit(solution)/shard_map/reduce_scatter | solution.py:1298
  416.5 39.7 %copy-start.6 = (bf16[2048,256]{0,1:T(8,128)(2,1)S(1)}, bf16[2048,256]{0,1:T(8,128)(2,1)}, u32[]{:S(2)}) copy-start(bf16[2048,256]{0,1:T(8,128)(2,1)} %copy-done.5) | copy-start | bytes 3145732
  460.8 54.2 %slice-start.1 = ((s8[4325376]{0:T(1024)(128)(4,1)}), s8[131072]{0:T(1024)(128)(4,1)S(1)}, s32[]{:S(2)}) async-start(s8[4325376]{0:T(1024)(128)(4,1)} %bitcast.202), calls=%async_computation.5 | async-start | bytes 262144
  505.4 9.6 %slice-start.2 = ((s8[4325376]{0:T(1024)(128)(4,1)}), s8[4194304]{0:T(1024)(128)(4,1)S(1)}, s32[]{:S(2)}) async-start(s8[4325376]{0:T(1024)(128)(4,1)} %bitcast.202), calls=%async_computation.6 | async-start | bytes 8388608
  505.4 9.6 %copy-start.22 = (bf16[8,264,896]{2,1,0:T(8,128)(2,1)S(1)}, bf16[8,264,896]{2,1,0:T(8,128)(2,1)}, u32[]{:S(2)}) copy-start(bf16[8,264,896]{2,1,0:T(8,128)(2,1)} %get-tuple-element.126) | copy-start | bytes 11354116
  556.3 2.8 copy-start.2
  556.3 3.0 copy-start.17
  556.3 3.4 copy-start.19
  577.7 5.7 copy-start.18
  587.8 2.1 copy-start.16
  587.8 2.7 copy-start.12
  587.8 3.4 copy-start.11
Sparse Core Ops, SparseCore 0:
  124.8 53.7 all-gather.4
  379.3 36.1 all-gather.6
  459.7 49.4 reduce-scatter.1

commit v4 on v3

--- a/solution.py
+++ b/solution.py
@@ -18,9 +18,10 @@
 SPAN = 256
 TP = 8
 RIM = 8
+KEYS = 512
 
 EPS = 1e-06
-HIGH = lax.Precision.HIGHEST
+HIGH = lax.Precision.HIGH
 NEG = -1e30
 BF = jnp.bfloat16
 F32 = jnp.float32
@@ -169,7 +170,7 @@
     state = states[i]
     state_out[0] = state
     entry = jnp.where(ds[0] < first, jnp.exp(cum[0]), 0.0)
-    carried = hdot_rt(u[0, :, STATE : 2 * STATE], state)
+    carried = hdot_rt(u[0], state)
     y = yl[0] + heads_wide(entry) * carried
     y_out[0] = y
     z = pay[0, RIM:, :MW].astype(F32)
@@ -184,7 +185,7 @@
     dym = dh[0].astype(F32)[:, HDIM:]
     entry = jnp.where(ds[0] < first, jnp.exp(cum[0]), 0.0)
     scaled = dym * (z * sigmoid(z)) * heads_wide(entry)
-    entry_out[0] = hdot_lt(scaled, u[0, :, STATE : 2 * STATE]).astype(BF)
+    entry_out[0] = hdot_lt(scaled, u[0]).astype(BF)
 
 
 def mixer_back(
@@ -343,7 +344,9 @@
     first = sc[0, i]
     low = sc[2, i]
     base = sc[4, i]
-    mine = first // SPAN
+    origin = base * SPAN
+    mine = (first - origin) // KEYS
+    low = (low - base) // (KEYS // SPAN)
     lane = iota((SPAN, 128), 1)
     q = jnp.where(lane >= HDIM, pay_q[0, RIM:] * jnp.asarray(HDIM**-0.5, BF), jnp.asarray(0, BF))
     start = ds[0]
@@ -351,10 +354,9 @@
 
     def one(c, carry):
         top, total, acc = carry
-        slot = c - base
-        keys = kv[slot]
+        keys = kv[c]
         s = dot_rt(q, keys)
-        key = c * SPAN + iota((SPAN, SPAN), 1)
+        key = origin + c * KEYS + iota((SPAN, KEYS), 1)
         s = jnp.where((key >= start) & (key <= pos), s, NEG)
         new_top = jnp.maximum(top, jnp.max(s, axis=1, keepdims=True))
         fade = jnp.exp(top - new_top)
@@ -379,7 +381,9 @@
     first = sc[0, i]
     low = sc[2, i]
     base = sc[4, i]
-    mine = first // SPAN
+    origin = base * SPAN
+    mine = (first - origin) // KEYS
+    low = (low - base) // (KEYS // SPAN)
     lane = iota((SPAN, 128), 1)
     scale = HDIM**-0.5
     q = jnp.where(lane >= HDIM, pay_q[0, RIM:] * jnp.asarray(scale, BF), jnp.asarray(0, BF))
@@ -390,14 +394,13 @@
     sums = lse[0]
 
     def one(c, d_q):
-        slot = c - base
-        keys = kv[slot]
+        keys = kv[c]
         s = dot_rt(q, keys)
-        key = c * SPAN + iota((SPAN, SPAN), 1)
+        key = origin + c * KEYS + iota((SPAN, KEYS), 1)
         p = jnp.exp(jnp.where((key >= start) & (key <= pos), s - sums, NEG))
         dp = dot_rt(do, keys)
         d_s = (p * (dp - delta)).astype(BF)
-        acc_kv[slot] += dot_lt(d_s, q) + dot_lt(p.astype(BF), do)
+        acc_kv[c] += dot_lt(d_s, q) + dot_lt(p.astype(BF), do)
         return d_q + dot(d_s, keys)
 
     dq_out[0] = lax.fori_loop(low, mine + 1, one, jnp.zeros((SPAN, 128), F32)) * scale
@@ -1137,6 +1140,17 @@
             plane_gather(cotangent),
         ],
     )
+    if n_grp == 1:
+        w_rows, normed = lax.optimization_barrier(
+            (jnp.concatenate([w_attn_out, w_mamba_out, w_down], axis=0), normed)
+        )
+        w_rows = lax.all_gather(w_rows, SEQ)
+    else:
+        w_outs = [
+            lax.dynamic_slice_in_dim(lax.all_gather(w, ALL, tiled=True), t * size, size, 0)
+            for w, size in ((w_attn_out, HDIM), (w_mamba_out, MW))
+        ]
+        w_dn = lax.all_gather(w_down, SEQ, tiled=True)
     normed = normed.reshape(TP * (RIM + SPAN), width)
     w_in = w_in.reshape(width, COLS)
     pay = dot(normed, w_in).astype(BF).reshape(TP, RIM + SPAN, COLS)
@@ -1167,26 +1181,26 @@
         [],
         "mixer_local",
     )
-    kv, slab = lax.optimization_barrier((pay[:, RIM:, COL_KV:], slab))
+    kv = pay[:, RIM:, COL_KV:]
+    if n_grp == 1:
+        kv, slab, w_rows = lax.optimization_barrier((kv, slab, w_rows))
+        w_attn_rows, w_mamba_rows = w_attn_out.shape[0], w_mamba_out.shape[0]
+        w_outs = [w_rows[:, :w_attn_rows], w_rows[:, w_attn_rows : w_attn_rows + w_mamba_rows]]
+        w_dn = w_rows[:, w_attn_rows + w_mamba_rows :]
     slabs = lax.all_gather(slab, SEQ)
-    moves = [quad_gather(kv)]
-    if n_grp == 1:
-        moves += [line_gather(w_attn_out[None]), line_gather(w_mamba_out[None])]
-    kv, *w_outs = run("states", 3, jobs=moves)
+    (kv,) = run("states", 3, jobs=[quad_gather(kv)])
     kv = kv.reshape(TP * n_head, SPAN, 128)
     if n_grp > 1:
         before = lax.ppermute(kv, "grp", [(a, a + 1) for a in range(n_grp - 1)])
         kv = jnp.concatenate([before, kv], axis=0)
-        w_outs = [
-            lax.dynamic_slice_in_dim(lax.all_gather(w, ALL, tiled=True), t * size, size, 0)
-            for w, size in ((w_attn_out, HDIM), (w_mamba_out, MW))
-        ]
     w_out = jnp.concatenate([w.reshape(-1, width) for w in w_outs], axis=0)
     cot_all = cot_all.reshape(TP * SPAN, width)
 
     s_q = block((1, RIM + SPAN, 128), "i", 0, 3)
     s_o = block((1, SPAN, 128), "i", 0, 0)
-    s_kv = whole((n_win * TP, SPAN, 128))
+    key_blocks = (n_win * TP * SPAN // KEYS, KEYS, 128)
+    kv = kv.reshape(key_blocks)
+    s_kv = whole(key_blocks)
     o, lse = call(
         functools.partial(attend, n_head),
         sc,
@@ -1197,13 +1211,15 @@
         [],
         "attend",
     )
+    w_gu, slabs, o = lax.optimization_barrier((w_gu_mine, slabs, o))
+    w_gu = line_gather(w_gu).plain(n_grp, n_head)
     s_slabs = whole((n_seq, TP, SLAB, STATE))
     s_state = block((1, MW, STATE), "i", 0, 0)
     branch, y_all, state_in = call(
         functools.partial(mixer_finish, n_head),
         sc,
         (slabs, u, cum, y_local, pay, ds, o),
-        [s_slabs, block(f_u, "i", 0, 0), block(f_c, "i", 0, 0), block(f_y, "i", 0, 0), s_z, s_ds, s_o],
+        [s_slabs, block(f_c, "i", 0, 1), block(f_c, "i", 0, 0), block(f_y, "i", 0, 0), s_z, s_ds, s_o],
         [((TP, SPAN, 256), BF), ((TP, SPAN, MW), F32), ((TP, MW, STATE), F32)],
         [block((1, SPAN, 256), "i", 0, 0), block(f_y, "i", 0, 0), s_state],
         [pltpu.VMEM((TP, MW, STATE), F32)],
@@ -1214,17 +1230,11 @@
     def by_token(partial):
         return plane_scatter(partial.astype(BF).reshape(TP, -1, width))
 
-    mixed, w_dn = run(
-        "middle",
-        4,
-        jobs=[by_token(dot(branch, w_out)), line_gather(w_down[None])],
-    )
+    (mixed,) = run("middle", 4, jobs=[by_token(dot(branch, w_out))])
     w_dn = w_dn.reshape(ff_part, width)
     mixed = tokens.astype(F32) + mixed
     ffn_local, inv_ffn = norm_parts(mixed, gain_ffn)
-    ffn_in, w_gu = run(
-        "ffn", 5, jobs=[plane_gather(ffn_local.astype(BF)), line_gather(w_gu_mine)]
-    )
+    (ffn_in,) = run("ffn", 5, jobs=[plane_gather(ffn_local.astype(BF))])
     w_gu = w_gu.reshape(width, 2 * ff_part)
     ffn_in = ffn_in.reshape(TP * SPAN, width)
     gate = dot(ffn_in, w_gu[:, :ff_part])
@@ -1266,7 +1276,7 @@
         mixer_entry,
         sc,
         (dh, u, cum, pay, ds),
-        [s_dh, block(f_u, "i", 0, 0), block(f_c, "i", 0, 0), s_z, s_ds],
+        [s_dh, block(f_c, "i", 0, 1), block(f_c, "i", 0, 0), s_z, s_ds],
         [((TP, MW, STATE), BF)],
         [s_state],
         [],
@@ -1279,22 +1289,18 @@
         sc,
         (pay, ds, dh, o, lse, kv),
         [s_q, s_ds, block((1, SPAN, 128), "i", 0, 0), s_o, s_ds, s_kv],
-        [((TP, SPAN, 128), F32), ((n_win * TP, SPAN, 128), BF)],
+        [((TP, SPAN, 128), F32), (key_blocks, BF)],
         [s_o, s_kv],
-        [pltpu.VMEM((n_win * TP, SPAN, 128), F32)],
+        [pltpu.VMEM(key_blocks, F32)],
         "attend_back",
     )
+    dkv = dkv.reshape(n_win * TP, SPAN, 128)
     if n_grp > 1:
         back = lax.ppermute(dkv[: TP * n_head], "grp", [(a + 1, a) for a in range(n_grp - 1)])
         dkv = dkv[TP * n_head :] + back
     moves = [quad_scatter(dkv.reshape(TP, n_head, SPAN, 128)), plane_swap(g_gu)]
-    if n_grp == 1:
-        moves += [
-            line_scatter(g_out[:HDIM].astype(BF).reshape(1, n_head, -1, width), F32),
-            line_scatter(g_out[HDIM:].astype(BF).reshape(1, n_head, -1, width), F32),
-        ]
-    dkv, parts_gu, *g_outs = run("states_back", 8, jobs=moves)
-    ffn_out, dkv = lax.optimization_barrier((ffn_out, dkv))
+    dkv, parts_gu = run("states_back", 8, jobs=moves)
+    ffn_out, dkv, d_entries = lax.optimization_barrier((ffn_out, dkv, d_entries))
     ffn_out = lax.psum_scatter(ffn_out, "tp", tiled=True).astype(F32)
     result = (mixed + ffn_out).astype(BF)
     d_pay, d_taps, d_small = call(
@@ -1337,15 +1343,17 @@
         ],
         axis=1,
     )
-    smalls, parts, rim_back = run(
-        "close",
-        10,
-        jobs=[
-            small_scatter(packets.reshape(n_grp * TP, n_head, 8, lanes)),
-            plane_swap(g_in),
-            chunk_shift(d_norm_in[:RIM].astype(BF), -1),
-        ],
-    )
+    moves = [
+        small_scatter(packets.reshape(n_grp * TP, n_head, 8, lanes)),
+        plane_swap(g_in),
+        chunk_shift(d_norm_in[:RIM].astype(BF), -1),
+    ]
+    if n_grp == 1:
+        moves += [
+            line_scatter(g_out[:HDIM].astype(BF).reshape(1, n_head, -1, width), F32),
+            line_scatter(g_out[HDIM:].astype(BF).reshape(1, n_head, -1, width), F32),
+        ]
+    smalls, parts, rim_back, *g_outs = run("close", 10, jobs=moves)
     d_norm_in = d_norm_in[RIM:].at[rows - RIM :].add(rim_back.astype(F32))
     d_tok, _ = norm_back(ext[RIM:], inv_ext[RIM:], gain_mix, d_norm_in)
     grad_tokens = d_mixed + d_tok

time: 595 us -> 559 us (0.939); the launches traced: 599 us -> 555 us
  Pallas kernels: 467 us -> 419 us
    pallas_call x10, Pallas kernels: 319 us -> 285 us  [communicate(): pl.pallas_call(kernel, out_shape=[job.out for job in jobs], in_specs=[pl....]
    pallas_call x6, Pallas kernels: 146 us -> 132 us  [call(): pl.pallas_call(kernel, out_shape=[jax.ShapeDtypeStruct(s, d) for s, d in...]
  transfers between devices with their start and end apart: 3 -> 5, of which waited for: 0 -> 0; matrix products, arithmetic and copies ran while one was open for 6% -> 11% of each run, Pallas kernels for 40% -> 52%
where the time goes in v4:
time: 559 us; the launch traced here: 555 us
  Pallas kernels  419 us (75%)
  matrix products  59.5 us (11%)
  local copies, waits for them, and re-layouts  27.7 us (5%)
  other arithmetic  22.7 us (4%)
  between operations  14.7 us (3%)
  starting transfers between devices  11.2 us (2%)
    pallas_call x10, Pallas kernels, communicate(): pl.pallas_call(kernel, out_shape=[job.out for job in jobs], in_specs=[pl....  285 us
    pallas_call x6, Pallas kernels, call(): pl.pallas_call(kernel, out_shape=[jax.ShapeDtypeStruct(s, d) for s, d in...  132 us
    dot_general x4, matrix products, dot_rt(): lax.dot_general(a, b, (((1,), (1,)), ((), ())), preferred_element_type=F32)  23.2 us
    dot_general x5, matrix products, dot(): return jnp.dot(a, b, preferred_element_type=F32)  21.1 us
    dot_general x4, matrix products, dot_lt(): lax.dot_general(a, b, (((0,), (0,)), ((), ())), preferred_element_type=F32)  15.2 us
  transfers between devices with their start and end apart: 5, of which 0 were waited for; matrix products, arithmetic and copies ran while one was open for 11% of the time, Pallas kernels for 52%

profile of v4, /device:TPU:0, one launch (start us, length us, event | category | flops | bytes accessed | tf_op | source)
XLA Modules:
  0.0 554.7 jit_solution(3990892000914027295)
XLA Ops:
  16.6 18.0 %open.1 = (f32[8,4,8,128]{3,2,1,0:T(8,128)}, bf16[8,1024]{1,0:T(8,128)(2,1)}, bf16[8,32,896]{2,1,0:T(8,128)(2,1)}) custom-call(f32[8,128]{1,0:T(8,128)} %select_maximum_fusion.2.refs_0_, bf16[8,1024]{1,0:T(8,128)(2,1)} %slice.188.refs_1_, bf16[8,32,896]{2,1,0:T(8,128)(2,1)} %concatenate.41.refs_2_), custom_call_target="tpu_custom_call" | custom-call | tf_op jit(solution)/shard_map/open/pallas_call | solution.py:561
  39.9 49.3 %inputs.1 = (bf16[8,264,1024]{2,1,0:T(8,128)(2,1)}, bf16[8,4,32,896]{3,2,1,0:T(8,128)(2,1)}, bf16[8,32,512]{2,1,0:T(8,128)(2,1)}, bf16[8,256,1024]{2,1,0:T(8,128)(2,1)}) custom-call(bf16[264,1024]{1,0:T(8,128)(2,1)} %multiply_convert_fusion.3.refs_0_, bf16[8,32,896]{2,1,0:T(8,128)(2,1)} %get-tuple-element.93.refs_1_, ...), custom_call_target="tpu_custom_call" | custom-call | tf_op jit(solution)/shard_map/inputs/pallas_call | solution.py:561
  91.4 7.5 %convolution_convert_fusion.1 = bf16[2112,896]{1,0:T(8,128)(2,1)S(1)} fusion(bf16[2112,1024]{1,0:T(8,128)(2,1)} %bitcast.209, bf16[1024,896]{1,0:T(8,128)(2,1)} %bitcast.216), kind=kOutput, calls=%fused_computation.1 | convolution fusion | flops 3877429248 | bytes 9945088 | tf_op jit(solution)/shard_map/dot_general | solution.py:43
  104.3 17.1 %mixer_local.1 = (f32[8,256,448]{2,1,0:T(8,128)}, f32[8,256,128]{2,1,0:T(8,128)}, f32[8,256,192]{2,1,0:T(8,128)}, bf16[8,200,128]{2,1,0:T(8,128)(2,1)}) custom-call(s32[6,8]{1,0:T(8,128)} %stack.35.sc, bf16[8,264,896]{2,1,0:T(8,128)(2,1)} %bitcast.136, s32[8,256,1]{2,1,0:T(8,128)} %copy.117.ds, f32[8,448]{1,0:T(8,128)} %concatenate.46.taps, ...), custom_call_target="tpu_custom_call" | custom-call | tf_op jit(solution)/shard_map/mixer_local/pallas_call | solution.py:466
  121.4 27.8 %states.1 = bf16[8,4,256,128]{3,2,1,0:T(8,128)(2,1)} custom-call(bf16[8,256,128]{2,1,0:T(8,128)(2,1)} %slice.233.refs_0_), custom_call_target="tpu_custom_call" | custom-call | tf_op jit(solution)/shard_map/states/pallas_call | solution.py:561
  149.3 19.5 %attend.1 = (f32[8,256,128]{2,1,0:T(8,128)}, f32[8,256,1]{2,1,0:T(8,128)}) custom-call(s32[6,8]{1,0:T(8,128)} %stack.35.sc, bf16[8,264,896]{2,1,0:T(8,128)(2,1)} %bitcast.137, s32[8,256,1]{2,1,0:T(8,128)} %copy.117.ds, bf16[16,512,128]{2,1,0:T(8,128)(2,1)} %bitcast.143), custom_call_target="tpu_custom_call" | custom-call | tf_op jit(solution)/shard_map/attend/pallas_call | solution.py:466
  168.8 11.0 %all-gather.15.cloned.1.call-start = ((), (), s32[]{:S(2)}) async-start(), calls=%async_computation.5 | async-start | bytes 1966080 | tf_op jit(solution)/shard_map/all_gather | solution.py:1286
  180.0 4.9 fusion.23
  184.9 11.1 %mixer_finish.1 = (bf16[8,256,256]{2,1,0:T(8,128)(2,1)}, f32[8,256,192]{2,1,0:T(8,128)}, f32[8,192,128]{2,1,0:T(8,128)}) custom-call(s32[6,8]{1,0:T(8,128)} %stack.35.sc, bf16[4,8,200,128]{3,2,1,0:T(8,128)(2,1)} %bitcast.148, f32[8,256,448]{2,1,0:T(8,128)} %get-tuple-element.104.u, f32[8,256,128]{2,1,0:T(8,128)} %get-tuple-element.105.cum, ...), custom_call_target="tpu_custom_call" | custom-call | tf_op jit(solution)/shard_map/mixer_finish/pallas_call | solution.py:466
  196.0 4.4 convolution_convert_fusion.4
  200.4 25.9 %middle.1 = f32[256,1024]{1,0:T(8,128)} custom-call(bf16[8,256,1024]{2,1,0:T(8,128)(2,1)} %bitcast.142), custom_call_target="tpu_custom_call" | custom-call | tf_op jit(solution)/shard_map/middle/pallas_call | solution.py:561
  229.4 24.8 %ffn.1 = bf16[8,256,1024]{2,1,0:T(8,128)(2,1)} custom-call(bf16[256,1024]{1,0:T(8,128)(2,1)} %multiply_convert_fusion.4.refs_0_), custom_call_target="tpu_custom_call" | custom-call | tf_op jit(solution)/shard_map/ffn/pallas_call | solution.py:561
  255.6 3.6 fusion.1
  259.7 2.2 multiply_convert_fusion.1
  262.0 3.4 convolution_convert_fusion.6
  265.4 4.4 convolution_convert_fusion.2
  271.9 29.9 %ffn_back.1 = (f32[256,1024]{1,0:T(8,128)}, f32[1,64,1024]{2,1,0:T(8,128)}) custom-call(bf16[8,256,1024]{2,1,0:T(8,128)(2,1)} %bitcast.154, bf16[1,4,64,1024]{3,2,1,0:T(8,128)(2,1)} %bitcast.174), custom_call_target="tpu_custom_call" | custom-call | tf_op jit(solution)/shard_map/ffn_back/pallas_call | solution.py:561
  301.8 2.2 multiply_reduce_fusion.3
  305.5 25.7 %branch_back.1 = (bf16[8,256,1024]{2,1,0:T(8,128)(2,1)}, bf16[8,32,512]{2,1,0:T(8,128)(2,1)}) custom-call(bf16[256,1024]{1,0:T(8,128)(2,1)} %get-tuple-element.148.refs_0_, bf16[8,4,32,512]{3,2,1,0:T(8,128)(2,1)} %bitcast.167), custom_call_target="tpu_custom_call" | custom-call | tf_op jit(solution)/shard_map/branch_back/pallas_call | solution.py:561
  331.2 4.5 convolution_convert_fusion.5
  335.7 9.5 %mixer_entry.1 = bf16[8,192,128]{2,1,0:T(8,128)(2,1)} custom-call(s32[6,8]{1,0:T(8,128)} %stack.35.sc, bf16[8,256,256]{2,1,0:T(8,128)(2,1)} %bitcast.145, f32[8,256,448]{2,1,0:T(8,128)} %get-tuple-element.104.u, f32[8,256,128]{2,1,0:T(8,128)} %get-tuple-element.105.cum, bf16[8,264,896]{2,1,0:T(8,128)(2,1)} %bitcast.139, s32[8,256,1]{2,1,0:T(8,128)} %copy.117.ds), custom_call_target="tpu_custom_call" | custom-call | tf_op jit(solution)/shard_map/mixer_entry/pallas_call | solution.py:466
  345.3 27.9 %attend_back.1 = (f32[8,256,128]{2,1,0:T(8,128)}, bf16[16,512,128]{2,1,0:T(8,128)(2,1)}) custom-call(s32[6,8]{1,0:T(8,128)} %stack.35.sc, bf16[8,264,896]{2,1,0:T(8,128)(2,1)} %bitcast.140, s32[8,256,1]{2,1,0:T(8,128)} %copy.117.ds, bf16[8,256,256]{2,1,0:T(8,128)(2,1)} %bitcast.146, f32[8,256,128]{2,1,0:T(8,128)} %get-tuple-element.107.o, ...), custom_call_target="tpu_custom_call" | custom-call | tf_op jit(solution)/shard_map/attend_back/pallas_call | solution.py:466
  373.2 26.1 %states_back.1 = (bf16[8,64,128]{2,1,0:T(8,128)(2,1)}, bf16[8,32,512]{2,1,0:T(8,128)(2,1)}) custom-call(bf16[8,4,256,128]{3,2,1,0:T(8,128)(2,1)} %bitcast.158, bf16[8,32,512]{2,1,0:T(8,128)(2,1)} %get-tuple-element.117.refs_1_), custom_call_target="tpu_custom_call" | custom-call | tf_op jit(solution)/shard_map/states_back/pallas_call | solution.py:561
  399.3 3.4 convolution_convert_fusion.3
  404.5 3.5 fusion
  409.4 46.8 %mixer_back.1 = (bf16[8,264,896]{2,1,0:T(8,128)(2,1)}, f32[8,448]{1,0:T(8,128)}, f32[8,128]{1,0:T(8,128)}) custom-call(s32[6,8]{1,0:T(8,128)} %stack.35.sc, bf16[4,8,200,128]{3,2,1,0:T(8,128)(2,1)} %bitcast.149, bf16[4,8,192,128]{3,2,1,0:T(8,128)(2,1)} %bitcast.163, bf16[8,256,256]{2,1,0:T(8,128)(2,1)} %bitcast.147, bf16[8,264,896]{2,1,0:T(8,128)(2,1)} %bitcast.141, ...), custom_call_target="tpu_custom_call" | custom-call | tf_op jit(solution)/shard_map/mixer_back/pallas_call | solution.py:466
  456.3 9.5 %convolution_convert_fusion = bf16[2112,1024]{1,0:T(8,128)(2,1)} fusion(bf16[2112,896]{1,0:T(8,128)(2,1)} %bitcast.215, bf16[1024,896]{1,0:T(8,128)(2,1)} %bitcast.217), kind=kOutput, calls=%fused_computation | convolution fusion | flops 3877699584 | bytes 9945088 | tf_op jit(solution)/shard_map/dot_general | solution.py:51
  465.8 6.2 %bitcast_convert_fusion = bf16[1024,896]{1,0:T(8,128)(2,1)} fusion(bf16[8,264,1024]{2,1,0:T(8,128)(2,1)S(1)} %bitcast.211, bf16[8,264,896]{2,1,0:T(8,128)(2,1)S(1)} %copy-done.26), kind=kOutput, calls=%fused_computation.5 | convolution fusion | flops 3876454400 | bytes 9945088 | tf_op jit(solution)/shard_map/dot_general | solution.py:47
  472.0 36.5 %inputs_back.1 = (f32[264,1024]{1,0:T(8,128)}, bf16[8,32,896]{2,1,0:T(8,128)(2,1)}) custom-call(bf16[8,264,1024]{2,1,0:T(8,128)(2,1)} %bitcast.150, bf16[8,4,32,896]{3,2,1,0:T(8,128)(2,1)} %bitcast.159), custom_call_target="tpu_custom_call" | custom-call | tf_op jit(solution)/shard_map/inputs_back/pallas_call | solution.py:561
  513.1 20.7 %close.1 = (f32[8,128]{1,0:T(8,128)}, bf16[8,32,896]{2,1,0:T(8,128)(2,1)}, bf16[8,1024]{1,0:T(8,128)(2,1)}, f32[1,16,1024]{2,1,0:T(8,128)}, f32[1,48,1024]{2,1,0:T(8,128)}) custom-call(f32[8,4,8,128]{3,2,1,0:T(8,128)} %bitcast.176, bf16[8,32,896]{2,1,0:T(8,128)(2,1)} %get-tuple-element.130.refs_1_, bf16[8,1024]{1,0:T(8,128)(2,1)} %slice.274.refs_2_, ...), custom_call_target="tpu_custom_call" | custom-call | tf_op jit(solution)/shard_map/close/pallas_call | solution.py:561
  535.2 2.2 assemble.1
  541.1 2.8 subtract_add_fusion
  (190 shorter events, 47.8 us)
Async XLA Ops:
  7.2 8.3 %slice-start = ((bf16[32,3352]{1,0:T(8,128)(2,1)}), bf16[32,256]{1,0:T(8,128)(2,1)S(1)}, s32[]{:S(2)}) async-start(bf16[32,3352]{1,0:T(8,128)(2,1)} %param.24), calls=%async_computation.6 | async-start | bytes 32768 | tf_op jit(solution)/shard_map/slice | solution.py:1061
  7.2 28.5 %copy-start.1 = (bf16[256,1024]{1,0:T(8,128)(2,1)S(1)}, bf16[256,1024]{1,0:T(8,128)(2,1)}, u32[]{:S(2)}) copy-start(bf16[256,1024]{1,0:T(8,128)(2,1)} %param.21) | copy-start | bytes 1572868
  7.2 114.1 %all-gather.9.cloned.1.call-start = ((), (), s32[]{:S(2)}) async-start(), calls=%async_computation.2 | async-start | bytes 1310720 | tf_op jit(solution)/shard_map/all_gather | solution.py:1147
  10.4 26.2 %copy-start.14 = (bf16[32,2048]{1,0:T(8,128)(2,1)S(1)}, bf16[32,2048]{1,0:T(8,128)(2,1)}, u32[]{:S(2)}) copy-start(bf16[32,2048]{1,0:T(8,128)(2,1)} %param.33) | copy-start | bytes 393220
  10.6 26.1 %copy-start.15 = (bf16[32,2048]{1,0:T(8,128)(2,1)S(1)}, bf16[32,2048]{1,0:T(8,128)(2,1)}, u32[]{:S(2)}) copy-start(bf16[32,2048]{1,0:T(8,128)(2,1)} %param.34) | copy-start | bytes 393220
  16.6 22.6 %copy-start.16 = (bf16[64,1024]{1,0:T(8,128)(2,1)S(1)}, bf16[64,1024]{1,0:T(8,128)(2,1)}, u32[]{:S(2)}) copy-start(bf16[64,1024]{1,0:T(8,128)(2,1)} %param.35) | copy-start | bytes 393220
  16.6 22.6 %copy-start.17 = (bf16[48,1024]{1,0:T(8,128)(2,1)S(1)}, bf16[48,1024]{1,0:T(8,128)(2,1)}, u32[]{:S(2)}) copy-start(bf16[48,1024]{1,0:T(8,128)(2,1)} %param.31) | copy-start | bytes 294916
  16.6 22.6 %copy-start.19 = (bf16[16,1024]{1,0:T(8,128)(2,1)S(1)}, bf16[16,1024]{1,0:T(8,128)(2,1)}, u32[]{:S(2)}) copy-start(bf16[16,1024]{1,0:T(8,128)(2,1)} %param.30) | copy-start | bytes 98308
  38.4 50.9 %copy-start.12 = (f32[8,4,8,128]{3,2,1,0:T(8,128)S(1)}, f32[8,4,8,128]{3,2,1,0:T(8,128)}, u32[]{:S(2)}) copy-start(f32[8,4,8,128]{3,2,1,0:T(8,128)} %get-tuple-element.92) | copy-start | bytes 393220
  38.4 51.0 %copy-start.27 = (s32[4]{0:T(128)S(1)}, s32[4]{0:T(128)}, u32[]{:S(2)}) copy-start(s32[4]{0:T(128)} %param.36) | copy-start | bytes 52
  89.3 79.5 %all-gather.11.cloned.1.call-start = ((), (), s32[]{:S(2)}) async-start(), calls=%async_computation.3 | async-start | bytes 2048000 | tf_op jit(solution)/shard_map/all_gather | solution.py:1190
  121.4 132.8 %all-gather.13.cloned.1.call-start = ((), (), s32[]{:S(2)}) async-start(), calls=%async_computation.4 | async-start | bytes 1310720 | tf_op jit(solution)/shard_map/all_gather | solution.py:736
  149.3 30.6 %copy-start.7 = (bf16[512,1024]{1,0:T(8,128)(2,1)S(1)}, bf16[512,1024]{1,0:T(8,128)(2,1)}, u32[]{:S(2)}) copy-start(bf16[512,1024]{1,0:T(8,128)(2,1)} %all-gather.9.cloned.1.call-done) | copy-start | bytes 3145732
  168.8 233.8 %all-gather.15.cloned.1.call-start = ((), (), s32[]{:S(2)}) async-start(), calls=%async_computation.5 | async-start | bytes 1966080 | tf_op jit(solution)/shard_map/all_gather | solution.py:1286
  180.0 16.1 %copy-start.8 = (bf16[4,16,1024]{2,1,0:T(8,128)(2,1)}, bf16[4,16,1024]{2,1,0:T(8,128)(2,1)S(1)}, u32[]{:S(2)}) copy-start(bf16[4,16,1024]{2,1,0:T(8,128)(2,1)S(1)} %slice.206) | copy-start | bytes 393220
  255.6 3.7 copy-start.4
  255.6 4.1 copy-start.28
  265.4 4.4 copy-start.25
  301.8 2.2 copy-start.3
  301.8 2.2 copy-start.6
  304.0 27.2 %copy-start.9 = (bf16[4,16,1024]{2,1,0:T(8,128)(2,1)S(1)}, bf16[4,16,1024]{2,1,0:T(8,128)(2,1)}, u32[]{:S(2)}) copy-start(bf16[4,16,1024]{2,1,0:T(8,128)(2,1)} %copy-done.8) | copy-start | bytes 393220
  345.2 198.7 %reduce-scatter.2.cloned.1.call-start = ((), (), s32[]{:S(2)}) async-start(), calls=%async_computation.1 | async-start | bytes 4718592 | tf_op jit(solution)/shard_map/reduce_scatter | solution.py:1304
  404.5 4.9 copy-start.20
  409.4 56.4 %slice-start.1 = ((s8[4325376]{0:T(1024)(128)(4,1)}), s8[131072]{0:T(1024)(128)(4,1)S(1)}, s32[]{:S(2)}) async-start(s8[4325376]{0:T(1024)(128)(4,1)} %bitcast.210), calls=%async_computation.7 | async-start | bytes 262144
  456.3 9.6 %slice-start.2 = ((s8[4325376]{0:T(1024)(128)(4,1)}), s8[4194304]{0:T(1024)(128)(4,1)S(1)}, s32[]{:S(2)}) async-start(s8[4325376]{0:T(1024)(128)(4,1)} %bitcast.210), calls=%async_computation.8 | async-start | bytes 8388608
  456.3 9.6 %copy-start.26 = (bf16[8,264,896]{2,1,0:T(8,128)(2,1)S(1)}, bf16[8,264,896]{2,1,0:T(8,128)(2,1)}, u32[]{:S(2)}) copy-start(bf16[8,264,896]{2,1,0:T(8,128)(2,1)} %get-tuple-element.126) | copy-start | bytes 11354116
  508.5 2.8 copy-start.2
  508.6 3.0 copy-start.21
  508.6 3.4 copy-start.24
  533.8 5.7 %copy-start.22 = (f32[8,128]{1,0:T(8,128)S(1)}, f32[8,128]{1,0:T(8,128)}, u32[]{:S(2)}) copy-start(f32[8,128]{1,0:T(8,128)} %get-tuple-element.132) | copy-start | bytes 12292
  543.9 2.7 copy-start.13
  543.9 3.4 copy-start.11
  (5 other events, 8.7 us)
Sparse Core Ops, SparseCore 0:
  89.4 26.7 all-gather.8
  121.5 40.7 all-gather.10
  168.9 30.7 all-gather.12
  345.4 36.2 all-gather.14
  402.8 50.3 reduce-scatter.1
